TPU v7x, 32 devices: a whole 2x2x4 slice. The times are simulated.
32 devices in a mesh: parts: 2 (over y), tile: 8 (over z, x), cond: 2 (over core).
Axes of the slice: x: 2, y: 2, z: 4, core: 2. Of those that a mesh axis runs over, the one named last changes fastest.
Arguments:
- mask: bfloat16 [16, 256, 256], P(('parts', 'tile')), parts along dimension 0, may hold values from -1 to 1
- kernels: bfloat16 [8, 24, 64, 128], P('cond'), may hold values from -6 to 6
- socs_weight: float32 [8, 24], P('cond'), may hold values from 0.02 to 1
- dose: float32 [8], P('cond'), may hold values from 0.8 to 1.25
- threshold: float32 [8], P('cond'), may hold values from 0.5 to 0.85
Outputs:
- band_max: float32 [16, 256, 256], P(('parts', 'tile'), 'cond'), parts along dimension 0
- band_min: float32 [16, 256, 256], P(('parts', 'tile'), 'cond'), parts along dimension 0
There are 2 independent parts, one for each index of `parts`. A program takes and returns all parts, laid end to end along the dimension named above; an argument that names none is the same for every part. Nothing has to cross between parts.
All inputs are finite; a program needn't handle non-finite values.
Results may differ from a plain program's by a relative error of at most 0.0068.
Values may be sent and summed in bfloat16 or wider, within the bound.
No kernel may reach another device: no remote copies, remote signals or barrier semaphores. Data moves between devices by JAX's collectives and lax.ppermute only.
A program may use at most 64 MiB of HBM per device.

v0:
```python
import math

import jax
import jax.numpy as jnp
from jax import lax
from jax.sharding import PartitionSpec as P

MARGIN = 64
BLUR = 8


diffusion = 2.0
steepness = 8.0


def shifted(block, axis, distance):
    devices = range(lax.axis_size(axis))
    route = [((i - distance) % len(devices), i) for i in devices]
    return lax.ppermute(block, axis, route)


def merged(value, axis, join):
    pieces = jax.tree.map(lambda part: lax.all_gather(part, axis), value)
    head = jax.tree.map(lambda part: part[0], pieces)
    tail = jax.tree.map(lambda part: part[1:], pieces)
    subtotal, _ = lax.scan(lambda subtotal, piece: (join(subtotal, piece), None), head, tail)
    return subtotal


def phase_table(first, count, pad_width, band_width):
    pixel_index = jnp.arange(count, dtype=jnp.int32) + first
    freq_index = (jnp.arange(band_width, dtype=jnp.int32) - band_width // 2) % pad_width
    turn_count = pixel_index[:, None] * freq_index[None, :] % pad_width
    angle_grid = turn_count.astype(jnp.float32) * (2.0 * math.pi / pad_width)
    return (jnp.cos(angle_grid).astype(jnp.bfloat16), jnp.sin(angle_grid).astype(jnp.bfloat16))


def blur_table(core):
    offset_grid = (
        jnp.arange(core + 2 * BLUR, dtype=jnp.int32)[None, :]
        - jnp.arange(core, dtype=jnp.int32)[:, None]
        - BLUR
    )
    distance = offset_grid.astype(jnp.float32)
    taps_grid = jnp.exp(-distance * distance / (2.0 * diffusion * diffusion))
    taps_grid = jnp.where(jnp.abs(offset_grid) <= BLUR, taps_grid, jnp.zeros_like(taps_grid))
    reach_grid = jnp.arange(-BLUR, BLUR + 1, dtype=jnp.int32).astype(jnp.float32)
    total_taps = jnp.sum(jnp.exp(-reach_grid * reach_grid / (2.0 * diffusion * diffusion)))
    return taps_grid / total_taps


def make_tables(core, band_width):
    pad_width = core + 2 * MARGIN
    cos_in, sin_in = phase_table(0, pad_width, pad_width, band_width)
    cos_out, sin_out = phase_table(MARGIN - BLUR, core + 2 * BLUR, pad_width, band_width)
    return (cos_in, sin_in, cos_out, sin_out, blur_table(core))


def expose(window, kernel_set, weights, dose_one, threshold_one, tables):
    cos_in, sin_in, cos_out, sin_out, blur_rows = tables
    pad_width = window.shape[0]
    band_width = cos_in.shape[1]
    hp = lax.Precision.HIGHEST
    part_real = jnp.dot(cos_in.T, window, preferred_element_type=jnp.float32).astype(jnp.bfloat16)
    part_imag = (-jnp.dot(sin_in.T, window, preferred_element_type=jnp.float32)).astype(
        jnp.bfloat16
    )
    spec_real = (
        jnp.dot(part_real, cos_in, preferred_element_type=jnp.float32)
        + jnp.dot(part_imag, sin_in, preferred_element_type=jnp.float32)
    ) / pad_width
    spec_imag = (
        jnp.dot(part_imag, cos_in, preferred_element_type=jnp.float32)
        - jnp.dot(part_real, sin_in, preferred_element_type=jnp.float32)
    ) / pad_width
    group_size = min(8, kernel_set.shape[0])
    kernel_groups = kernel_set.reshape(-1, group_size, band_width, 2 * band_width)
    weight_groups = weights.reshape(-1, group_size)

    def group_power(packed):
        kernel_part, weight_part = packed
        kern_real = kernel_part[:, :, :band_width].astype(jnp.float32)
        kern_imag = kernel_part[:, :, band_width:].astype(jnp.float32)
        prod_real = (spec_real * kern_real - spec_imag * kern_imag).astype(jnp.bfloat16)
        prod_imag = (spec_real * kern_imag + spec_imag * kern_real).astype(jnp.bfloat16)
        half_real = (
            jnp.einsum("nfg,yg->nfy", prod_real, cos_out, preferred_element_type=jnp.float32)
            - jnp.einsum("nfg,yg->nfy", prod_imag, sin_out, preferred_element_type=jnp.float32)
        ).astype(jnp.bfloat16)
        half_imag = (
            jnp.einsum("nfg,yg->nfy", prod_real, sin_out, preferred_element_type=jnp.float32)
            + jnp.einsum("nfg,yg->nfy", prod_imag, cos_out, preferred_element_type=jnp.float32)
        ).astype(jnp.bfloat16)
        field_real = (
            jnp.einsum("xf,nfy->nxy", cos_out, half_real, preferred_element_type=jnp.float32)
            - jnp.einsum("xf,nfy->nxy", sin_out, half_imag, preferred_element_type=jnp.float32)
        ) / band_width
        field_imag = (
            jnp.einsum("xf,nfy->nxy", cos_out, half_imag, preferred_element_type=jnp.float32)
            + jnp.einsum("xf,nfy->nxy", sin_out, half_real, preferred_element_type=jnp.float32)
        ) / band_width
        power = field_real * field_real + field_imag * field_imag
        return jnp.tensordot(weight_part, power, axes=1, precision=hp)

    intensity = jnp.sum(lax.map(group_power, (kernel_groups, weight_groups)), axis=0) / jnp.sum(
        weights
    )
    blurred = jnp.dot(jnp.dot(blur_rows, intensity, precision=hp), blur_rows.T, precision=hp)
    return jax.nn.sigmoid(steepness * (dose_one * blurred - threshold_one))


def from_rows(piece, offset):
    return shifted(piece, "tile", offset)


def from_cols(piece, offset):
    return shifted(piece, "tile", offset)


def masked_by(flag, piece):
    return jnp.where(flag, piece, jnp.zeros_like(piece))


def gather_margins(tile_mask):
    count = lax.axis_size("tile")
    columns = min(8, count // 2)
    grid_rows = count // columns
    position = (lax.axis_index("tile") + columns // 2) % count
    column = position % columns
    row = position // columns
    has_left = column > 0
    has_right = column < columns - 1
    has_up = row > 0
    has_down = row < grid_rows - 1
    margin_rows = MARGIN
    upper_rows = masked_by(has_up, from_rows(tile_mask[-margin_rows:], columns))
    lower_rows = masked_by(has_down, from_rows(tile_mask[:margin_rows], -columns))
    tall_block = jnp.concatenate([upper_rows, tile_mask, lower_rows], axis=0)
    left_part = masked_by(has_left, from_cols(tall_block[:, -margin_rows:], 1))
    right_part = masked_by(has_right, from_cols(tall_block[:, :margin_rows], -1))
    return jnp.concatenate([left_part, tall_block, right_part], axis=1)


def pair_bounds(first_pair, second_pair):
    return (jnp.maximum(first_pair[0], second_pair[0]), jnp.minimum(first_pair[1], second_pair[1]))


def on_device(mask, kernels, socs_weight, dose, threshold):
    core = mask.shape[1]
    window = gather_margins(mask[0])
    tables = make_tables(core, kernels.shape[2])

    def one_condition(packed):
        kernel_set, weights, dose_one, threshold_one = packed
        return expose(window, kernel_set, weights, dose_one, threshold_one, tables)

    resist = lax.map(one_condition, (kernels, socs_weight, dose, threshold))
    highest = jnp.max(resist, axis=0)
    lowest = jnp.min(resist, axis=0)
    row_share = core // lax.axis_size("cond")
    whole_high, whole_low = merged((highest, lowest), "cond", pair_bounds)
    start = lax.axis_index("cond") * row_share
    top_band = lax.dynamic_slice_in_dim(whole_high, start, row_share, 0)
    bottom_band = lax.dynamic_slice_in_dim(whole_low, start, row_share, 0)
    return (top_band[None], bottom_band[None])


def solution(mesh):
    return jax.shard_map(
        on_device,
        mesh=mesh,
        in_specs=(
            P(("parts", "tile"), None, None),
            P("cond", None, None, None),
            P("cond", None),
            P("cond"),
            P("cond"),
        ),
        out_specs=(P(("parts", "tile"), "cond", None), P(("parts", "tile"), "cond", None)),
        check_vma=False,
    )
```

profile of v0, /device:TPU:0, one launch (start us, length us, event | category | flops | bytes accessed | tf_op | source)
XLA Modules:
  0.0 254.2 jit_solution(13842338668658044846)
XLA Ops:
  1.4 4.1 %collective-permute-start = (bf16[64,256]{1,0:T(8,128)(2,1)S(1)}, bf16[64,256]{1,0:T(8,128)(2,1)S(1)}, u32[]{:S(2)}, u32[]{:S(2)}) collective-permute-start(bf16[64,256]{1,0:T(8,128)(2,1)S(1)} %get-tuple-element.422), channel_id=1, source_target_pairs={{8,0},{10,2},{12,4},{14,6},{0,8},{2,10},{4,12},{6,14},{9,1},{11,3}... | collective-permute-start | bytes 98312 | tf_op jit(solution)/shard_map/ppermute | solution.py:19
  7.8 2.6 %collective-permute-done.1 = bf16[64,256]{1,0:T(8,128)(2,1)S(1)} collective-permute-done((bf16[64,256]{1,0:T(8,128)(2,1)S(1)}, bf16[64,256]{1,0:T(8,128)(2,1)S(1)}, u32[]{:S(2)}, u32[]{:S(2)}) %collective-permute-start.1) | collective-permute-done | bytes 32800 | tf_op jit(solution)/shard_map/ppermute | solution.py:19
  13.6 3.2 %collective-permute-start.3 = (bf16[384,64]{1,0:T(8,128)(2,1)S(1)}, bf16[384,64]{1,0:T(8,128)(2,1)S(1)}, u32[]{:S(2)}, u32[]{:S(2)}) collective-permute-start(bf16[384,64]{1,0:T(8,128)(2,1)S(1)} %get-tuple-element.421), channel_id=1, source_target_pairs={{2,0},{4,2},{6,4},{8,6},{10,8},{12,10},{14,12},{0,14},{3,1},{5,3},... | collective-permute-start | bytes 147464 | tf_op jit(solution)/shard_map/ppermute | solution.py:19
  25.9 221.0 %while.41 = (s32[]{:T(128)}, f32[4,256,256]{2,1,0:T(8,128)}, f32[4]{0:T(128)S(1)}, bf16[4,24,64,128]{3,2,1,0:T(8,128)(2,1)}, f32[4,24]{1,0:T(4,128)}, /*index=5*...) while((s32[]{:T(128)}, f32[4,256,256]{2,1,0:T(8,128)}, ...), condition=%wide.region_6.7_spmd.clone.clone.clone, body=%wide.region_1.6_spmd.clone.clone.clone.sunk | while | flops 830326528 | bytes 35282148 | solution.py:157
  31.1 42.9 %while.42 = (s32[]{:T(128)}, f32[3,272,272]{2,1,0:T(8,128)}, f32[3,8]{1,0:T(4,128)S(1)}, f32[64,64]{1,0:T(8,128)S(1)}, bf16[3,8,64,128]{3,2,1,0:T(8,128)(2,1)}, ...) while((s32[]{:T(128)}, f32[3,272,272]{2,1,0:T(8,128)}, ...), condition=%wide.region_3.3_spmd.clone, body=%wide.region_2.2_spmd.clone.sunk | while | flops 386930688 | bytes 31926896 | solution.py:105
  35.2 2.7 %add_bitcast_fusion.2 = f32[8,272,272]{1,2,0:T(8,128)} fusion(f32[8,272,272]{2,1,0:T(8,128)S(1)} %fusion.171, f32[8,272,272]{2,1,0:T(8,128)S(1)} %fusion.174, f32[8,272,272]{2,1,0:T(8,128)S(1)} %fusion.175, bf16[8,64,272]{2,1,0:T(8,128)(2,1)S(1)} %fusion.173, bf16[272,64]{0,1:T(8,128)(2,1)S(1)} %get-tuple-element.596), kind=kOutput, calls=%fused_computation.3.clone.1 | convolution fusion | flops 79902720 | bytes 9783296 | tf_op jit(solution)/shard_map/while/body/eval_jaxpr/while/body/eval_jaxpr/xf,nfy->nxy/dot_general | solution.py:100
  37.9 3.8 %copy.13 = f32[8,272,272]{2,0,1:T(8,128)S(1)} copy(f32[8,272,272]{1,2,0:T(8,128)} %add_bitcast_fusion.2) | data formatting | bytes 4734976 | tf_op jit(solution)/shard_map/while/body/eval_jaxpr/while/body/eval_jaxpr/add | solution.py:102
  41.7 2.9 %fusion.176 = f32[1,272,272]{2,0,1:T(1,128)S(1)} fusion(f32[8,272,272]{2,0,1:T(8,128)S(1)} %copy.13, f32[3,8]{1,0:T(4,128)S(1)} %get-tuple-element.591, s32[]{:T(128)S(6)} %copy.17), kind=kOutput, calls=%fused_computation.33.clone.1 | convolution fusion | flops 7102464 | bytes 3638788 | tf_op jit(solution)/shard_map/while/body/eval_jaxpr/while/body/eval_jaxpr/dot_general | solution.py:103
  49.5 2.7 %add_bitcast_fusion.2 = f32[8,272,272]{1,2,0:T(8,128)} fusion(f32[8,272,272]{2,1,0:T(8,128)S(1)} %fusion.171, f32[8,272,272]{2,1,0:T(8,128)S(1)} %fusion.174, f32[8,272,272]{2,1,0:T(8,128)S(1)} %fusion.175, bf16[8,64,272]{2,1,0:T(8,128)(2,1)S(1)} %fusion.173, bf16[272,64]{0,1:T(8,128)(2,1)S(1)} %get-tuple-element.596), kind=kOutput, calls=%fused_computation.3.clone.1 | convolution fusion | flops 79902720 | bytes 9783296 | tf_op jit(solution)/shard_map/while/body/eval_jaxpr/while/body/eval_jaxpr/xf,nfy->nxy/dot_general | solution.py:100
  52.2 3.8 %copy.13 = f32[8,272,272]{2,0,1:T(8,128)S(1)} copy(f32[8,272,272]{1,2,0:T(8,128)} %add_bitcast_fusion.2) | data formatting | bytes 4734976 | tf_op jit(solution)/shard_map/while/body/eval_jaxpr/while/body/eval_jaxpr/add | solution.py:102
  56.0 2.9 %fusion.176 = f32[1,272,272]{2,0,1:T(1,128)S(1)} fusion(f32[8,272,272]{2,0,1:T(8,128)S(1)} %copy.13, f32[3,8]{1,0:T(4,128)S(1)} %get-tuple-element.591, s32[]{:T(128)S(6)} %copy.17), kind=kOutput, calls=%fused_computation.33.clone.1 | convolution fusion | flops 7102464 | bytes 3638788 | tf_op jit(solution)/shard_map/while/body/eval_jaxpr/while/body/eval_jaxpr/dot_general | solution.py:103
  63.8 2.7 %add_bitcast_fusion.2 = f32[8,272,272]{1,2,0:T(8,128)} fusion(f32[8,272,272]{2,1,0:T(8,128)S(1)} %fusion.171, f32[8,272,272]{2,1,0:T(8,128)S(1)} %fusion.174, f32[8,272,272]{2,1,0:T(8,128)S(1)} %fusion.175, bf16[8,64,272]{2,1,0:T(8,128)(2,1)S(1)} %fusion.173, bf16[272,64]{0,1:T(8,128)(2,1)S(1)} %get-tuple-element.596), kind=kOutput, calls=%fused_computation.3.clone.1 | convolution fusion | flops 79902720 | bytes 9783296 | tf_op jit(solution)/shard_map/while/body/eval_jaxpr/while/body/eval_jaxpr/xf,nfy->nxy/dot_general | solution.py:100
  66.5 3.8 %copy.13 = f32[8,272,272]{2,0,1:T(8,128)S(1)} copy(f32[8,272,272]{1,2,0:T(8,128)} %add_bitcast_fusion.2) | data formatting | bytes 4734976 | tf_op jit(solution)/shard_map/while/body/eval_jaxpr/while/body/eval_jaxpr/add | solution.py:102
  70.3 2.9 %fusion.176 = f32[1,272,272]{2,0,1:T(1,128)S(1)} fusion(f32[8,272,272]{2,0,1:T(8,128)S(1)} %copy.13, f32[3,8]{1,0:T(4,128)S(1)} %get-tuple-element.591, s32[]{:T(128)S(6)} %copy.17), kind=kOutput, calls=%fused_computation.33.clone.1 | convolution fusion | flops 7102464 | bytes 3638788 | tf_op jit(solution)/shard_map/while/body/eval_jaxpr/while/body/eval_jaxpr/dot_general | solution.py:103
  77.8 3.5 %fusion.150 = f32[4,256,256]{2,1,0:T(8,128)} fusion(f32[4,256,256]{2,1,0:T(8,128)} %get-tuple-element.614, s32[]{:T(128)S(6)} %copy.24, f32[272,256]{1,0:T(8,128)S(1)} %fusion.149, f32[]{:T(128)} %get-tuple-element.638, f32[]{:T(128)} %bitcast.80, f32[]{:T(128)} %bitcast.81), kind=kOutput, calls=%fused_computation.42.clone.1 | convolution fusion | flops 214999040 | bytes 542212 | tf_op jit(solution)/shard_map/while/body/eval_jaxpr/dot_general | solution.py:108
  86.3 42.9 %while.42 = (s32[]{:T(128)}, f32[3,272,272]{2,1,0:T(8,128)}, f32[3,8]{1,0:T(4,128)S(1)}, f32[64,64]{1,0:T(8,128)S(1)}, bf16[3,8,64,128]{3,2,1,0:T(8,128)(2,1)}, ...) while((s32[]{:T(128)}, f32[3,272,272]{2,1,0:T(8,128)}, ...), condition=%wide.region_3.3_spmd.clone, body=%wide.region_2.2_spmd.clone.sunk | while | flops 386930688 | bytes 31926896 | solution.py:105
  90.4 2.7 %add_bitcast_fusion.2 = f32[8,272,272]{1,2,0:T(8,128)} fusion(f32[8,272,272]{2,1,0:T(8,128)S(1)} %fusion.171, f32[8,272,272]{2,1,0:T(8,128)S(1)} %fusion.174, f32[8,272,272]{2,1,0:T(8,128)S(1)} %fusion.175, bf16[8,64,272]{2,1,0:T(8,128)(2,1)S(1)} %fusion.173, bf16[272,64]{0,1:T(8,128)(2,1)S(1)} %get-tuple-element.596), kind=kOutput, calls=%fused_computation.3.clone.1 | convolution fusion | flops 79902720 | bytes 9783296 | tf_op jit(solution)/shard_map/while/body/eval_jaxpr/while/body/eval_jaxpr/xf,nfy->nxy/dot_general | solution.py:100
  93.1 3.8 %copy.13 = f32[8,272,272]{2,0,1:T(8,128)S(1)} copy(f32[8,272,272]{1,2,0:T(8,128)} %add_bitcast_fusion.2) | data formatting | bytes 4734976 | tf_op jit(solution)/shard_map/while/body/eval_jaxpr/while/body/eval_jaxpr/add | solution.py:102
  97.0 2.9 %fusion.176 = f32[1,272,272]{2,0,1:T(1,128)S(1)} fusion(f32[8,272,272]{2,0,1:T(8,128)S(1)} %copy.13, f32[3,8]{1,0:T(4,128)S(1)} %get-tuple-element.591, s32[]{:T(128)S(6)} %copy.17), kind=kOutput, calls=%fused_computation.33.clone.1 | convolution fusion | flops 7102464 | bytes 3638788 | tf_op jit(solution)/shard_map/while/body/eval_jaxpr/while/body/eval_jaxpr/dot_general | solution.py:103
  104.7 2.7 %add_bitcast_fusion.2 = f32[8,272,272]{1,2,0:T(8,128)} fusion(f32[8,272,272]{2,1,0:T(8,128)S(1)} %fusion.171, f32[8,272,272]{2,1,0:T(8,128)S(1)} %fusion.174, f32[8,272,272]{2,1,0:T(8,128)S(1)} %fusion.175, bf16[8,64,272]{2,1,0:T(8,128)(2,1)S(1)} %fusion.173, bf16[272,64]{0,1:T(8,128)(2,1)S(1)} %get-tuple-element.596), kind=kOutput, calls=%fused_computation.3.clone.1 | convolution fusion | flops 79902720 | bytes 9783296 | tf_op jit(solution)/shard_map/while/body/eval_jaxpr/while/body/eval_jaxpr/xf,nfy->nxy/dot_general | solution.py:100
  107.4 3.8 %copy.13 = f32[8,272,272]{2,0,1:T(8,128)S(1)} copy(f32[8,272,272]{1,2,0:T(8,128)} %add_bitcast_fusion.2) | data formatting | bytes 4734976 | tf_op jit(solution)/shard_map/while/body/eval_jaxpr/while/body/eval_jaxpr/add | solution.py:102
  111.3 2.9 %fusion.176 = f32[1,272,272]{2,0,1:T(1,128)S(1)} fusion(f32[8,272,272]{2,0,1:T(8,128)S(1)} %copy.13, f32[3,8]{1,0:T(4,128)S(1)} %get-tuple-element.591, s32[]{:T(128)S(6)} %copy.17), kind=kOutput, calls=%fused_computation.33.clone.1 | convolution fusion | flops 7102464 | bytes 3638788 | tf_op jit(solution)/shard_map/while/body/eval_jaxpr/while/body/eval_jaxpr/dot_general | solution.py:103
  119.0 2.7 %add_bitcast_fusion.2 = f32[8,272,272]{1,2,0:T(8,128)} fusion(f32[8,272,272]{2,1,0:T(8,128)S(1)} %fusion.171, f32[8,272,272]{2,1,0:T(8,128)S(1)} %fusion.174, f32[8,272,272]{2,1,0:T(8,128)S(1)} %fusion.175, bf16[8,64,272]{2,1,0:T(8,128)(2,1)S(1)} %fusion.173, bf16[272,64]{0,1:T(8,128)(2,1)S(1)} %get-tuple-element.596), kind=kOutput, calls=%fused_computation.3.clone.1 | convolution fusion | flops 79902720 | bytes 9783296 | tf_op jit(solution)/shard_map/while/body/eval_jaxpr/while/body/eval_jaxpr/xf,nfy->nxy/dot_general | solution.py:100
  121.7 3.8 %copy.13 = f32[8,272,272]{2,0,1:T(8,128)S(1)} copy(f32[8,272,272]{1,2,0:T(8,128)} %add_bitcast_fusion.2) | data formatting | bytes 4734976 | tf_op jit(solution)/shard_map/while/body/eval_jaxpr/while/body/eval_jaxpr/add | solution.py:102
  125.5 2.9 %fusion.176 = f32[1,272,272]{2,0,1:T(1,128)S(1)} fusion(f32[8,272,272]{2,0,1:T(8,128)S(1)} %copy.13, f32[3,8]{1,0:T(4,128)S(1)} %get-tuple-element.591, s32[]{:T(128)S(6)} %copy.17), kind=kOutput, calls=%fused_computation.33.clone.1 | convolution fusion | flops 7102464 | bytes 3638788 | tf_op jit(solution)/shard_map/while/body/eval_jaxpr/while/body/eval_jaxpr/dot_general | solution.py:103
  133.1 3.5 %fusion.150 = f32[4,256,256]{2,1,0:T(8,128)} fusion(f32[4,256,256]{2,1,0:T(8,128)} %get-tuple-element.614, s32[]{:T(128)S(6)} %copy.24, f32[272,256]{1,0:T(8,128)S(1)} %fusion.149, f32[]{:T(128)} %get-tuple-element.638, f32[]{:T(128)} %bitcast.80, f32[]{:T(128)} %bitcast.81), kind=kOutput, calls=%fused_computation.42.clone.1 | convolution fusion | flops 214999040 | bytes 542212 | tf_op jit(solution)/shard_map/while/body/eval_jaxpr/dot_general | solution.py:108
  141.6 42.9 %while.42 = (s32[]{:T(128)}, f32[3,272,272]{2,1,0:T(8,128)}, f32[3,8]{1,0:T(4,128)S(1)}, f32[64,64]{1,0:T(8,128)S(1)}, bf16[3,8,64,128]{3,2,1,0:T(8,128)(2,1)}, ...) while((s32[]{:T(128)}, f32[3,272,272]{2,1,0:T(8,128)}, ...), condition=%wide.region_3.3_spmd.clone, body=%wide.region_2.2_spmd.clone.sunk | while | flops 386930688 | bytes 31926896 | solution.py:105
  145.6 2.7 %add_bitcast_fusion.2 = f32[8,272,272]{1,2,0:T(8,128)} fusion(f32[8,272,272]{2,1,0:T(8,128)S(1)} %fusion.171, f32[8,272,272]{2,1,0:T(8,128)S(1)} %fusion.174, f32[8,272,272]{2,1,0:T(8,128)S(1)} %fusion.175, bf16[8,64,272]{2,1,0:T(8,128)(2,1)S(1)} %fusion.173, bf16[272,64]{0,1:T(8,128)(2,1)S(1)} %get-tuple-element.596), kind=kOutput, calls=%fused_computation.3.clone.1 | convolution fusion | flops 79902720 | bytes 9783296 | tf_op jit(solution)/shard_map/while/body/eval_jaxpr/while/body/eval_jaxpr/xf,nfy->nxy/dot_general | solution.py:100
  148.3 3.8 %copy.13 = f32[8,272,272]{2,0,1:T(8,128)S(1)} copy(f32[8,272,272]{1,2,0:T(8,128)} %add_bitcast_fusion.2) | data formatting | bytes 4734976 | tf_op jit(solution)/shard_map/while/body/eval_jaxpr/while/body/eval_jaxpr/add | solution.py:102
  152.2 2.9 %fusion.176 = f32[1,272,272]{2,0,1:T(1,128)S(1)} fusion(f32[8,272,272]{2,0,1:T(8,128)S(1)} %copy.13, f32[3,8]{1,0:T(4,128)S(1)} %get-tuple-element.591, s32[]{:T(128)S(6)} %copy.17), kind=kOutput, calls=%fused_computation.33.clone.1 | convolution fusion | flops 7102464 | bytes 3638788 | tf_op jit(solution)/shard_map/while/body/eval_jaxpr/while/body/eval_jaxpr/dot_general | solution.py:103
  159.9 2.7 %add_bitcast_fusion.2 = f32[8,272,272]{1,2,0:T(8,128)} fusion(f32[8,272,272]{2,1,0:T(8,128)S(1)} %fusion.171, f32[8,272,272]{2,1,0:T(8,128)S(1)} %fusion.174, f32[8,272,272]{2,1,0:T(8,128)S(1)} %fusion.175, bf16[8,64,272]{2,1,0:T(8,128)(2,1)S(1)} %fusion.173, bf16[272,64]{0,1:T(8,128)(2,1)S(1)} %get-tuple-element.596), kind=kOutput, calls=%fused_computation.3.clone.1 | convolution fusion | flops 79902720 | bytes 9783296 | tf_op jit(solution)/shard_map/while/body/eval_jaxpr/while/body/eval_jaxpr/xf,nfy->nxy/dot_general | solution.py:100
  162.6 3.8 %copy.13 = f32[8,272,272]{2,0,1:T(8,128)S(1)} copy(f32[8,272,272]{1,2,0:T(8,128)} %add_bitcast_fusion.2) | data formatting | bytes 4734976 | tf_op jit(solution)/shard_map/while/body/eval_jaxpr/while/body/eval_jaxpr/add | solution.py:102
  166.5 2.9 %fusion.176 = f32[1,272,272]{2,0,1:T(1,128)S(1)} fusion(f32[8,272,272]{2,0,1:T(8,128)S(1)} %copy.13, f32[3,8]{1,0:T(4,128)S(1)} %get-tuple-element.591, s32[]{:T(128)S(6)} %copy.17), kind=kOutput, calls=%fused_computation.33.clone.1 | convolution fusion | flops 7102464 | bytes 3638788 | tf_op jit(solution)/shard_map/while/body/eval_jaxpr/while/body/eval_jaxpr/dot_general | solution.py:103
  174.2 2.7 %add_bitcast_fusion.2 = f32[8,272,272]{1,2,0:T(8,128)} fusion(f32[8,272,272]{2,1,0:T(8,128)S(1)} %fusion.171, f32[8,272,272]{2,1,0:T(8,128)S(1)} %fusion.174, f32[8,272,272]{2,1,0:T(8,128)S(1)} %fusion.175, bf16[8,64,272]{2,1,0:T(8,128)(2,1)S(1)} %fusion.173, bf16[272,64]{0,1:T(8,128)(2,1)S(1)} %get-tuple-element.596), kind=kOutput, calls=%fused_computation.3.clone.1 | convolution fusion | flops 79902720 | bytes 9783296 | tf_op jit(solution)/shard_map/while/body/eval_jaxpr/while/body/eval_jaxpr/xf,nfy->nxy/dot_general | solution.py:100
  176.9 3.8 %copy.13 = f32[8,272,272]{2,0,1:T(8,128)S(1)} copy(f32[8,272,272]{1,2,0:T(8,128)} %add_bitcast_fusion.2) | data formatting | bytes 4734976 | tf_op jit(solution)/shard_map/while/body/eval_jaxpr/while/body/eval_jaxpr/add | solution.py:102
  180.8 2.9 %fusion.176 = f32[1,272,272]{2,0,1:T(1,128)S(1)} fusion(f32[8,272,272]{2,0,1:T(8,128)S(1)} %copy.13, f32[3,8]{1,0:T(4,128)S(1)} %get-tuple-element.591, s32[]{:T(128)S(6)} %copy.17), kind=kOutput, calls=%fused_computation.33.clone.1 | convolution fusion | flops 7102464 | bytes 3638788 | tf_op jit(solution)/shard_map/while/body/eval_jaxpr/while/body/eval_jaxpr/dot_general | solution.py:103
  188.3 3.5 %fusion.150 = f32[4,256,256]{2,1,0:T(8,128)} fusion(f32[4,256,256]{2,1,0:T(8,128)} %get-tuple-element.614, s32[]{:T(128)S(6)} %copy.24, f32[272,256]{1,0:T(8,128)S(1)} %fusion.149, f32[]{:T(128)} %get-tuple-element.638, f32[]{:T(128)} %bitcast.80, f32[]{:T(128)} %bitcast.81), kind=kOutput, calls=%fused_computation.42.clone.1 | convolution fusion | flops 214999040 | bytes 542212 | tf_op jit(solution)/shard_map/while/body/eval_jaxpr/dot_general | solution.py:108
  196.8 42.9 %while.42 = (s32[]{:T(128)}, f32[3,272,272]{2,1,0:T(8,128)}, f32[3,8]{1,0:T(4,128)S(1)}, f32[64,64]{1,0:T(8,128)S(1)}, bf16[3,8,64,128]{3,2,1,0:T(8,128)(2,1)}, ...) while((s32[]{:T(128)}, f32[3,272,272]{2,1,0:T(8,128)}, ...), condition=%wide.region_3.3_spmd.clone, body=%wide.region_2.2_spmd.clone.sunk | while | flops 386930688 | bytes 31926896 | solution.py:105
  200.8 2.7 %add_bitcast_fusion.2 = f32[8,272,272]{1,2,0:T(8,128)} fusion(f32[8,272,272]{2,1,0:T(8,128)S(1)} %fusion.171, f32[8,272,272]{2,1,0:T(8,128)S(1)} %fusion.174, f32[8,272,272]{2,1,0:T(8,128)S(1)} %fusion.175, bf16[8,64,272]{2,1,0:T(8,128)(2,1)S(1)} %fusion.173, bf16[272,64]{0,1:T(8,128)(2,1)S(1)} %get-tuple-element.596), kind=kOutput, calls=%fused_computation.3.clone.1 | convolution fusion | flops 79902720 | bytes 9783296 | tf_op jit(solution)/shard_map/while/body/eval_jaxpr/while/body/eval_jaxpr/xf,nfy->nxy/dot_general | solution.py:100
  203.5 3.8 %copy.13 = f32[8,272,272]{2,0,1:T(8,128)S(1)} copy(f32[8,272,272]{1,2,0:T(8,128)} %add_bitcast_fusion.2) | data formatting | bytes 4734976 | tf_op jit(solution)/shard_map/while/body/eval_jaxpr/while/body/eval_jaxpr/add | solution.py:102
  207.4 2.9 %fusion.176 = f32[1,272,272]{2,0,1:T(1,128)S(1)} fusion(f32[8,272,272]{2,0,1:T(8,128)S(1)} %copy.13, f32[3,8]{1,0:T(4,128)S(1)} %get-tuple-element.591, s32[]{:T(128)S(6)} %copy.17), kind=kOutput, calls=%fused_computation.33.clone.1 | convolution fusion | flops 7102464 | bytes 3638788 | tf_op jit(solution)/shard_map/while/body/eval_jaxpr/while/body/eval_jaxpr/dot_general | solution.py:103
  215.1 2.7 %add_bitcast_fusion.2 = f32[8,272,272]{1,2,0:T(8,128)} fusion(f32[8,272,272]{2,1,0:T(8,128)S(1)} %fusion.171, f32[8,272,272]{2,1,0:T(8,128)S(1)} %fusion.174, f32[8,272,272]{2,1,0:T(8,128)S(1)} %fusion.175, bf16[8,64,272]{2,1,0:T(8,128)(2,1)S(1)} %fusion.173, bf16[272,64]{0,1:T(8,128)(2,1)S(1)} %get-tuple-element.596), kind=kOutput, calls=%fused_computation.3.clone.1 | convolution fusion | flops 79902720 | bytes 9783296 | tf_op jit(solution)/shard_map/while/body/eval_jaxpr/while/body/eval_jaxpr/xf,nfy->nxy/dot_general | solution.py:100
  217.8 3.8 %copy.13 = f32[8,272,272]{2,0,1:T(8,128)S(1)} copy(f32[8,272,272]{1,2,0:T(8,128)} %add_bitcast_fusion.2) | data formatting | bytes 4734976 | tf_op jit(solution)/shard_map/while/body/eval_jaxpr/while/body/eval_jaxpr/add | solution.py:102
  221.7 2.9 %fusion.176 = f32[1,272,272]{2,0,1:T(1,128)S(1)} fusion(f32[8,272,272]{2,0,1:T(8,128)S(1)} %copy.13, f32[3,8]{1,0:T(4,128)S(1)} %get-tuple-element.591, s32[]{:T(128)S(6)} %copy.17), kind=kOutput, calls=%fused_computation.33.clone.1 | convolution fusion | flops 7102464 | bytes 3638788 | tf_op jit(solution)/shard_map/while/body/eval_jaxpr/while/body/eval_jaxpr/dot_general | solution.py:103
  229.4 2.7 %add_bitcast_fusion.2 = f32[8,272,272]{1,2,0:T(8,128)} fusion(f32[8,272,272]{2,1,0:T(8,128)S(1)} %fusion.171, f32[8,272,272]{2,1,0:T(8,128)S(1)} %fusion.174, f32[8,272,272]{2,1,0:T(8,128)S(1)} %fusion.175, bf16[8,64,272]{2,1,0:T(8,128)(2,1)S(1)} %fusion.173, bf16[272,64]{0,1:T(8,128)(2,1)S(1)} %get-tuple-element.596), kind=kOutput, calls=%fused_computation.3.clone.1 | convolution fusion | flops 79902720 | bytes 9783296 | tf_op jit(solution)/shard_map/while/body/eval_jaxpr/while/body/eval_jaxpr/xf,nfy->nxy/dot_general | solution.py:100
  232.1 3.8 %copy.13 = f32[8,272,272]{2,0,1:T(8,128)S(1)} copy(f32[8,272,272]{1,2,0:T(8,128)} %add_bitcast_fusion.2) | data formatting | bytes 4734976 | tf_op jit(solution)/shard_map/while/body/eval_jaxpr/while/body/eval_jaxpr/add | solution.py:102
  236.0 2.9 %fusion.176 = f32[1,272,272]{2,0,1:T(1,128)S(1)} fusion(f32[8,272,272]{2,0,1:T(8,128)S(1)} %copy.13, f32[3,8]{1,0:T(4,128)S(1)} %get-tuple-element.591, s32[]{:T(128)S(6)} %copy.17), kind=kOutput, calls=%fused_computation.33.clone.1 | convolution fusion | flops 7102464 | bytes 3638788 | tf_op jit(solution)/shard_map/while/body/eval_jaxpr/while/body/eval_jaxpr/dot_general | solution.py:103
  243.5 3.5 %fusion.150 = f32[4,256,256]{2,1,0:T(8,128)} fusion(f32[4,256,256]{2,1,0:T(8,128)} %get-tuple-element.614, s32[]{:T(128)S(6)} %copy.24, f32[272,256]{1,0:T(8,128)S(1)} %fusion.149, f32[]{:T(128)} %get-tuple-element.638, f32[]{:T(128)} %bitcast.80, f32[]{:T(128)} %bitcast.81), kind=kOutput, calls=%fused_computation.42.clone.1 | convolution fusion | flops 214999040 | bytes 542212 | tf_op jit(solution)/shard_map/while/body/eval_jaxpr/dot_general | solution.py:108
  (206 shorter events, 115.6 us)
Async XLA Ops:
  0.6 25.3 %copy-start.3 = (f32[4]{0:T(128)S(1)}, f32[4]{0:T(128)}, u32[]{:S(2)}) copy-start(f32[4]{0:T(128)} %param.13) | copy-start | bytes 52
  0.6 25.3 %copy-start.2 = (f32[4]{0:T(128)S(1)}, f32[4]{0:T(128)}, u32[]{:S(2)}) copy-start(f32[4]{0:T(128)} %param.12) | copy-start | bytes 52
  1.4 6.3 %collective-permute-start = (bf16[64,256]{1,0:T(8,128)(2,1)S(1)}, bf16[64,256]{1,0:T(8,128)(2,1)S(1)}, u32[]{:S(2)}, u32[]{:S(2)}) collective-permute-start(bf16[64,256]{1,0:T(8,128)(2,1)S(1)} %get-tuple-element.422), channel_id=1, source_target_pairs={{8,0},{10,2},{12,4},{14,6},{0,8},{2,10},{4,12},{6,14},{9,1},{11,3}... | collective-permute-start | bytes 98312 | tf_op jit(solution)/shard_map/ppermute | solution.py:19
  5.5 4.8 %collective-permute-start.1 = (bf16[64,256]{1,0:T(8,128)(2,1)S(1)}, bf16[64,256]{1,0:T(8,128)(2,1)S(1)}, u32[]{:S(2)}, u32[]{:S(2)}) collective-permute-start(bf16[64,256]{1,0:T(8,128)(2,1)S(1)} %get-tuple-element.423), channel_id=1, source_target_pairs={{8,0},{10,2},{12,4},{14,6},{0,8},{2,10},{4,12},{6,14},{9,1},{11,3}... | collective-permute-start | bytes 98312 | tf_op jit(solution)/shard_map/ppermute | solution.py:19
  11.4 7.5 %collective-permute-start.2 = (bf16[384,64]{1,0:T(8,128)(2,1)S(1)}, bf16[384,64]{1,0:T(8,128)(2,1)S(1)}, u32[]{:S(2)}, u32[]{:S(2)}) collective-permute-start(bf16[384,64]{1,0:T(8,128)(2,1)S(1)} %get-tuple-element.420), channel_id=1, source_target_pairs={{14,0},{0,2},{2,4},{4,6},{6,8},{8,10},{10,12},{12,14},{15,1},{1,3}... | collective-permute-start | bytes 147464 | tf_op jit(solution)/shard_map/ppermute | solution.py:19
  13.6 5.7 %collective-permute-start.3 = (bf16[384,64]{1,0:T(8,128)(2,1)S(1)}, bf16[384,64]{1,0:T(8,128)(2,1)S(1)}, u32[]{:S(2)}, u32[]{:S(2)}) collective-permute-start(bf16[384,64]{1,0:T(8,128)(2,1)S(1)} %get-tuple-element.421), channel_id=1, source_target_pairs={{2,0},{4,2},{6,4},{8,6},{10,8},{12,10},{14,12},{0,14},{3,1},{5,3},... | collective-permute-start | bytes 147464 | tf_op jit(solution)/shard_map/ppermute | solution.py:19
  26.1 2.7 %copy-start = (f32[64,64]{1,0:T(8,128)}, f32[64,64]{1,0:T(8,128)S(1)}, u32[]{:S(2)}) copy-start(f32[64,64]{1,0:T(8,128)S(1)} %get-tuple-element.634) | copy-start | bytes 49156 | tf_op jit(solution)/shard_map/while
  75.4 6.0 %copy-start.4 = (f32[4]{0:T(128)S(1)}, f32[4]{0:T(128)}, u32[]{:S(2)}) copy-start(f32[4]{0:T(128)} %get-tuple-element.666) | copy-start | bytes 52 | tf_op jit(solution)/shard_map/while
  77.8 3.5 %copy-start.1 = (f32[64,64]{1,0:T(8,128)S(1)}, f32[64,64]{1,0:T(8,128)}, u32[]{:S(2)}) copy-start(f32[64,64]{1,0:T(8,128)} %copy-done) | copy-start | bytes 49156 | tf_op jit(solution)/shard_map/while
  81.4 2.7 %copy-start = (f32[64,64]{1,0:T(8,128)}, f32[64,64]{1,0:T(8,128)S(1)}, u32[]{:S(2)}) copy-start(f32[64,64]{1,0:T(8,128)S(1)} %get-tuple-element.634) | copy-start | bytes 49156 | tf_op jit(solution)/shard_map/while
  130.6 6.0 %copy-start.4 = (f32[4]{0:T(128)S(1)}, f32[4]{0:T(128)}, u32[]{:S(2)}) copy-start(f32[4]{0:T(128)} %get-tuple-element.666) | copy-start | bytes 52 | tf_op jit(solution)/shard_map/while
  133.1 3.5 %copy-start.1 = (f32[64,64]{1,0:T(8,128)S(1)}, f32[64,64]{1,0:T(8,128)}, u32[]{:S(2)}) copy-start(f32[64,64]{1,0:T(8,128)} %copy-done) | copy-start | bytes 49156 | tf_op jit(solution)/shard_map/while
  136.6 2.7 %copy-start = (f32[64,64]{1,0:T(8,128)}, f32[64,64]{1,0:T(8,128)S(1)}, u32[]{:S(2)}) copy-start(f32[64,64]{1,0:T(8,128)S(1)} %get-tuple-element.634) | copy-start | bytes 49156 | tf_op jit(solution)/shard_map/while
  185.8 5.9 %copy-start.4 = (f32[4]{0:T(128)S(1)}, f32[4]{0:T(128)}, u32[]{:S(2)}) copy-start(f32[4]{0:T(128)} %get-tuple-element.666) | copy-start | bytes 52 | tf_op jit(solution)/shard_map/while
  188.3 3.5 %copy-start.1 = (f32[64,64]{1,0:T(8,128)S(1)}, f32[64,64]{1,0:T(8,128)}, u32[]{:S(2)}) copy-start(f32[64,64]{1,0:T(8,128)} %copy-done) | copy-start | bytes 49156 | tf_op jit(solution)/shard_map/while
  191.8 2.7 %copy-start = (f32[64,64]{1,0:T(8,128)}, f32[64,64]{1,0:T(8,128)S(1)}, u32[]{:S(2)}) copy-start(f32[64,64]{1,0:T(8,128)S(1)} %get-tuple-element.634) | copy-start | bytes 49156 | tf_op jit(solution)/shard_map/while
  241.0 6.0 %copy-start.4 = (f32[4]{0:T(128)S(1)}, f32[4]{0:T(128)}, u32[]{:S(2)}) copy-start(f32[4]{0:T(128)} %get-tuple-element.666) | copy-start | bytes 52 | tf_op jit(solution)/shard_map/while
  243.5 3.5 %copy-start.1 = (f32[64,64]{1,0:T(8,128)S(1)}, f32[64,64]{1,0:T(8,128)}, u32[]{:S(2)}) copy-start(f32[64,64]{1,0:T(8,128)} %copy-done) | copy-start | bytes 49156 | tf_op jit(solution)/shard_map/while
where the time goes:
time: 256 us; the launch traced here: 254 us
  matrix products  134 us (52%)
  local copies, waits for them, and re-layouts  79.6 us (31%)
  other arithmetic  18.6 us (7%)
  starting transfers between devices  8.9 us (3%)
  waiting for transfers between devices  7.16 us (3%)
  blocking collectives  4.36 us (2%)
    add x12, local copies, waits for them, and re-layouts, group_power(): power = field_real * field_real + field_imag * field_imag  45.8 us
    dot_general x12, matrix products, group_power(): return jnp.tensordot(weight_part, power, axes=1, precision=hp)  34.4 us
    dot_general x12, matrix products, group_power(): jnp.einsum('xf,nfy->nxy', sin_out, half_real, preferred_element_type=jnp....  32.6 us
    dot_general x4, matrix products, expose(): jnp.dot(jnp.dot(blur_rows, intensity, precision=hp), blur_rows.T, precisi...  14.1 us
    dynamic_slice x12, local copies, waits for them, and re-layouts, on_device(): resist = lax.map(one_condition, (kernels, socs_weight, dose, threshold))  12 us
    squeeze x12, local copies, waits for them, and re-layouts, expose(): lax.map(group_power, (kernel_groups, weight_groups))  11 us
    dot_general x4, matrix products, expose(): jnp.dot(blur_rows, intensity, precision=hp)  9.69 us
    dynamic_update_slice x12, local copies, waits for them, and re-layouts, expose(): lax.map(group_power, (kernel_groups, weight_groups))  9.51 us
  transfers between devices with their start and end apart: 4, of which 4 were waited for; matrix products, arithmetic and copies ran while one was open for 0% of the time, Pallas kernels for 0%

commit v1 on v0

v1 whole, which is shorter than its diff:
```python
import math

import jax
import jax.numpy as jnp
import numpy as np
from jax import lax
from jax.experimental import pallas as pl
from jax.experimental.pallas import tpu as pltpu
from jax.sharding import PartitionSpec as P

MARGIN = 64
BLUR = 8

diffusion = 2.0
steepness = 8.0


def phases(pixels, freqs, period):
    angle = 2.0 * np.pi * ((pixels[:, None] * freqs[None, :]) % period) / period
    return np.cos(angle), np.sin(angle)


def make_tables(core, band):
    pad = core + 2 * MARGIN
    freqs = np.arange(band) - band // 2
    cos_in, sin_in = phases(np.arange(pad), freqs, pad)
    row_all = np.concatenate([cos_in, -sin_in], axis=1).T
    row_core = row_all[:, MARGIN : MARGIN + core]
    row_side = np.stack([row_all[:, :MARGIN], row_all[:, MARGIN + core :]])
    order = np.concatenate(
        [np.arange(MARGIN, MARGIN + core), np.arange(MARGIN + core, pad), np.arange(MARGIN)]
    )
    col_real = np.concatenate([cos_in, -sin_in], axis=1)[order]
    col_imag = np.concatenate([sin_in, cos_in], axis=1)[order]
    grid = 2 * band
    cos_g, sin_g = phases(np.arange(grid), freqs, grid)
    half_table = np.concatenate(
        [np.concatenate([cos_g.T, sin_g.T], axis=1), np.concatenate([-sin_g.T, cos_g.T], axis=1)],
        axis=0,
    )
    field_table = np.concatenate(
        [np.concatenate([cos_g, -sin_g], axis=1), np.concatenate([sin_g, cos_g], axis=1)], axis=0
    )
    pixel = np.arange(core + 2 * BLUR) + MARGIN - BLUR
    sample = np.arange(grid) * (pad / grid)
    degrees = np.arange(1, grid // 2)
    gap = pixel[:, None] - sample[None, :]
    interp = (
        1.0 + 2.0 * np.cos(2.0 * np.pi * gap[:, :, None] * degrees / pad).sum(axis=-1)
    ) / grid
    offset = np.arange(core + 2 * BLUR)[None, :] - np.arange(core)[:, None] - BLUR
    taps = np.where(
        np.abs(offset) <= BLUR, np.exp(-(offset**2) / (2.0 * diffusion * diffusion)), 0.0
    )
    reach = np.arange(-BLUR, BLUR + 1)
    taps = taps / np.exp(-(reach**2) / (2.0 * diffusion * diffusion)).sum()
    spread = taps @ interp
    return row_core, row_side, col_real, col_imag, half_table, field_table, spread


def split(value):
    high = value.astype(jnp.bfloat16)
    low = (value - high.astype(jnp.float32)).astype(jnp.bfloat16)
    return high, low


def dot(a, b):
    return jnp.dot(a, b, preferred_element_type=jnp.float32)


def imaging(
    scal_ref,
    place_ref,
    tile_ref,
    left_ref,
    right_ref,
    *rest,
    sides,
    pad,
):
    upright_refs = rest[: len(sides)]
    (
        kern_ref,
        row_core_ref,
        row_side_ref,
        col_real_ref,
        col_imag_ref,
        half_ref,
        field_ref,
        spread_ref,
        across_ref,
        keep_ref,
        send_ref,
        halves_ref,
        coarse_ref,
    ) = rest[len(sides) :]
    conds, kerns, band, _ = kern_ref.shape
    grid = 2 * band
    core = tile_ref.shape[0]
    lane = lax.broadcasted_iota(jnp.int32, (core, 2 * MARGIN), 1)
    right_ok = place_ref[0] > 0
    left_ok = place_ref[1] > 0
    zero = jnp.zeros((core, 2 * MARGIN), jnp.float32)
    ring = jnp.where(
        lane < MARGIN,
        jnp.where(right_ok, right_ref[...].astype(jnp.float32), zero),
        jnp.where(left_ok, left_ref[...].astype(jnp.float32), zero),
    ).astype(jnp.bfloat16)
    part_core = dot(row_core_ref[...], tile_ref[...])
    part_ring = dot(row_core_ref[...], ring)
    lane = lane[:MARGIN]
    edge_ok = jnp.where(lane < MARGIN, place_ref[0], place_ref[1]) > 0
    for n, side in enumerate(sides):
        there = place_ref[2 + n] > 0
        table = row_side_ref[place_ref[4]] if side is None else row_side_ref[side]
        strip = upright_refs[n][...].astype(jnp.float32)
        strip = jnp.where(there, strip, jnp.zeros_like(strip))
        edge = jnp.where(edge_ok, strip[:, core:], jnp.zeros_like(strip[:, core:]))
        part_core = part_core + dot(table, strip[:, :core].astype(jnp.bfloat16))
        part_ring = part_ring + dot(table, edge.astype(jnp.bfloat16))
    part = jnp.concatenate([part_core, part_ring], axis=1).astype(jnp.bfloat16)
    spec = dot(part[:band], col_real_ref[...]) + dot(part[band:], col_imag_ref[...])
    spec = spec * (1.0 / pad)
    swapped = pltpu.roll(spec, band, 1)
    first = lax.broadcasted_iota(jnp.int32, spec.shape, 1) < band
    spec_same = jnp.where(first, spec, swapped)
    spec_cross = jnp.where(first, -swapped, spec)

    def condition(c, carry):
        prods = []
        for k in range(kerns):
            kern = kern_ref[c, k].astype(jnp.float32)
            prod = kern * spec_same + pltpu.roll(kern, band, 1) * spec_cross
            prods.append(prod.astype(jnp.bfloat16))
        halves_ref[...] = dot(jnp.concatenate(prods, axis=0), half_ref[...]).astype(jnp.bfloat16)
        total = jnp.zeros((grid, grid), jnp.float32)
        for k in range(0, kerns, 2):
            a = halves_ref[k * band : (k + 1) * band]
            b = halves_ref[(k + 1) * band : (k + 2) * band]
            both = jnp.concatenate(
                [
                    jnp.concatenate([a[:, :grid], b[:, :grid]], axis=1),
                    jnp.concatenate([a[:, grid:], b[:, grid:]], axis=1),
                ],
                axis=0,
            )
            field = dot(field_ref[...], both)
            power = field[:grid] * field[:grid] + field[grid:] * field[grid:]
            total = total + scal_ref[c, k] * power[:, :grid] + scal_ref[c, k + 1] * power[:, grid:]
        coarse_ref[c] = total
        return carry

    lax.fori_loop(0, conds, condition, 0)
    coarse = coarse_ref[...].reshape(conds * grid, grid)
    high, low = split(coarse)
    across = (
        dot(high, across_ref[0])
        + dot(low, across_ref[0])
        + dot(high, across_ref[1])
    )
    high, low = split(across)
    own = place_ref[5]
    share = core // 2
    for turn in range(2):
        part_of = 1 - own if turn == 0 else own
        rows = pl.ds(pl.multiple_of(part_of * share, share), share)
        most = None
        for c in range(conds):
            h = high[c * grid : (c + 1) * grid]
            l = low[c * grid : (c + 1) * grid]
            blurred = dot(spread_ref[0, rows], h)
            blurred = blurred + dot(spread_ref[0, rows], l) + dot(spread_ref[1, rows], h)
            level = scal_ref[c, kerns] * blurred - scal_ref[c, kerns + 1]
            most = level if most is None else jnp.maximum(most, level)
            least = level if c == 0 else jnp.minimum(least, level)
        if turn == 0:
            send_ref[0] = jax.nn.sigmoid(most).astype(jnp.bfloat16)
            send_ref[1] = jax.nn.sigmoid(least).astype(jnp.bfloat16)
        else:
            keep_ref[0] = jax.nn.sigmoid(most)
            keep_ref[1] = jax.nn.sigmoid(least)


def two_parts(table):
    high = np.asarray(table, np.float32).astype(jnp.bfloat16)
    low = (table - high.astype(np.float64)).astype(jnp.bfloat16)
    return np.stack([high, low])


def shifted(block, axis, distance):
    count = lax.axis_size(axis)
    return lax.ppermute(block, axis, [((i - distance) % count, i) for i in range(count)])


def on_device(mask, kernels, socs_weight, dose, threshold):
    tile = mask[0]
    core = tile.shape[0]
    conds, kerns, band, _ = kernels.shape
    pad = core + 2 * MARGIN
    grid = 2 * band
    count = lax.axis_size("tile")
    columns = min(8, count // 2)
    grid_rows = count // columns
    position = (lax.axis_index("tile") + columns // 2) % count
    column = position % columns
    row = position // columns

    left = shifted(tile[:, -2 * MARGIN :], "tile", 1)
    right = shifted(tile[:, : 2 * MARGIN], "tile", -1)

    def wide(rows):
        lane = lax.broadcasted_iota(jnp.int32, (MARGIN, 2 * MARGIN), 1)
        edge = jnp.where(lane < MARGIN, right[rows], left[rows])
        return jnp.concatenate([tile[rows], edge], axis=1)

    top, bottom = slice(0, MARGIN), slice(core - MARGIN, core)
    if grid_rows == 2:
        sides = (None,)
        strips = [shifted(jnp.where(row == 0, wide(bottom), wide(top)), "tile", columns)]
        there = [1, 1]
    else:
        sides = (0, 1)
        strips = [
            shifted(wide(bottom), "tile", columns),
            shifted(wide(top), "tile", -columns),
        ]
        there = [row > 0, row < grid_rows - 1]
    place = jnp.stack(
        [
            jnp.asarray(v, jnp.int32)
            for v in (column < columns - 1, column > 0, *there, row == 0, lax.axis_index("cond"))
        ]
    )
    norm = socs_weight / (jnp.sum(socs_weight, axis=1, keepdims=True) * (band * band))
    scal = jnp.concatenate(
        [norm, steepness * dose[:, None], steepness * threshold[:, None]], axis=1
    )
    row_core, row_side, col_real, col_imag, half_t, field_t, spread = make_tables(core, band)
    bf = lambda t: np.asarray(t).astype(jnp.bfloat16)
    consts = (
        bf(row_core),
        bf(row_side),
        bf(col_real),
        bf(col_imag),
        bf(half_t),
        bf(field_t),
        two_parts(spread),
        two_parts(spread.T),
    )
    smem = pl.BlockSpec(memory_space=pltpu.SMEM)
    vmem = pl.BlockSpec(memory_space=pltpu.VMEM)
    share = core // lax.axis_size("cond")
    keep, send = pl.pallas_call(
        lambda *refs: imaging(*refs, sides=sides, pad=pad),
        out_shape=(
            jax.ShapeDtypeStruct((2, share, core), jnp.float32),
            jax.ShapeDtypeStruct((2, share, core), jnp.bfloat16),
        ),
        in_specs=[smem, smem] + [vmem] * (4 + len(strips) + len(consts)),
        out_specs=(vmem, vmem),
        scratch_shapes=[
            pltpu.VMEM((kerns * band, 2 * grid), jnp.bfloat16),
            pltpu.VMEM((conds, grid, grid), jnp.float32),
        ],
        name="imaging",
    )(scal, place, tile, left, right, *strips, kernels, *[jnp.asarray(t) for t in consts])
    other = lax.ppermute(send, "cond", [(0, 1), (1, 0)]).astype(jnp.float32)
    return (jnp.maximum(keep[0], other[0])[None], jnp.minimum(keep[1], other[1])[None])


def solution(mesh):
    return jax.shard_map(
        on_device,
        mesh=mesh,
        in_specs=(
            P(("parts", "tile"), None, None),
            P("cond", None, None, None),
            P("cond", None),
            P("cond"),
            P("cond"),
        ),
        out_specs=(P(("parts", "tile"), "cond", None), P(("parts", "tile"), "cond", None)),
        check_vma=False,
    )
```

time: 256 us -> 32 us (0.12)
  matrix products: 134 us -> 0 us
  local copies, waits for them, and re-layouts: 79.6 us -> 3.14 us
  other arithmetic: 18.6 us -> 5.28 us
  Pallas kernels: 0 us -> 8.03 us
  blocking collectives: 4.36 us -> 0 us
  starting transfers between devices: 8.9 us -> 6.13 us
    dot_general x122 -> x0, matrix products: 134 us -> none  [the longest x12 34.4 us: group_power(): return jnp.tensordot(weight_part, power, axes=1, precision=hp)]
    add x12 -> x0, local copies, waits for them, and re-layouts: 45.8 us -> none  [group_power(): power = field_real * field_real + field_imag * field_imag]
    dynamic_slice x12 -> x0, local copies, waits for them, and re-layouts: 12 us -> none  [on_device(): resist = lax.map(one_condition, (kernels, socs_weight, dose, threshold))]
    reduce_sum x9 -> x1, other arithmetic: 11.9 us -> 0.8 us  [on_device(): jnp.sum(socs_weight, axis=1, keepdims=True) * (band * band)]
    squeeze x12 -> x0, local copies, waits for them, and re-layouts: 11 us -> none  [expose(): lax.map(group_power, (kernel_groups, weight_groups))]
    dynamic_update_slice x12 -> x0, local copies, waits for them, and re-layouts: 9.51 us -> none  [expose(): lax.map(group_power, (kernel_groups, weight_groups))]
    pallas_call x0 -> x1, Pallas kernels: none -> 8.03 us  [on_device(): pl.pallas_call(lambda *refs: imaging(*refs, sides=sides, pad=pad), out_sh...]
    all_gather x2 -> x0, blocking collectives: 4.36 us -> none  [merged(): pieces = jax.tree.map(lambda part: lax.all_gather(part, axis), value)]
  transfers between devices with their start and end apart: 4 -> 4, of which waited for: 4 -> 3; matrix products, arithmetic and copies ran while one was open for 0% -> 16% of each run, Pallas kernels for 0% -> 0%
where the time goes in v1:
time: 32 us; the launch traced here: 31.7 us
  waiting for transfers between devices  8.4 us (26%)
  Pallas kernels  8.03 us (25%)
  starting transfers between devices  6.13 us (19%)
  other arithmetic  5.28 us (16%)
  local copies, waits for them, and re-layouts  3.14 us (10%)
  between operations  0.68 us (2%)
    pallas_call x1, Pallas kernels, on_device(): pl.pallas_call(lambda *refs: imaging(*refs, sides=sides, pad=pad), out_sh...  8.03 us
    ppermute x3, waiting for transfers between devices, shifted(): lax.ppermute(block, axis, [((i - distance) % count, i) for i in range(cou...  6.85 us
    ppermute x3, starting transfers between devices, shifted(): lax.ppermute(block, axis, [((i - distance) % count, i) for i in range(cou...  6.13 us
    min x1, other arithmetic, on_device(): jnp.minimum(keep[1], other[1])[None]  1.7 us
    ppermute x1, waiting for transfers between devices, on_device(): other = lax.ppermute(send, 'cond', [(0, 1), (1, 0)]).astype(jnp.float32)  1.55 us
    slice x1, local copies, waits for them, and re-layouts, on_device(): right = shifted(tile[:, :2 * MARGIN], 'tile', -1)  0.88 us
    reduce_sum x1, other arithmetic, on_device(): jnp.sum(socs_weight, axis=1, keepdims=True) * (band * band)  0.8 us
    slice x1, local copies, waits for them, and re-layouts, wide(): return jnp.concatenate([tile[rows], edge], axis=1)  0.78 us
  transfers between devices with their start and end apart: 4, of which 3 were waited for; matrix products, arithmetic and copies ran while one was open for 16% of the time, Pallas kernels for 0%

profile of v1, /device:TPU:0, one launch (start us, length us, event | category | flops | bytes accessed | tf_op | source)
XLA Modules:
  0.0 31.7 jit_solution(14855112933006256881)
XLA Ops:
  0.6 0.9 %fusion = (bf16[256,128]{1,0:T(8,128)(2,1)S(1)}, bf16[256,128]{1,0:T(8,128)(2,1)S(1)}) fusion(bf16[256,256]{1,0:T(8,128)(2,1)} %bitcast.13), kind=kLoop, calls=%fused_computation.13 | loop fusion | bytes 262144 | tf_op jit(solution)/shard_map/slice | solution.py:209
  1.5 6.1 %collective-permute-start.1 = (bf16[256,128]{1,0:T(8,128)(2,1)S(1)}, bf16[256,128]{1,0:T(8,128)(2,1)S(1)}, u32[]{:S(2)}, u32[]{:S(2)}) collective-permute-start(bf16[256,128]{1,0:T(8,128)(2,1)S(1)} %get-tuple-element.12), channel_id=1, source_target_pairs={{2,0},{4,2},{6,4},{8,6},{10,8},{12,10},{14,12},{0,14},{3,1},{5,3},... | collective-permute-start | bytes 196616 | tf_op jit(solution)/shard_map/ppermute | solution.py:192
  7.6 0.0 collective-permute-start
  7.6 0.8 %slice_bitcast_fusion = (bf16[64,256]{1,0:T(8,128)(2,1)S(1)}, bf16[64,256]{1,0:T(8,128)(2,1)S(1)}) fusion(bf16[1,256,256]{2,1,0:T(8,128)(2,1)} %param.13), kind=kLoop, calls=%fused_computation.3 | loop fusion | bytes 131072 | tf_op jit(solution)/shard_map/slice | solution.py:214
  8.4 0.7 %multiply_bitcast_fusion.1 = f32[4,1]{0,1:T(1,128)S(1)} fusion(f32[4]{0:T(128)} %param.16), kind=kLoop, calls=%fused_computation.11 | loop fusion | flops 4 | bytes 32 | tf_op jit(solution)/shard_map/mul | solution.py:236
  9.0 0.7 %multiply_bitcast_fusion = f32[4,1]{0,1:T(1,128)S(1)} fusion(f32[4]{0:T(128)} %param.17), kind=kLoop, calls=%fused_computation.10 | loop fusion | flops 4 | bytes 32 | tf_op jit(solution)/shard_map/mul | solution.py:236
  9.7 0.8 %reduce_sum.9 = f32[4]{0:T(128)S(1)} reduce(f32[4,24]{1,0:T(4,128)} %param.15, f32[]{:T(128)} %constant.58.clone.1), dimensions={1}, to_apply=%region_0.1 | reduce | flops 92 | bytes 404 | tf_op jit(solution)/shard_map/reduce_sum | solution.py:234
  10.5 0.8 %broadcast_divide_fusion = f32[4,24]{1,0:T(4,128)S(1)} fusion(f32[4,24]{1,0:T(4,128)} %param.15, f32[4]{0:T(128)S(1)} %broadcast_multiply_fusion), kind=kLoop, calls=%fused_computation.8 | loop fusion | flops 96 | bytes 784 | tf_op jit(solution)/shard_map/div | solution.py:234
  11.2 0.1 copy.16
  11.3 0.1 copy.15
  11.4 0.0 collective-permute-done.1.refs_4_
  11.4 0.0 copy-start
  11.4 3.2 %collective-permute-done.refs_3_ = bf16[256,128]{1,0:T(8,128)(2,1)S(1)} collective-permute-done((bf16[256,128]{1,0:T(8,128)(2,1)S(1)}, bf16[256,128]{1,0:T(8,128)(2,1)S(1)}, u32[]{:S(2)}, u32[]{:S(2)}) %collective-permute-start) | collective-permute-done | bytes 65568 | tf_op jit(solution)/shard_map/ppermute | solution.py:192
  14.6 0.0 copy-start.1
  14.7 0.1 collective-permute-start.2
  14.8 0.7 %pad_maximum_fusion.refs_0_ = f32[4,26]{1,0:T(4,128)} fusion(f32[4,1]{1,0:T(4,128)S(1)} %copy.16, f32[4,1]{1,0:T(4,128)S(1)} %copy.15, f32[4,24]{1,0:T(4,128)S(1)} %broadcast_divide_fusion), kind=kLoop, calls=%fused_computation.7 | loop fusion | flops 208 | bytes 832 | tf_op jit(solution)/shard_map/concatenate | solution.py:235
  15.4 0.7 %stack.31.refs_1_ = s32[6]{0:T(128)} concatenate(s32[1]{0:T(128)} %bitcast.2, s32[1]{0:T(128)} %bitcast.3, s32[2]{0:T(128)S(1)} %broadcast.26, s32[1]{0:T(128)} %bitcast.4, s32[1]{0:T(128)} %bitcast.5), dimensions={0} | concatenate | bytes 48 | tf_op jit(solution)/shard_map/stack | solution.py:228
  16.1 3.6 %collective-permute-done.2.refs_5_ = bf16[64,384]{1,0:T(8,128)(2,1)S(1)} collective-permute-done((bf16[64,384]{1,0:T(8,128)(2,1)S(1)}, bf16[64,384]{1,0:T(8,128)(2,1)S(1)}, u32[]{:S(2)}, u32[]{:S(2)}) %collective-permute-start.2) | collective-permute-done | bytes 49184 | tf_op jit(solution)/shard_map/ppermute | solution.py:192
  19.7 0.0 copy-done
  19.7 0.0 copy-done.1
  19.7 0.0 copy-start.2
  19.7 0.6 %copy-done.2 = bf16[64,384]{1,0:T(8,128)(2,1)} copy-done((bf16[64,384]{1,0:T(8,128)(2,1)}, bf16[64,384]{1,0:T(8,128)(2,1)S(1)}, u32[]{:S(2)}) %copy-start.2) | copy-done | bytes 49176
  20.3 8.0 %imaging.1 = (f32[2,128,256]{2,1,0:T(8,128)}, bf16[2,128,256]{2,1,0:T(8,128)(2,1)}) custom-call(f32[4,26]{1,0:T(4,128)} %pad_maximum_fusion.refs_0_, s32[6]{0:T(128)} %stack.31.refs_1_, bf16[256,256]{1,0:T(8,128)(2,1)} %bitcast.14, bf16[256,128]{1,0:T(8,128)(2,1)} %copy-done.1, bf16[256,128]{1,0:T(8,128)(2,1)} %copy-done, bf16[64,384]{1,0:T(8,128)(2,1)} %copy-done.2, ...), custom_call_target="tpu_custom_call" | custom-call | tf_op jit(solution)/shard_map/imaging/pallas_call | solution.py:253
  28.4 0.0 collective-permute-start.3
  28.4 1.6 %collective-permute-done.3 = bf16[2,128,256]{2,1,0:T(8,128)(2,1)S(1)} collective-permute-done((bf16[2,128,256]{2,1,0:T(8,128)(2,1)}, bf16[2,128,256]{2,1,0:T(8,128)(2,1)S(1)}, u32[]{:S(2)}, u32[]{:S(2)}) %collective-permute-start.3) | collective-permute-done | bytes 131104 | tf_op jit(solution)/shard_map/ppermute | solution.py:267
  30.0 1.7 %slice_minimum_fusion = (f32[1,128,256]{2,1,0:T(8,128)}, f32[1,128,256]{2,1,0:T(8,128)}) fusion(f32[2,128,256]{2,1,0:T(8,128)S(1)} %convert_element_type.2, f32[2,128,256]{2,1,0:T(8,128)} %get-tuple-element.4), kind=kLoop, calls=%fused_computation | loop fusion | flops 65536 | bytes 786432 | tf_op jit(solution)/shard_map/min | solution.py:268
  (6 shorter events, 0.1 us)
Async XLA Ops:
  1.5 9.9 %collective-permute-start.1 = (bf16[256,128]{1,0:T(8,128)(2,1)S(1)}, bf16[256,128]{1,0:T(8,128)(2,1)S(1)}, u32[]{:S(2)}, u32[]{:S(2)}) collective-permute-start(bf16[256,128]{1,0:T(8,128)(2,1)S(1)} %get-tuple-element.12), channel_id=1, source_target_pairs={{2,0},{4,2},{6,4},{8,6},{10,8},{12,10},{14,12},{0,14},{3,1},{5,3},... | collective-permute-start | bytes 196616 | tf_op jit(solution)/shard_map/ppermute | solution.py:192
  7.6 7.1 %collective-permute-start = (bf16[256,128]{1,0:T(8,128)(2,1)S(1)}, bf16[256,128]{1,0:T(8,128)(2,1)S(1)}, u32[]{:S(2)}, u32[]{:S(2)}) collective-permute-start(bf16[256,128]{1,0:T(8,128)(2,1)S(1)} %get-tuple-element.13), channel_id=1, source_target_pairs={{14,0},{0,2},{2,4},{4,6},{6,8},{8,10},{10,12},{12,14},{15,1},{1,3}... | collective-permute-start | bytes 196616 | tf_op jit(solution)/shard_map/ppermute | solution.py:192
  11.4 8.3 %copy-start = (bf16[256,128]{1,0:T(8,128)(2,1)}, bf16[256,128]{1,0:T(8,128)(2,1)S(1)}, u32[]{:S(2)}) copy-start(bf16[256,128]{1,0:T(8,128)(2,1)S(1)} %collective-permute-done.1.refs_4_) | copy-start | bytes 196612
  14.6 5.1 %copy-start.1 = (bf16[256,128]{1,0:T(8,128)(2,1)}, bf16[256,128]{1,0:T(8,128)(2,1)S(1)}, u32[]{:S(2)}) copy-start(bf16[256,128]{1,0:T(8,128)(2,1)S(1)} %collective-permute-done.refs_3_) | copy-start | bytes 196612
  14.7 5.1 %collective-permute-start.2 = (bf16[64,384]{1,0:T(8,128)(2,1)S(1)}, bf16[64,384]{1,0:T(8,128)(2,1)S(1)}, u32[]{:S(2)}, u32[]{:S(2)}) collective-permute-start(bf16[64,384]{1,0:T(8,128)(2,1)S(1)} %maximum_select_fusion), channel_id=1, source_target_pairs={{8,0},{10,2},{12,4},{14,6},{0,8},{2,10},{4,12},{6,14},{9,1},{11,3}... | collective-permute-start | bytes 147464 | tf_op jit(solution)/shard_map/ppermute | solution.py:192
  19.7 0.6 %copy-start.2 = (bf16[64,384]{1,0:T(8,128)(2,1)}, bf16[64,384]{1,0:T(8,128)(2,1)S(1)}, u32[]{:S(2)}) copy-start(bf16[64,384]{1,0:T(8,128)(2,1)S(1)} %collective-permute-done.2.refs_5_) | copy-start | bytes 147460
  28.4 1.6 %collective-permute-start.3 = (bf16[2,128,256]{2,1,0:T(8,128)(2,1)}, bf16[2,128,256]{2,1,0:T(8,128)(2,1)S(1)}, u32[]{:S(2)}, u32[]{:S(2)}) collective-permute-start(bf16[2,128,256]{2,1,0:T(8,128)(2,1)} %get-tuple-element.5), channel_id=1, source_target_pairs={{0,1},{1,0},{2,3},{3,2},{4,5},{5,4},{6,7},{7,6},{8,9},{9,8},{10,11... | collective-permute-start | bytes 393224 | tf_op jit(solution)/shard_map/ppermute | solution.py:267

commit v2 on v1

--- a/solution.py
+++ b/solution.py
@@ -68,19 +68,47 @@
     return jnp.dot(a, b, preferred_element_type=jnp.float32)
 
 
-def imaging(
-    scal_ref,
-    place_ref,
-    tile_ref,
-    left_ref,
-    right_ref,
-    *rest,
-    sides,
-    pad,
-):
+def placement():
+    count = lax.axis_size("tile")
+    columns = min(8, count // 2)
+    grid_rows = count // columns
+    position = (lax.axis_index("tile") + columns // 2) % count
+    column = position % columns
+    row = position // columns
+    return dict(
+        columns=columns,
+        grid_rows=grid_rows,
+        right=column < columns - 1,
+        left=column > 0,
+        above=row > 0,
+        below=row < grid_rows - 1,
+        top=row == 0,
+        half=lax.axis_index("cond"),
+    )
+
+
+def dma_all(pairs, sems):
+    return [pltpu.make_async_copy(src, dst, sems.at[n]) for n, (src, dst) in enumerate(pairs)]
+
+
+def staging(tile_ref, *refs):
+    count = (len(refs) - 3) // 2
+    sources, targets = refs[:count], refs[count : 2 * count]
+    part_ref, tile_v, sems = refs[2 * count :]
+    copies = dma_all([(tile_ref, tile_v)] + list(zip(sources, targets)), sems)
+    for copy in copies:
+        copy.start()
+    copies[0].wait()
+    copies[1].wait()
+    part_ref[...] = dot(targets[0][...], tile_v[...])
+    for copy in copies[2:]:
+        copy.wait()
+
+
+def imaging(weight_hbm, dose_hbm, threshold_hbm, part_ref, left_ref, right_ref, *rest, sides, pad):
+    place = placement()
     upright_refs = rest[: len(sides)]
     (
-        kern_ref,
         row_core_ref,
         row_side_ref,
         col_real_ref,
@@ -89,33 +117,50 @@
         field_ref,
         spread_ref,
         across_ref,
-        keep_ref,
+        kern_ref,
         send_ref,
+        level_ref,
+        gain_ref,
         halves_ref,
         coarse_ref,
+        weight_ref,
+        dose_ref,
+        threshold_ref,
+        sems,
     ) = rest[len(sides) :]
+    copies = dma_all(
+        [(weight_hbm, weight_ref), (dose_hbm, dose_ref), (threshold_hbm, threshold_ref)], sems
+    )
+    for copy in copies:
+        copy.start()
     conds, kerns, band, _ = kern_ref.shape
     grid = 2 * band
-    core = tile_ref.shape[0]
+    core = part_ref.shape[1]
     lane = lax.broadcasted_iota(jnp.int32, (core, 2 * MARGIN), 1)
-    right_ok = place_ref[0] > 0
-    left_ok = place_ref[1] > 0
+    right_ok, left_ok = place["right"], place["left"]
     zero = jnp.zeros((core, 2 * MARGIN), jnp.float32)
     ring = jnp.where(
         lane < MARGIN,
         jnp.where(right_ok, right_ref[...].astype(jnp.float32), zero),
         jnp.where(left_ok, left_ref[...].astype(jnp.float32), zero),
     ).astype(jnp.bfloat16)
-    part_core = dot(row_core_ref[...], tile_ref[...])
+    part_core = part_ref[...]
     part_ring = dot(row_core_ref[...], ring)
     lane = lane[:MARGIN]
-    edge_ok = jnp.where(lane < MARGIN, place_ref[0], place_ref[1]) > 0
     for n, side in enumerate(sides):
-        there = place_ref[2 + n] > 0
-        table = row_side_ref[place_ref[4]] if side is None else row_side_ref[side]
         strip = upright_refs[n][...].astype(jnp.float32)
-        strip = jnp.where(there, strip, jnp.zeros_like(strip))
-        edge = jnp.where(edge_ok, strip[:, core:], jnp.zeros_like(strip[:, core:]))
+        if side is None:
+            table = row_side_ref[place["top"].astype(jnp.int32)]
+        else:
+            table = row_side_ref[side]
+            there = place["below"] if side else place["above"]
+            strip = jnp.where(there, strip, jnp.zeros_like(strip))
+        none = jnp.zeros_like(strip[:, core:])
+        edge = jnp.where(
+            lane < MARGIN,
+            jnp.where(right_ok, strip[:, core:], none),
+            jnp.where(left_ok, strip[:, core:], none),
+        )
         part_core = part_core + dot(table, strip[:, :core].astype(jnp.bfloat16))
         part_ring = part_ring + dot(table, edge.astype(jnp.bfloat16))
     part = jnp.concatenate([part_core, part_ring], axis=1).astype(jnp.bfloat16)
@@ -125,6 +170,8 @@
     first = lax.broadcasted_iota(jnp.int32, spec.shape, 1) < band
     spec_same = jnp.where(first, spec, swapped)
     spec_cross = jnp.where(first, -swapped, spec)
+    for copy in copies:
+        copy.wait()
 
     def condition(c, carry):
         prods = []
@@ -146,45 +193,56 @@
             )
             field = dot(field_ref[...], both)
             power = field[:grid] * field[:grid] + field[grid:] * field[grid:]
-            total = total + scal_ref[c, k] * power[:, :grid] + scal_ref[c, k + 1] * power[:, grid:]
+            total = (
+                total + weight_ref[c, k] * power[:, :grid] + weight_ref[c, k + 1] * power[:, grid:]
+            )
         coarse_ref[c] = total
         return carry
 
     lax.fori_loop(0, conds, condition, 0)
-    coarse = coarse_ref[...].reshape(conds * grid, grid)
-    high, low = split(coarse)
-    across = (
-        dot(high, across_ref[0])
-        + dot(low, across_ref[0])
-        + dot(high, across_ref[1])
-    )
-    high, low = split(across)
-    own = place_ref[5]
+    high, low = split(coarse_ref[...].reshape(conds * grid, grid))
+    across = dot(high, across_ref[0]) + dot(low, across_ref[0]) + dot(high, across_ref[1])
+    level_ref[0], level_ref[1] = split(across)
+    for c in range(conds):
+        mass = weight_ref[c, 0]
+        for k in range(1, kerns):
+            mass = mass + weight_ref[c, k]
+        gain_ref[0, c] = steepness * dose_ref[c] / jnp.full((8, core), mass * float(band * band))
+        gain_ref[1, c] = jnp.full((8, core), steepness * threshold_ref[c])
+    most, least = band_of(1 - place["half"], level_ref, gain_ref, spread_ref)
+    send_ref[0] = most.astype(jnp.bfloat16)
+    send_ref[1] = least.astype(jnp.bfloat16)
+
+
+def band_of(part_of, level_ref, gain_ref, spread_ref):
+    conds = gain_ref.shape[1]
+    core = spread_ref.shape[1]
+    grid = level_ref.shape[1] // conds
     share = core // 2
-    for turn in range(2):
-        part_of = 1 - own if turn == 0 else own
-        rows = pl.ds(pl.multiple_of(part_of * share, share), share)
-        most = None
-        for c in range(conds):
-            h = high[c * grid : (c + 1) * grid]
-            l = low[c * grid : (c + 1) * grid]
-            blurred = dot(spread_ref[0, rows], h)
-            blurred = blurred + dot(spread_ref[0, rows], l) + dot(spread_ref[1, rows], h)
-            level = scal_ref[c, kerns] * blurred - scal_ref[c, kerns + 1]
-            most = level if most is None else jnp.maximum(most, level)
-            least = level if c == 0 else jnp.minimum(least, level)
-        if turn == 0:
-            send_ref[0] = jax.nn.sigmoid(most).astype(jnp.bfloat16)
-            send_ref[1] = jax.nn.sigmoid(least).astype(jnp.bfloat16)
-        else:
-            keep_ref[0] = jax.nn.sigmoid(most)
-            keep_ref[1] = jax.nn.sigmoid(least)
+    rows = pl.ds(pl.multiple_of(part_of * share, share), share)
+    for c in range(conds):
+        h = level_ref[0, c * grid : (c + 1) * grid]
+        l = level_ref[1, c * grid : (c + 1) * grid]
+        blurred = dot(spread_ref[0, rows], h)
+        blurred = blurred + dot(spread_ref[0, rows], l) + dot(spread_ref[1, rows], h)
+        level = gain_ref[0, c, :1] * blurred - gain_ref[1, c, :1]
+        most = level if c == 0 else jnp.maximum(most, level)
+        least = level if c == 0 else jnp.minimum(least, level)
+    return jax.nn.sigmoid(most), jax.nn.sigmoid(least)
+
+
+def own_share(level_ref, gain_ref, spread_ref, keep_ref):
+    keep_ref[0], keep_ref[1] = band_of(lax.axis_index("cond"), level_ref, gain_ref, spread_ref)
 
 
 def two_parts(table):
     high = np.asarray(table, np.float32).astype(jnp.bfloat16)
     low = (table - high.astype(np.float64)).astype(jnp.bfloat16)
     return np.stack([high, low])
+
+
+def in_hbm(value):
+    return pltpu.with_memory_space_constraint(value, pltpu.HBM)
 
 
 def shifted(block, axis, distance):
@@ -198,12 +256,8 @@
     conds, kerns, band, _ = kernels.shape
     pad = core + 2 * MARGIN
     grid = 2 * band
-    count = lax.axis_size("tile")
-    columns = min(8, count // 2)
-    grid_rows = count // columns
-    position = (lax.axis_index("tile") + columns // 2) % count
-    column = position % columns
-    row = position // columns
+    place = placement()
+    columns, grid_rows = place["columns"], place["grid_rows"]
 
     left = shifted(tile[:, -2 * MARGIN :], "tile", 1)
     right = shifted(tile[:, : 2 * MARGIN], "tile", -1)
@@ -216,25 +270,13 @@
     top, bottom = slice(0, MARGIN), slice(core - MARGIN, core)
     if grid_rows == 2:
         sides = (None,)
-        strips = [shifted(jnp.where(row == 0, wide(bottom), wide(top)), "tile", columns)]
-        there = [1, 1]
+        strips = [shifted(jnp.where(place["top"], wide(bottom), wide(top)), "tile", columns)]
     else:
         sides = (0, 1)
         strips = [
             shifted(wide(bottom), "tile", columns),
             shifted(wide(top), "tile", -columns),
         ]
-        there = [row > 0, row < grid_rows - 1]
-    place = jnp.stack(
-        [
-            jnp.asarray(v, jnp.int32)
-            for v in (column < columns - 1, column > 0, *there, row == 0, lax.axis_index("cond"))
-        ]
-    )
-    norm = socs_weight / (jnp.sum(socs_weight, axis=1, keepdims=True) * (band * band))
-    scal = jnp.concatenate(
-        [norm, steepness * dose[:, None], steepness * threshold[:, None]], axis=1
-    )
     row_core, row_side, col_real, col_imag, half_t, field_t, spread = make_tables(core, band)
     bf = lambda t: np.asarray(t).astype(jnp.bfloat16)
     consts = (
@@ -247,24 +289,54 @@
         two_parts(spread),
         two_parts(spread.T),
     )
-    smem = pl.BlockSpec(memory_space=pltpu.SMEM)
+    consts = [jnp.asarray(t) for t in consts] + [kernels]
     vmem = pl.BlockSpec(memory_space=pltpu.VMEM)
+    hbm = pl.BlockSpec(memory_space=pltpu.HBM)
     share = core // lax.axis_size("cond")
-    keep, send = pl.pallas_call(
+    params = pltpu.CompilerParams(vmem_limit_bytes=16 * 2**20)
+    *staged, part = pl.pallas_call(
+        staging,
+        out_shape=[jax.ShapeDtypeStruct(t.shape, t.dtype) for t in consts]
+        + [jax.ShapeDtypeStruct((2 * band, core), jnp.float32)],
+        in_specs=[hbm] * (1 + len(consts)),
+        out_specs=[vmem] * (1 + len(consts)),
+        scratch_shapes=[
+            pltpu.VMEM((core, core), jnp.bfloat16),
+            pltpu.SemaphoreType.DMA((1 + len(consts),)),
+        ],
+        compiler_params=params,
+        name="staging",
+    )(in_hbm(tile), *map(in_hbm, consts))
+    send, level, gain = pl.pallas_call(
         lambda *refs: imaging(*refs, sides=sides, pad=pad),
         out_shape=(
-            jax.ShapeDtypeStruct((2, share, core), jnp.float32),
             jax.ShapeDtypeStruct((2, share, core), jnp.bfloat16),
+            jax.ShapeDtypeStruct((2, conds * grid, core), jnp.bfloat16),
+            jax.ShapeDtypeStruct((2, conds, 8, core), jnp.float32),
         ),
-        in_specs=[smem, smem] + [vmem] * (4 + len(strips) + len(consts)),
-        out_specs=(vmem, vmem),
+        in_specs=[hbm] * 3 + [vmem] * (3 + len(strips) + len(staged)),
+        out_specs=(vmem, vmem, vmem),
         scratch_shapes=[
             pltpu.VMEM((kerns * band, 2 * grid), jnp.bfloat16),
             pltpu.VMEM((conds, grid, grid), jnp.float32),
+            pltpu.SMEM(socs_weight.shape, jnp.float32),
+            pltpu.SMEM(dose.shape, jnp.float32),
+            pltpu.SMEM(threshold.shape, jnp.float32),
+            pltpu.SemaphoreType.DMA((3,)),
         ],
+        compiler_params=params,
         name="imaging",
-    )(scal, place, tile, left, right, *strips, kernels, *[jnp.asarray(t) for t in consts])
-    other = lax.ppermute(send, "cond", [(0, 1), (1, 0)]).astype(jnp.float32)
+    )(in_hbm(socs_weight), in_hbm(dose), in_hbm(threshold), part, left, right, *strips, *staged)
+    other = lax.ppermute(send, "cond", [(0, 1), (1, 0)])
+    keep = pl.pallas_call(
+        own_share,
+        out_shape=jax.ShapeDtypeStruct((2, share, core), jnp.float32),
+        in_specs=[vmem] * 3,
+        out_specs=vmem,
+        compiler_params=params,
+        name="own_share",
+    )(level, gain, staged[6])
+    other = other.astype(jnp.float32)
     return (jnp.maximum(keep[0], other[0])[None], jnp.minimum(keep[1], other[1])[None])
 
 

time: 32 us -> 28.2 us (0.88)
  other arithmetic: 5.28 us -> 0.78 us
  waiting for transfers between devices: 8.4 us -> 10.6 us
  local copies, waits for them, and re-layouts: 3.14 us -> 1.66 us
    ppermute x3, waiting for transfers between devices: 6.85 us -> 9.71 us  [shifted(): lax.ppermute(block, axis, [((i - distance) % count, i) for i in range(cou...]
    pallas_call x1, Pallas kernels: 8.03 us -> 5.64 us  [on_device(): pl.pallas_call(lambda *refs: imaging(*refs, sides=sides, pad=pad), out_sh...]
    pallas_call x0 -> x2, Pallas kernels: none -> 2.27 us  [the longest x1 1.89 us: on_device(): pl.pallas_call(staging, out_shape=[jax.ShapeDtypeStruct(t.shape, t.dtype)...]
    mul x3 -> x0, other arithmetic: 1.32 us -> none  [the longest x1 0.66 us: on_device(): steepness * dose[:, None]]
    min x1, other arithmetic: 1.7 us -> 0.73 us  [on_device(): jnp.minimum(keep[1], other[1])[None]]
    reduce_sum x1 -> x0, other arithmetic: 0.8 us -> none  [on_device(): jnp.sum(socs_weight, axis=1, keepdims=True) * (band * band)]
    div x1 -> x0, other arithmetic: 0.75 us -> none  [on_device(): socs_weight / (jnp.sum(socs_weight, axis=1, keepdims=True) * (band * band))]
    another operation x2 -> x0, local copies, waits for them, and re-layouts: 0.67 us -> none  [the longest x1 0.67 us: on_device(): jnp.stack([jnp.asarray(v, jnp.int32) for v in (column < columns - 1, colu...]
  transfers between devices with their start and end apart: 4 -> 4, of which waited for: 3 -> 4; matrix products, arithmetic and copies ran while one was open for 16% -> 3% of each run, Pallas kernels for 0% -> 8%
where the time goes in v2:
time: 28.2 us; the launch traced here: 27.9 us
  waiting for transfers between devices  10.6 us (38%)
  Pallas kernels  7.91 us (28%)
  starting transfers between devices  6.2 us (22%)
  local copies, waits for them, and re-layouts  1.66 us (6%)
  other arithmetic  0.78 us (3%)
  between operations  0.69 us (2%)
    ppermute x3, waiting for transfers between devices, shifted(): lax.ppermute(block, axis, [((i - distance) % count, i) for i in range(cou...  9.71 us
    ppermute x3, starting transfers between devices, shifted(): lax.ppermute(block, axis, [((i - distance) % count, i) for i in range(cou...  6.13 us
    pallas_call x1, Pallas kernels, on_device(): pl.pallas_call(lambda *refs: imaging(*refs, sides=sides, pad=pad), out_sh...  5.64 us
    pallas_call x1, Pallas kernels, on_device(): pl.pallas_call(staging, out_shape=[jax.ShapeDtypeStruct(t.shape, t.dtype)...  1.89 us
    ppermute x1, waiting for transfers between devices, on_device(): other = lax.ppermute(send, 'cond', [(0, 1), (1, 0)])  0.94 us
    slice x1, local copies, waits for them, and re-layouts, on_device(): right = shifted(tile[:, :2 * MARGIN], 'tile', -1)  0.88 us
    slice x1, local copies, waits for them, and re-layouts, wide(): return jnp.concatenate([tile[rows], edge], axis=1)  0.78 us
    min x1, other arithmetic, on_device(): jnp.minimum(keep[1], other[1])[None]  0.73 us
  transfers between devices with their start and end apart: 4, of which 4 were waited for; matrix products, arithmetic and copies ran while one was open for 3% of the time, Pallas kernels for 8%

profile of v2, /device:TPU:0, one launch (start us, length us, event | category | flops | bytes accessed | tf_op | source)
XLA Modules:
  0.0 27.9 jit_solution(190758716999154983)
XLA Ops:
  0.6 0.9 %fusion = (bf16[256,128]{1,0:T(8,128)(2,1)S(1)}, bf16[256,128]{1,0:T(8,128)(2,1)S(1)}) fusion(bf16[256,256]{1,0:T(8,128)(2,1)} %bitcast.5), kind=kLoop, calls=%fused_computation.8 | loop fusion | bytes 262144 | tf_op jit(solution)/shard_map/slice | solution.py:263
  1.5 6.1 %collective-permute-start.1 = (bf16[256,128]{1,0:T(8,128)(2,1)S(1)}, bf16[256,128]{1,0:T(8,128)(2,1)S(1)}, u32[]{:S(2)}, u32[]{:S(2)}) collective-permute-start(bf16[256,128]{1,0:T(8,128)(2,1)S(1)} %get-tuple-element.34), channel_id=1, source_target_pairs={{2,0},{4,2},{6,4},{8,6},{10,8},{12,10},{14,12},{0,14},{3,1},{5,3},... | collective-permute-start | bytes 196616 | tf_op jit(solution)/shard_map/ppermute | solution.py:250
  7.6 0.0 collective-permute-start
  7.6 0.8 %slice_bitcast_fusion = (bf16[64,256]{1,0:T(8,128)(2,1)S(1)}, bf16[64,256]{1,0:T(8,128)(2,1)S(1)}) fusion(bf16[1,256,256]{2,1,0:T(8,128)(2,1)} %param.13), kind=kLoop, calls=%fused_computation.3 | loop fusion | bytes 131072 | tf_op jit(solution)/shard_map/slice | solution.py:268
  8.4 1.1 %collective-permute-done.1.refs_5_ = bf16[256,128]{1,0:T(8,128)(2,1)S(1)} collective-permute-done((bf16[256,128]{1,0:T(8,128)(2,1)S(1)}, bf16[256,128]{1,0:T(8,128)(2,1)S(1)}, u32[]{:S(2)}, u32[]{:S(2)}) %collective-permute-start.1) | collective-permute-done | bytes 65568 | tf_op jit(solution)/shard_map/ppermute | solution.py:250
  9.5 5.5 %collective-permute-done.refs_4_ = bf16[256,128]{1,0:T(8,128)(2,1)S(1)} collective-permute-done((bf16[256,128]{1,0:T(8,128)(2,1)S(1)}, bf16[256,128]{1,0:T(8,128)(2,1)S(1)}, u32[]{:S(2)}, u32[]{:S(2)}) %collective-permute-start) | collective-permute-done | bytes 65568 | tf_op jit(solution)/shard_map/ppermute | solution.py:250
  15.0 0.1 collective-permute-start.2
  15.1 1.9 %staging.1 = (bf16[128,256]{1,0:T(8,128)(2,1)S(1)}, bf16[2,128,64]{2,1,0:T(8,128)(2,1)S(1)}, bf16[384,128]{1,0:T(8,128)(2,1)S(1)}, bf16[384,128]{1,0:T(8,128)(2,...) custom-call(bf16[256,256]{1,0:T(8,128)(2,1)} %bitcast.6, ...), custom_call_target="tpu_custom_call" | custom-call | tf_op jit(solution)/shard_map/staging/pallas_call | solution.py:297
  17.0 3.1 %collective-permute-done.2.refs_6_ = bf16[64,384]{1,0:T(8,128)(2,1)S(1)} collective-permute-done((bf16[64,384]{1,0:T(8,128)(2,1)S(1)}, bf16[64,384]{1,0:T(8,128)(2,1)S(1)}, u32[]{:S(2)}, u32[]{:S(2)}) %collective-permute-start.2) | collective-permute-done | bytes 49184 | tf_op jit(solution)/shard_map/ppermute | solution.py:250
  20.1 5.6 %imaging.1 = (bf16[2,128,256]{2,1,0:T(8,128)(2,1)S(1)}, bf16[2,512,256]{2,1,0:T(8,128)(2,1)S(1)}, f32[2,4,8,256]{3,2,1,0:T(8,128)S(1)}) custom-call(f32[4,24]{1,0:T(4,128)} %refs_0_.2, f32[4]{0:T(128)} %refs_1_.2, f32[4]{0:T(128)} %refs_2_.2, f32[128,256]{1,0:T(8,128)S(1)} %get-tuple-element.15.refs_3_, bf16[256,128]{1,0:T(8,128)(2,1)S(1)} %collective-permute-done.refs_4_, ...), custom_call_target="tpu_custom_call" | custom-call | tf_op jit(solution)/shard_map/imaging/pallas_call | solution.py:310
  25.7 0.1 collective-permute-start.3
  25.8 0.4 %own_share.1 = f32[2,128,256]{2,1,0:T(8,128)S(1)} custom-call(bf16[2,512,256]{2,1,0:T(8,128)(2,1)S(1)} %get-tuple-element.25.level_ref, f32[2,4,8,256]{3,2,1,0:T(8,128)S(1)} %get-tuple-element.26.gain_ref, bf16[2,256,128]{2,1,0:T(8,128)(2,1)S(1)} %get-tuple-element.22.refs_13_.spread_ref), custom_call_target="tpu_custom_call" | custom-call | tf_op jit(solution)/shard_map/own_share/pallas_call | solution.py:331
  26.2 0.9 %collective-permute-done.3 = bf16[2,128,256]{2,1,0:T(8,128)(2,1)S(1)} collective-permute-done((bf16[2,128,256]{2,1,0:T(8,128)(2,1)S(1)}, bf16[2,128,256]{2,1,0:T(8,128)(2,1)S(1)}, u32[]{:S(2)}, u32[]{:S(2)}) %collective-permute-start.3) | collective-permute-done | bytes 131104 | tf_op jit(solution)/shard_map/ppermute | solution.py:330
  27.2 0.7 %slice_minimum_fusion = (f32[1,128,256]{2,1,0:T(8,128)}, f32[1,128,256]{2,1,0:T(8,128)}) fusion(f32[2,128,256]{2,1,0:T(8,128)S(1)} %convert_element_type.3, f32[2,128,256]{2,1,0:T(8,128)S(1)} %own_share.1), kind=kLoop, calls=%fused_computation | loop fusion | flops 65536 | bytes 786432 | tf_op jit(solution)/shard_map/min | solution.py:340
  (4 shorter events, 0.0 us)
Async XLA Ops:
  1.5 8.0 %collective-permute-start.1 = (bf16[256,128]{1,0:T(8,128)(2,1)S(1)}, bf16[256,128]{1,0:T(8,128)(2,1)S(1)}, u32[]{:S(2)}, u32[]{:S(2)}) collective-permute-start(bf16[256,128]{1,0:T(8,128)(2,1)S(1)} %get-tuple-element.34), channel_id=1, source_target_pairs={{2,0},{4,2},{6,4},{8,6},{10,8},{12,10},{14,12},{0,14},{3,1},{5,3},... | collective-permute-start | bytes 196616 | tf_op jit(solution)/shard_map/ppermute | solution.py:250
  7.6 7.4 %collective-permute-start = (bf16[256,128]{1,0:T(8,128)(2,1)S(1)}, bf16[256,128]{1,0:T(8,128)(2,1)S(1)}, u32[]{:S(2)}, u32[]{:S(2)}) collective-permute-start(bf16[256,128]{1,0:T(8,128)(2,1)S(1)} %get-tuple-element.35), channel_id=1, source_target_pairs={{14,0},{0,2},{2,4},{4,6},{6,8},{8,10},{10,12},{12,14},{15,1},{1,3}... | collective-permute-start | bytes 196616 | tf_op jit(solution)/shard_map/ppermute | solution.py:250
  15.0 5.1 %collective-permute-start.2 = (bf16[64,384]{1,0:T(8,128)(2,1)S(1)}, bf16[64,384]{1,0:T(8,128)(2,1)S(1)}, u32[]{:S(2)}, u32[]{:S(2)}) collective-permute-start(bf16[64,384]{1,0:T(8,128)(2,1)S(1)} %maximum_select_fusion), channel_id=1, source_target_pairs={{8,0},{10,2},{12,4},{14,6},{0,8},{2,10},{4,12},{6,14},{9,1},{11,3}... | collective-permute-start | bytes 147464 | tf_op jit(solution)/shard_map/ppermute | solution.py:250
  25.7 1.4 %collective-permute-start.3 = (bf16[2,128,256]{2,1,0:T(8,128)(2,1)S(1)}, bf16[2,128,256]{2,1,0:T(8,128)(2,1)S(1)}, u32[]{:S(2)}, u32[]{:S(2)}) collective-permute-start(bf16[2,128,256]{2,1,0:T(8,128)(2,1)S(1)} %get-tuple-element.27), channel_id=1, source_target_pairs={{0,1},{1,0},{2,3},{3,2},{4,5},{5,4},{6,7},{7,6},{8,9},{9,8},{10,11... | collective-permute-start | bytes 393224 | tf_op jit(solution)/shard_map/ppermute | solution.py:330

commit v3 on v2

--- a/solution.py
+++ b/solution.py
@@ -27,11 +27,18 @@
     row_all = np.concatenate([cos_in, -sin_in], axis=1).T
     row_core = row_all[:, MARGIN : MARGIN + core]
     row_side = np.stack([row_all[:, :MARGIN], row_all[:, MARGIN + core :]])
-    order = np.concatenate(
-        [np.arange(MARGIN, MARGIN + core), np.arange(MARGIN + core, pad), np.arange(MARGIN)]
-    )
-    col_real = np.concatenate([cos_in, -sin_in], axis=1)[order]
-    col_imag = np.concatenate([sin_in, cos_in], axis=1)[order]
+    table = np.stack(
+        [np.concatenate([cos_in, -sin_in], axis=1), np.concatenate([sin_in, cos_in], axis=1)]
+    )
+    none = np.zeros((2, MARGIN, 2 * band))
+    half = core // 2
+    middle = MARGIN + half
+    columns = np.stack(
+        [
+            np.concatenate([table[:, MARGIN:middle], none, table[:, :MARGIN]], axis=1),
+            np.concatenate([table[:, middle : middle + half], table[:, -MARGIN:], none], axis=1),
+        ]
+    )
     grid = 2 * band
     cos_g, sin_g = phases(np.arange(grid), freqs, grid)
     half_table = np.concatenate(
@@ -55,7 +62,7 @@
     reach = np.arange(-BLUR, BLUR + 1)
     taps = taps / np.exp(-(reach**2) / (2.0 * diffusion * diffusion)).sum()
     spread = taps @ interp
-    return row_core, row_side, col_real, col_imag, half_table, field_table, spread
+    return row_core, row_side, columns, half_table, field_table, spread
 
 
 def split(value):
@@ -91,43 +98,71 @@
     return [pltpu.make_async_copy(src, dst, sems.at[n]) for n, (src, dst) in enumerate(pairs)]
 
 
-def staging(tile_ref, *refs):
-    count = (len(refs) - 3) // 2
-    sources, targets = refs[:count], refs[count : 2 * count]
-    part_ref, tile_v, sems = refs[2 * count :]
-    copies = dma_all([(tile_ref, tile_v)] + list(zip(sources, targets)), sems)
+def staging(*refs):
+    count = (len(refs) - 1) // 2
+    own = lax.axis_index("cond")
+    sources = [refs[0].at[own], *refs[1:count]]
+    copies = dma_all(zip(sources, refs[count : 2 * count]), refs[-1])
     for copy in copies:
         copy.start()
-    copies[0].wait()
-    copies[1].wait()
-    part_ref[...] = dot(targets[0][...], tile_v[...])
-    for copy in copies[2:]:
+    for copy in copies:
         copy.wait()
 
 
-def imaging(weight_hbm, dose_hbm, threshold_hbm, part_ref, left_ref, right_ref, *rest, sides, pad):
+def row_analysis(tile_hbm, strip_ref, row_core_ref, part_ref, tile_ref, sem):
+    half = tile_ref.shape[1]
+    first = pl.multiple_of(lax.axis_index("cond") * half, half)
+    copy = pltpu.make_async_copy(tile_hbm.at[:, pl.ds(first, half)], tile_ref, sem)
+    copy.start()
+    part_ref[:, half:] = dot(row_core_ref[...], strip_ref[...])
+    copy.wait()
+    part_ref[:, :half] = dot(row_core_ref[...], tile_ref[...])
+
+
+def spectrum(part_ref, row_side_ref, columns_ref, *rest, sides):
+    *upright_refs, spec_ref = rest
     place = placement()
-    upright_refs = rest[: len(sides)]
-    (
-        row_core_ref,
-        row_side_ref,
-        col_real_ref,
-        col_imag_ref,
-        half_ref,
-        field_ref,
-        spread_ref,
-        across_ref,
-        kern_ref,
-        send_ref,
-        level_ref,
-        gain_ref,
-        halves_ref,
-        coarse_ref,
-        weight_ref,
-        dose_ref,
-        threshold_ref,
-        sems,
-    ) = rest[len(sides) :]
+    band = spec_ref.shape[0]
+    half = part_ref.shape[1] - 2 * MARGIN
+    part = part_ref[...]
+    for n, side in enumerate(sides):
+        if side is None:
+            table = row_side_ref[place["top"].astype(jnp.int32)]
+            part = part + dot(table, upright_refs[n][...])
+        else:
+            there = place["below"] if side else place["above"]
+            more = dot(row_side_ref[side], upright_refs[n][...])
+            part = part + jnp.where(there, more, jnp.zeros_like(more))
+    edge = part[:, half:]
+    beside = jnp.where(place["half"] == 0, place["left"], place["right"])
+    edge = jnp.where(beside, edge, jnp.zeros_like(edge))
+    part = jnp.concatenate([part[:, :half], edge], axis=1).astype(jnp.bfloat16)
+    spec_ref[...] = dot(part[:band], columns_ref[0]) + dot(part[band:], columns_ref[1])
+
+
+def imaging(
+    weight_hbm,
+    dose_hbm,
+    threshold_hbm,
+    mine_ref,
+    other_ref,
+    half_ref,
+    field_ref,
+    spread_ref,
+    across_ref,
+    kern_ref,
+    send_ref,
+    level_ref,
+    gain_ref,
+    halves_ref,
+    coarse_ref,
+    weight_ref,
+    dose_ref,
+    threshold_ref,
+    sems,
+    *,
+    pad,
+):
     copies = dma_all(
         [(weight_hbm, weight_ref), (dose_hbm, dose_ref), (threshold_hbm, threshold_ref)], sems
     )
@@ -135,37 +170,8 @@
         copy.start()
     conds, kerns, band, _ = kern_ref.shape
     grid = 2 * band
-    core = part_ref.shape[1]
-    lane = lax.broadcasted_iota(jnp.int32, (core, 2 * MARGIN), 1)
-    right_ok, left_ok = place["right"], place["left"]
-    zero = jnp.zeros((core, 2 * MARGIN), jnp.float32)
-    ring = jnp.where(
-        lane < MARGIN,
-        jnp.where(right_ok, right_ref[...].astype(jnp.float32), zero),
-        jnp.where(left_ok, left_ref[...].astype(jnp.float32), zero),
-    ).astype(jnp.bfloat16)
-    part_core = part_ref[...]
-    part_ring = dot(row_core_ref[...], ring)
-    lane = lane[:MARGIN]
-    for n, side in enumerate(sides):
-        strip = upright_refs[n][...].astype(jnp.float32)
-        if side is None:
-            table = row_side_ref[place["top"].astype(jnp.int32)]
-        else:
-            table = row_side_ref[side]
-            there = place["below"] if side else place["above"]
-            strip = jnp.where(there, strip, jnp.zeros_like(strip))
-        none = jnp.zeros_like(strip[:, core:])
-        edge = jnp.where(
-            lane < MARGIN,
-            jnp.where(right_ok, strip[:, core:], none),
-            jnp.where(left_ok, strip[:, core:], none),
-        )
-        part_core = part_core + dot(table, strip[:, :core].astype(jnp.bfloat16))
-        part_ring = part_ring + dot(table, edge.astype(jnp.bfloat16))
-    part = jnp.concatenate([part_core, part_ring], axis=1).astype(jnp.bfloat16)
-    spec = dot(part[:band], col_real_ref[...]) + dot(part[band:], col_imag_ref[...])
-    spec = spec * (1.0 / pad)
+    core = spread_ref.shape[1]
+    spec = (mine_ref[...] + other_ref[...]) * (1.0 / pad)
     swapped = pltpu.roll(spec, band, 1)
     first = lax.broadcasted_iota(jnp.int32, spec.shape, 1) < band
     spec_same = jnp.where(first, spec, swapped)
@@ -209,7 +215,7 @@
             mass = mass + weight_ref[c, k]
         gain_ref[0, c] = steepness * dose_ref[c] / jnp.full((8, core), mass * float(band * band))
         gain_ref[1, c] = jnp.full((8, core), steepness * threshold_ref[c])
-    most, least = band_of(1 - place["half"], level_ref, gain_ref, spread_ref)
+    most, least = band_of(1 - lax.axis_index("cond"), level_ref, gain_ref, spread_ref)
     send_ref[0] = most.astype(jnp.bfloat16)
     send_ref[1] = least.astype(jnp.bfloat16)
 
@@ -257,64 +263,78 @@
     pad = core + 2 * MARGIN
     grid = 2 * band
     place = placement()
+    count = lax.axis_size("tile")
     columns, grid_rows = place["columns"], place["grid_rows"]
 
-    left = shifted(tile[:, -2 * MARGIN :], "tile", 1)
-    right = shifted(tile[:, : 2 * MARGIN], "tile", -1)
-
-    def wide(rows):
-        lane = lax.broadcasted_iota(jnp.int32, (MARGIN, 2 * MARGIN), 1)
-        edge = jnp.where(lane < MARGIN, right[rows], left[rows])
-        return jnp.concatenate([tile[rows], edge], axis=1)
-
-    top, bottom = slice(0, MARGIN), slice(core - MARGIN, core)
+    half, wide = core // 2, 2 * MARGIN
+    left_core = lax.axis_index("cond") == 0
+    others = [((t - 1) % count, t) for t in range(count)]
+    route = [(2 * a, 2 * b) for a, b in others] + [(2 * b + 1, 2 * a + 1) for a, b in others]
+    strip = lax.ppermute(
+        jnp.where(left_core, tile[:, -wide:], tile[:, :wide]), ("tile", "cond"), route
+    )
+    columns_own = jnp.where(left_core, tile[:, :half], tile[:, half:])
+    upper = jnp.concatenate([columns_own[:MARGIN], strip[:MARGIN]], axis=1)
+    lower = jnp.concatenate([columns_own[-MARGIN:], strip[-MARGIN:]], axis=1)
     if grid_rows == 2:
         sides = (None,)
-        strips = [shifted(jnp.where(place["top"], wide(bottom), wide(top)), "tile", columns)]
+        uprights = [shifted(jnp.where(place["top"], lower, upper), "tile", columns)]
     else:
         sides = (0, 1)
-        strips = [
-            shifted(wide(bottom), "tile", columns),
-            shifted(wide(top), "tile", -columns),
-        ]
-    row_core, row_side, col_real, col_imag, half_t, field_t, spread = make_tables(core, band)
-    bf = lambda t: np.asarray(t).astype(jnp.bfloat16)
-    consts = (
+        uprights = [shifted(lower, "tile", columns), shifted(upper, "tile", -columns)]
+    row_core, row_side, col_table, half_t, field_t, spread = make_tables(core, band)
+    bf = lambda t: jnp.asarray(np.asarray(t).astype(jnp.bfloat16))
+    fixed = [
+        bf(col_table),
         bf(row_core),
         bf(row_side),
-        bf(col_real),
-        bf(col_imag),
         bf(half_t),
         bf(field_t),
-        two_parts(spread),
-        two_parts(spread.T),
-    )
-    consts = [jnp.asarray(t) for t in consts] + [kernels]
+        jnp.asarray(two_parts(spread)),
+        jnp.asarray(two_parts(spread.T)),
+        kernels,
+    ]
     vmem = pl.BlockSpec(memory_space=pltpu.VMEM)
     hbm = pl.BlockSpec(memory_space=pltpu.HBM)
     share = core // lax.axis_size("cond")
     params = pltpu.CompilerParams(vmem_limit_bytes=16 * 2**20)
-    *staged, part = pl.pallas_call(
+    shapes = [t.shape for t in fixed]
+    shapes[0] = shapes[0][1:]
+    col_v, row_v, side_v, half_v, field_v, spread_v, across_v, kernels_v = pl.pallas_call(
         staging,
-        out_shape=[jax.ShapeDtypeStruct(t.shape, t.dtype) for t in consts]
-        + [jax.ShapeDtypeStruct((2 * band, core), jnp.float32)],
-        in_specs=[hbm] * (1 + len(consts)),
-        out_specs=[vmem] * (1 + len(consts)),
-        scratch_shapes=[
-            pltpu.VMEM((core, core), jnp.bfloat16),
-            pltpu.SemaphoreType.DMA((1 + len(consts),)),
-        ],
+        out_shape=[jax.ShapeDtypeStruct(z, jnp.bfloat16) for z in shapes],
+        in_specs=[hbm] * len(fixed),
+        out_specs=[vmem] * len(fixed),
+        scratch_shapes=[pltpu.SemaphoreType.DMA((len(fixed),))],
         compiler_params=params,
         name="staging",
-    )(in_hbm(tile), *map(in_hbm, consts))
+    )(*map(in_hbm, fixed))
+    part = pl.pallas_call(
+        row_analysis,
+        out_shape=jax.ShapeDtypeStruct((2 * band, half + wide), jnp.float32),
+        in_specs=[hbm, vmem, vmem],
+        out_specs=vmem,
+        scratch_shapes=[pltpu.VMEM((core, half), jnp.bfloat16), pltpu.SemaphoreType.DMA],
+        compiler_params=params,
+        name="row_analysis",
+    )(in_hbm(tile), strip, row_v)
+    mine = pl.pallas_call(
+        lambda *refs: spectrum(*refs, sides=sides),
+        out_shape=jax.ShapeDtypeStruct((band, grid), jnp.float32),
+        in_specs=[vmem] * (3 + len(uprights)),
+        out_specs=vmem,
+        compiler_params=params,
+        name="spectrum",
+    )(part, side_v, col_v, *uprights)
+    other = lax.ppermute(mine, "cond", [(0, 1), (1, 0)])
     send, level, gain = pl.pallas_call(
-        lambda *refs: imaging(*refs, sides=sides, pad=pad),
+        lambda *refs: imaging(*refs, pad=pad),
         out_shape=(
             jax.ShapeDtypeStruct((2, share, core), jnp.bfloat16),
             jax.ShapeDtypeStruct((2, conds * grid, core), jnp.bfloat16),
             jax.ShapeDtypeStruct((2, conds, 8, core), jnp.float32),
         ),
-        in_specs=[hbm] * 3 + [vmem] * (3 + len(strips) + len(staged)),
+        in_specs=[hbm] * 3 + [vmem] * 7,
         out_specs=(vmem, vmem, vmem),
         scratch_shapes=[
             pltpu.VMEM((kerns * band, 2 * grid), jnp.bfloat16),
@@ -326,7 +346,18 @@
         ],
         compiler_params=params,
         name="imaging",
-    )(in_hbm(socs_weight), in_hbm(dose), in_hbm(threshold), part, left, right, *strips, *staged)
+    )(
+        in_hbm(socs_weight),
+        in_hbm(dose),
+        in_hbm(threshold),
+        mine,
+        other,
+        half_v,
+        field_v,
+        spread_v,
+        across_v,
+        kernels_v,
+    )
     other = lax.ppermute(send, "cond", [(0, 1), (1, 0)])
     keep = pl.pallas_call(
         own_share,
@@ -335,7 +366,7 @@
         out_specs=vmem,
         compiler_params=params,
         name="own_share",
-    )(level, gain, staged[6])
+    )(level, gain, spread_v)
     other = other.astype(jnp.float32)
     return (jnp.maximum(keep[0], other[0])[None], jnp.minimum(keep[1], other[1])[None])
 

time: 28.2 us -> 24.4 us (0.87)
  waiting for transfers between devices: 10.6 us -> 8.26 us
  starting transfers between devices: 6.2 us -> 4.36 us
  local copies, waits for them, and re-layouts: 1.66 us -> 0.01 us
  Pallas kernels: 7.91 us -> 9.12 us
  other arithmetic: 0.78 us -> 1.65 us
    ppermute x3 -> x1, waiting for transfers between devices: 9.71 us -> 1 us  [shifted(): lax.ppermute(block, axis, [((i - distance) % count, i) for i in range(cou...]
    ppermute x0 -> x2, waiting for transfers between devices: none -> 6.47 us  [the longest x1 5.28 us: on_device(): lax.ppermute(jnp.where(left_core, tile[:, -wide:], tile[:, :wide]), ('til...]
    ppermute x3 -> x1, starting transfers between devices: 6.13 us -> 1.04 us  [shifted(): lax.ppermute(block, axis, [((i - distance) % count, i) for i in range(cou...]
    ppermute x0 -> x2, starting transfers between devices: none -> 3.09 us  [the longest x1 3.02 us: on_device(): lax.ppermute(jnp.where(left_core, tile[:, -wide:], tile[:, :wide]), ('til...]
    slice x2, local copies, waits for them, and re-layouts: 1.66 us -> 0.01 us  [on_device(): upper = jnp.concatenate([columns_own[:MARGIN], strip[:MARGIN]], axis=1)]
    pallas_call x2 -> x4, Pallas kernels: 7.52 us -> 8.73 us  [the longest x1 5.62 us: on_device(): pl.pallas_call(lambda *refs: imaging(*refs, pad=pad), out_shape=(jax.Shap...]
    select_n x2, other arithmetic: 0.03 us -> 0.9 us  [the longest x1 0.89 us: on_device(): columns_own = jnp.where(left_core, tile[:, :half], tile[:, half:])]
  transfers between devices with their start and end apart: 4 -> 4, of which waited for: 4 -> 4; matrix products, arithmetic and copies ran while one was open for 3% -> 0% of each run, Pallas kernels for 8% -> 13%
where the time goes in v3:
time: 24.4 us; the launch traced here: 24.1 us
  Pallas kernels  9.12 us (37%)
  waiting for transfers between devices  8.26 us (34%)
  starting transfers between devices  4.36 us (18%)
  other arithmetic  1.65 us (7%)
  between operations  0.7 us (3%)
    pallas_call x1, Pallas kernels, on_device(): pl.pallas_call(lambda *refs: imaging(*refs, pad=pad), out_shape=(jax.Shap...  5.62 us
    ppermute x1, waiting for transfers between devices, on_device(): lax.ppermute(jnp.where(left_core, tile[:, -wide:], tile[:, :wide]), ('til...  5.28 us
    ppermute x1, starting transfers between devices, on_device(): lax.ppermute(jnp.where(left_core, tile[:, -wide:], tile[:, :wide]), ('til...  3.02 us
    pallas_call x1, Pallas kernels, on_device(): pl.pallas_call(staging, out_shape=[jax.ShapeDtypeStruct(z, jnp.bfloat16)...  1.8 us
    ppermute x1, waiting for transfers between devices, on_device(): other = lax.ppermute(mine, 'cond', [(0, 1), (1, 0)])  1.19 us
    ppermute x1, starting transfers between devices, shifted(): lax.ppermute(block, axis, [((i - distance) % count, i) for i in range(cou...  1.04 us
    pallas_call x1, Pallas kernels, on_device(): pl.pallas_call(row_analysis, out_shape=jax.ShapeDtypeStruct((2 * band, ha...  1.02 us
    ppermute x1, waiting for transfers between devices, shifted(): lax.ppermute(block, axis, [((i - distance) % count, i) for i in range(cou...  1 us
  transfers between devices with their start and end apart: 4, of which 4 were waited for; matrix products, arithmetic and copies ran while one was open for 0% of the time, Pallas kernels for 13%

profile of v3, /device:TPU:0, one launch (start us, length us, event | category | flops | bytes accessed | tf_op | source)
XLA Modules:
  0.0 24.1 jit_solution(17616833673071904664)
XLA Ops:
  0.6 0.9 %broadcast_select_fusion = (bf16[256,128]{1,0:T(8,128)(2,1)S(1)}, bf16[256,128]{1,0:T(8,128)(2,1)S(1)}) fusion(pred[]{:T(512)S(6)} %eq.8, bf16[256,256]{1,0:T(8,128)(2,1)} %bitcast.1), kind=kLoop, calls=%fused_computation.2 | loop fusion | flops 65536 | bytes 262145 | tf_op jit(solution)/shard_map/jit(_where)/select_n | solution.py:276
  1.5 3.0 %collective-permute-start = (bf16[256,128]{1,0:T(8,128)(2,1)S(1)}, bf16[256,128]{1,0:T(8,128)(2,1)S(1)}, u32[]{:S(2)}, u32[]{:S(2)}) collective-permute-start(bf16[256,128]{1,0:T(8,128)(2,1)S(1)} %get-tuple-element.27), channel_id=1, source_target_pairs={{14,0},{0,2},{2,4},{4,6},{6,8},{8,10},{10,12},{12,14},{1,15},{3,1}... | collective-permute-start | bytes 196616 | tf_op jit(solution)/shard_map/ppermute | solution.py:273
  4.5 5.3 %collective-permute-done.strip_ref = bf16[256,128]{1,0:T(8,128)(2,1)S(1)} collective-permute-done((bf16[256,128]{1,0:T(8,128)(2,1)S(1)}, bf16[256,128]{1,0:T(8,128)(2,1)S(1)}, u32[]{:S(2)}, u32[]{:S(2)}) %collective-permute-start) | collective-permute-done | bytes 65568 | tf_op jit(solution)/shard_map/ppermute | solution.py:273
  9.8 1.0 %collective-permute-start.1 = (bf16[64,256]{1,0:T(8,128)(2,1)S(1)}, bf16[64,256]{1,0:T(8,128)(2,1)S(1)}, u32[]{:S(2)}, u32[]{:S(2)}) collective-permute-start(bf16[64,256]{1,0:T(8,128)(2,1)S(1)} %maximum_select_fusion), channel_id=1, source_target_pairs={{8,0},{10,2},{12,4},{14,6},{0,8},{2,10},{4,12},{6,14},{9,1},{11,3}... | collective-permute-start | bytes 98312 | tf_op jit(solution)/shard_map/ppermute | solution.py:256
  10.9 1.8 %staging.1 = (bf16[2,256,128]{2,1,0:T(8,128)(2,1)S(1)}, bf16[128,256]{1,0:T(8,128)(2,1)S(1)}, bf16[2,128,64]{2,1,0:T(8,128)(2,1)S(1)}, bf16[128,256]{1,0:T(8,128...) custom-call(bf16[2,2,256,128]{3,2,1,0:T(8,128)(2,1)} %constant.52.cl, ...), custom_call_target="tpu_custom_call" | custom-call | tf_op jit(solution)/shard_map/staging/pallas_call | solution.py:303
  12.7 1.0 %row_analysis.1.refs_0_ = f32[128,256]{1,0:T(8,128)S(1)} custom-call(bf16[256,256]{1,0:T(8,128)(2,1)} %bitcast.2, bf16[256,128]{1,0:T(8,128)(2,1)S(1)} %collective-permute-done.strip_ref, bf16[128,256]{1,0:T(8,128)(2,1)S(1)} %get-tuple-element.13.row_core_ref), custom_call_target="tpu_custom_call" | custom-call | tf_op jit(solution)/shard_map/row_analysis/pallas_call | solution.py:312
  13.7 1.0 %collective-permute-done.1.refs_3_ = bf16[64,256]{1,0:T(8,128)(2,1)S(1)} collective-permute-done((bf16[64,256]{1,0:T(8,128)(2,1)S(1)}, bf16[64,256]{1,0:T(8,128)(2,1)S(1)}, u32[]{:S(2)}, u32[]{:S(2)}) %collective-permute-start.1) | collective-permute-done | bytes 32800 | tf_op jit(solution)/shard_map/ppermute | solution.py:256
  14.7 0.3 %spectrum.1.refs_3_ = f32[64,128]{1,0:T(8,128)S(1)} custom-call(f32[128,256]{1,0:T(8,128)S(1)} %row_analysis.1.refs_0_, bf16[2,128,64]{2,1,0:T(8,128)(2,1)S(1)} %get-tuple-element.14.refs_1_, bf16[2,256,128]{2,1,0:T(8,128)(2,1)S(1)} %get-tuple-element.15.refs_2_, bf16[64,256]{1,0:T(8,128)(2,1)S(1)} %collective-permute-done.1.refs_3_), custom_call_target="tpu_custom_call" | custom-call | tf_op jit(solution)/shard_map/spectrum/pallas_call | solution.py:321
  15.0 0.1 collective-permute-start.2
  15.1 1.2 %collective-permute-done.2.refs_4_ = f32[64,128]{1,0:T(8,128)S(1)} collective-permute-done((f32[64,128]{1,0:T(8,128)S(1)}, f32[64,128]{1,0:T(8,128)S(1)}, u32[]{:S(2)}, u32[]{:S(2)}) %collective-permute-start.2) | collective-permute-done | bytes 32800 | tf_op jit(solution)/shard_map/ppermute | solution.py:329
  16.3 5.6 %imaging.1 = (bf16[2,128,256]{2,1,0:T(8,128)(2,1)S(1)}, bf16[2,512,256]{2,1,0:T(8,128)(2,1)S(1)}, f32[2,4,8,256]{3,2,1,0:T(8,128)S(1)}) custom-call(f32[4,24]{1,0:T(4,128)} %refs_0_.2, f32[4]{0:T(128)} %refs_1_.2, f32[4]{0:T(128)} %refs_2_.2, f32[64,128]{1,0:T(8,128)S(1)} %spectrum.1.refs_3_, f32[64,128]{1,0:T(8,128)S(1)} %collective-permute-done.2.refs_4_, ...), custom_call_target="tpu_custom_call" | custom-call | tf_op jit(solution)/shard_map/imaging/pallas_call | solution.py:330
  21.9 0.2 collective-permute-start.3
  22.2 0.4 %own_share.1 = f32[2,128,256]{2,1,0:T(8,128)S(1)} custom-call(bf16[2,512,256]{2,1,0:T(8,128)(2,1)S(1)} %get-tuple-element.21.level_ref, f32[2,4,8,256]{3,2,1,0:T(8,128)S(1)} %get-tuple-element.22.gain_ref, bf16[2,256,128]{2,1,0:T(8,128)(2,1)S(1)} %get-tuple-element.18.refs_7_.spread_ref), custom_call_target="tpu_custom_call" | custom-call | tf_op jit(solution)/shard_map/own_share/pallas_call | solution.py:362
  22.5 0.8 %collective-permute-done.3 = bf16[2,128,256]{2,1,0:T(8,128)(2,1)S(1)} collective-permute-done((bf16[2,128,256]{2,1,0:T(8,128)(2,1)S(1)}, bf16[2,128,256]{2,1,0:T(8,128)(2,1)S(1)}, u32[]{:S(2)}, u32[]{:S(2)}) %collective-permute-start.3) | collective-permute-done | bytes 131104 | tf_op jit(solution)/shard_map/ppermute | solution.py:361
  23.4 0.7 %slice_minimum_fusion = (f32[1,128,256]{2,1,0:T(8,128)}, f32[1,128,256]{2,1,0:T(8,128)}) fusion(f32[2,128,256]{2,1,0:T(8,128)S(1)} %convert_element_type.3, f32[2,128,256]{2,1,0:T(8,128)S(1)} %own_share.1), kind=kLoop, calls=%fused_computation | loop fusion | flops 65536 | bytes 786432 | tf_op jit(solution)/shard_map/min | solution.py:371
  (4 shorter events, 0.0 us)
Async XLA Ops:
  1.5 8.3 %collective-permute-start = (bf16[256,128]{1,0:T(8,128)(2,1)S(1)}, bf16[256,128]{1,0:T(8,128)(2,1)S(1)}, u32[]{:S(2)}, u32[]{:S(2)}) collective-permute-start(bf16[256,128]{1,0:T(8,128)(2,1)S(1)} %get-tuple-element.27), channel_id=1, source_target_pairs={{14,0},{0,2},{2,4},{4,6},{6,8},{8,10},{10,12},{12,14},{1,15},{3,1}... | collective-permute-start | bytes 196616 | tf_op jit(solution)/shard_map/ppermute | solution.py:273
  9.8 4.9 %collective-permute-start.1 = (bf16[64,256]{1,0:T(8,128)(2,1)S(1)}, bf16[64,256]{1,0:T(8,128)(2,1)S(1)}, u32[]{:S(2)}, u32[]{:S(2)}) collective-permute-start(bf16[64,256]{1,0:T(8,128)(2,1)S(1)} %maximum_select_fusion), channel_id=1, source_target_pairs={{8,0},{10,2},{12,4},{14,6},{0,8},{2,10},{4,12},{6,14},{9,1},{11,3}... | collective-permute-start | bytes 98312 | tf_op jit(solution)/shard_map/ppermute | solution.py:256
  15.0 1.3 %collective-permute-start.2 = (f32[64,128]{1,0:T(8,128)S(1)}, f32[64,128]{1,0:T(8,128)S(1)}, u32[]{:S(2)}, u32[]{:S(2)}) collective-permute-start(f32[64,128]{1,0:T(8,128)S(1)} %spectrum.1.refs_3_), channel_id=1, source_target_pairs={{0,1},{1,0},{2,3},{3,2},{4,5},{5,4},{6,7},{7,6},{8,9},{9,8},{10,11... | collective-permute-start | bytes 98312 | tf_op jit(solution)/shard_map/ppermute | solution.py:329
  21.9 1.4 %collective-permute-start.3 = (bf16[2,128,256]{2,1,0:T(8,128)(2,1)S(1)}, bf16[2,128,256]{2,1,0:T(8,128)(2,1)S(1)}, u32[]{:S(2)}, u32[]{:S(2)}) collective-permute-start(bf16[2,128,256]{2,1,0:T(8,128)(2,1)S(1)} %get-tuple-element.23), channel_id=1, source_target_pairs={{0,1},{1,0},{2,3},{3,2},{4,5},{5,4},{6,7},{7,6},{8,9},{9,8},{10,11... | collective-permute-start | bytes 393224 | tf_op jit(solution)/shard_map/ppermute | solution.py:361

commit v4 on v3

--- a/solution.py
+++ b/solution.py
@@ -98,33 +98,66 @@
     return [pltpu.make_async_copy(src, dst, sems.at[n]) for n, (src, dst) in enumerate(pairs)]
 
 
-def staging(*refs):
-    count = (len(refs) - 1) // 2
+def staging(*refs, count):
+    tile_hbm, weight_hbm, dose_hbm, threshold_hbm, columns_hbm = refs[:5]
+    sources = refs[5 : count + 4]
+    columns_ref, *targets = refs[count + 4 : 2 * count + 4]
+    tile_ref, part_ref, share_ref, gain_ref, weight_ref, dose_ref, threshold_ref, sems = refs[
+        2 * count + 4 :
+    ]
+    core, half = tile_ref.shape
     own = lax.axis_index("cond")
-    sources = [refs[0].at[own], *refs[1:count]]
-    copies = dma_all(zip(sources, refs[count : 2 * count]), refs[-1])
+    first = pl.multiple_of(own * half, half)
+    pairs = [
+        (weight_hbm, weight_ref),
+        (dose_hbm, dose_ref),
+        (threshold_hbm, threshold_ref),
+        (tile_hbm.at[:, pl.ds(first, half)], tile_ref),
+        *zip(sources, targets),
+        (columns_hbm.at[own], columns_ref),
+    ]
+    copies = dma_all(pairs, sems)
     for copy in copies:
         copy.start()
-    for copy in copies:
+    for copy in copies[:5]:
         copy.wait()
-
-
-def row_analysis(tile_hbm, strip_ref, row_core_ref, part_ref, tile_ref, sem):
-    half = tile_ref.shape[1]
-    first = pl.multiple_of(lax.axis_index("cond") * half, half)
-    copy = pltpu.make_async_copy(tile_hbm.at[:, pl.ds(first, half)], tile_ref, sem)
-    copy.start()
-    part_ref[:, half:] = dot(row_core_ref[...], strip_ref[...])
-    copy.wait()
-    part_ref[:, :half] = dot(row_core_ref[...], tile_ref[...])
-
-
-def spectrum(part_ref, row_side_ref, columns_ref, *rest, sides):
+    row_core_ref = targets[0]
+    part_ref[...] = dot(row_core_ref[...], tile_ref[...])
+    conds, kerns = weight_hbm.shape
+    scale = float(row_core_ref.shape[0] // 2) ** 2
+    for c in range(conds):
+        mass = weight_ref[c, 0]
+        for k in range(kerns):
+            mass = mass + weight_ref[c, k] if k else mass
+            share_ref[c * kerns + k, :] = jnp.full((share_ref.shape[1],), weight_ref[c, k])
+        gain_ref[0, c] = steepness * dose_ref[c] / jnp.full((8, core), mass * scale)
+        gain_ref[1, c] = jnp.full((8, core), steepness * threshold_ref[c])
+    for copy in copies[5:]:
+        copy.wait()
+
+
+def pack(tile_ref, strip_ref, *out_refs, sides):
+    core, half = tile_ref.shape
+    for side, out_ref in zip(sides, out_refs):
+        if side is None:
+            lower = placement()["top"].astype(jnp.int32)
+            first = pl.multiple_of(lower * (core - MARGIN), MARGIN)
+        else:
+            first = 0 if side else core - MARGIN
+        out_ref[:, :half] = tile_ref[pl.ds(first, MARGIN)]
+        out_ref[:, half:] = strip_ref[pl.ds(first, MARGIN)]
+
+
+def edge_analysis(row_core_ref, strip_ref, part_ref):
+    part_ref[...] = dot(row_core_ref[...], strip_ref[...])
+
+
+def spectrum(core_ref, edge_ref, row_side_ref, columns_ref, *rest, sides):
     *upright_refs, spec_ref = rest
     place = placement()
     band = spec_ref.shape[0]
-    half = part_ref.shape[1] - 2 * MARGIN
-    part = part_ref[...]
+    half = core_ref.shape[1]
+    part = jnp.concatenate([core_ref[...], edge_ref[...]], axis=1)
     for n, side in enumerate(sides):
         if side is None:
             table = row_side_ref[place["top"].astype(jnp.int32)]
@@ -141,9 +174,6 @@
 
 
 def imaging(
-    weight_hbm,
-    dose_hbm,
-    threshold_hbm,
     mine_ref,
     other_ref,
     half_ref,
@@ -151,23 +181,15 @@
     spread_ref,
     across_ref,
     kern_ref,
+    share_ref,
+    gain_ref,
     send_ref,
     level_ref,
-    gain_ref,
     halves_ref,
     coarse_ref,
-    weight_ref,
-    dose_ref,
-    threshold_ref,
-    sems,
     *,
     pad,
 ):
-    copies = dma_all(
-        [(weight_hbm, weight_ref), (dose_hbm, dose_ref), (threshold_hbm, threshold_ref)], sems
-    )
-    for copy in copies:
-        copy.start()
     conds, kerns, band, _ = kern_ref.shape
     grid = 2 * band
     core = spread_ref.shape[1]
@@ -176,8 +198,6 @@
     first = lax.broadcasted_iota(jnp.int32, spec.shape, 1) < band
     spec_same = jnp.where(first, spec, swapped)
     spec_cross = jnp.where(first, -swapped, spec)
-    for copy in copies:
-        copy.wait()
 
     def condition(c, carry):
         prods = []
@@ -199,9 +219,8 @@
             )
             field = dot(field_ref[...], both)
             power = field[:grid] * field[:grid] + field[grid:] * field[grid:]
-            total = (
-                total + weight_ref[c, k] * power[:, :grid] + weight_ref[c, k + 1] * power[:, grid:]
-            )
+            shares = share_ref[pl.ds(c * kerns + k, 1)], share_ref[pl.ds(c * kerns + k + 1, 1)]
+            total = total + shares[0] * power[:, :grid] + shares[1] * power[:, grid:]
         coarse_ref[c] = total
         return carry
 
@@ -209,12 +228,6 @@
     high, low = split(coarse_ref[...].reshape(conds * grid, grid))
     across = dot(high, across_ref[0]) + dot(low, across_ref[0]) + dot(high, across_ref[1])
     level_ref[0], level_ref[1] = split(across)
-    for c in range(conds):
-        mass = weight_ref[c, 0]
-        for k in range(1, kerns):
-            mass = mass + weight_ref[c, k]
-        gain_ref[0, c] = steepness * dose_ref[c] / jnp.full((8, core), mass * float(band * band))
-        gain_ref[1, c] = jnp.full((8, core), steepness * threshold_ref[c])
     most, least = band_of(1 - lax.axis_index("cond"), level_ref, gain_ref, spread_ref)
     send_ref[0] = most.astype(jnp.bfloat16)
     send_ref[1] = least.astype(jnp.bfloat16)
@@ -273,15 +286,7 @@
     strip = lax.ppermute(
         jnp.where(left_core, tile[:, -wide:], tile[:, :wide]), ("tile", "cond"), route
     )
-    columns_own = jnp.where(left_core, tile[:, :half], tile[:, half:])
-    upper = jnp.concatenate([columns_own[:MARGIN], strip[:MARGIN]], axis=1)
-    lower = jnp.concatenate([columns_own[-MARGIN:], strip[-MARGIN:]], axis=1)
-    if grid_rows == 2:
-        sides = (None,)
-        uprights = [shifted(jnp.where(place["top"], lower, upper), "tile", columns)]
-    else:
-        sides = (0, 1)
-        uprights = [shifted(lower, "tile", columns), shifted(upper, "tile", -columns)]
+    sides = (None,) if grid_rows == 2 else (0, 1)
     row_core, row_side, col_table, half_t, field_t, spread = make_tables(core, band)
     bf = lambda t: jnp.asarray(np.asarray(t).astype(jnp.bfloat16))
     fixed = [
@@ -298,66 +303,71 @@
     hbm = pl.BlockSpec(memory_space=pltpu.HBM)
     share = core // lax.axis_size("cond")
     params = pltpu.CompilerParams(vmem_limit_bytes=16 * 2**20)
-    shapes = [t.shape for t in fixed]
-    shapes[0] = shapes[0][1:]
-    col_v, row_v, side_v, half_v, field_v, spread_v, across_v, kernels_v = pl.pallas_call(
-        staging,
-        out_shape=[jax.ShapeDtypeStruct(z, jnp.bfloat16) for z in shapes],
-        in_specs=[hbm] * len(fixed),
-        out_specs=[vmem] * len(fixed),
-        scratch_shapes=[pltpu.SemaphoreType.DMA((len(fixed),))],
-        compiler_params=params,
-        name="staging",
-    )(*map(in_hbm, fixed))
-    part = pl.pallas_call(
-        row_analysis,
-        out_shape=jax.ShapeDtypeStruct((2 * band, half + wide), jnp.float32),
-        in_specs=[hbm, vmem, vmem],
+    outs = [jax.ShapeDtypeStruct(t.shape, t.dtype) for t in fixed]
+    outs[0] = jax.ShapeDtypeStruct(fixed[0].shape[1:], fixed[0].dtype)
+    outs += [
+        jax.ShapeDtypeStruct((core, half), tile.dtype),
+        jax.ShapeDtypeStruct((2 * band, half), jnp.float32),
+        jax.ShapeDtypeStruct((conds * kerns, grid), jnp.float32),
+        jax.ShapeDtypeStruct((2, conds, 8, core), jnp.float32),
+    ]
+    scalars = (socs_weight, dose, threshold)
+    (col_v, row_v, side_v, half_v, field_v, spread_v, across_v, kernels_v, tile_v, part, *gains) = (
+        pl.pallas_call(
+            lambda *refs: staging(*refs, count=len(fixed)),
+            out_shape=outs,
+            in_specs=[hbm] * (4 + len(fixed)),
+            out_specs=[vmem] * len(outs),
+            scratch_shapes=[pltpu.SMEM(t.shape, t.dtype) for t in scalars]
+            + [pltpu.SemaphoreType.DMA((4 + len(fixed),))],
+            compiler_params=params,
+            name="staging",
+        )(*map(in_hbm, (tile, *scalars, *fixed)))
+    )
+    block = jax.ShapeDtypeStruct((MARGIN, half + wide), tile.dtype)
+    blocks = pl.pallas_call(
+        lambda *refs: pack(*refs, sides=sides),
+        out_shape=[block] * len(sides),
+        in_specs=[vmem, vmem],
+        out_specs=[vmem] * len(sides),
+        compiler_params=params,
+        name="pack",
+    )(tile_v, strip)
+    uprights = [
+        shifted(t, "tile", -columns if side else columns) for t, side in zip(blocks, sides)
+    ]
+    edge = pl.pallas_call(
+        edge_analysis,
+        out_shape=jax.ShapeDtypeStruct((2 * band, wide), jnp.float32),
+        in_specs=[vmem, vmem],
         out_specs=vmem,
-        scratch_shapes=[pltpu.VMEM((core, half), jnp.bfloat16), pltpu.SemaphoreType.DMA],
-        compiler_params=params,
-        name="row_analysis",
-    )(in_hbm(tile), strip, row_v)
+        compiler_params=params,
+        name="edge_analysis",
+    )(row_v, strip)
     mine = pl.pallas_call(
         lambda *refs: spectrum(*refs, sides=sides),
         out_shape=jax.ShapeDtypeStruct((band, grid), jnp.float32),
-        in_specs=[vmem] * (3 + len(uprights)),
+        in_specs=[vmem] * (4 + len(uprights)),
         out_specs=vmem,
         compiler_params=params,
         name="spectrum",
-    )(part, side_v, col_v, *uprights)
+    )(part, edge, side_v, col_v, *uprights)
     other = lax.ppermute(mine, "cond", [(0, 1), (1, 0)])
-    send, level, gain = pl.pallas_call(
+    send, level = pl.pallas_call(
         lambda *refs: imaging(*refs, pad=pad),
         out_shape=(
             jax.ShapeDtypeStruct((2, share, core), jnp.bfloat16),
             jax.ShapeDtypeStruct((2, conds * grid, core), jnp.bfloat16),
-            jax.ShapeDtypeStruct((2, conds, 8, core), jnp.float32),
         ),
-        in_specs=[hbm] * 3 + [vmem] * 7,
-        out_specs=(vmem, vmem, vmem),
+        in_specs=[vmem] * 9,
+        out_specs=(vmem, vmem),
         scratch_shapes=[
             pltpu.VMEM((kerns * band, 2 * grid), jnp.bfloat16),
             pltpu.VMEM((conds, grid, grid), jnp.float32),
-            pltpu.SMEM(socs_weight.shape, jnp.float32),
-            pltpu.SMEM(dose.shape, jnp.float32),
-            pltpu.SMEM(threshold.shape, jnp.float32),
-            pltpu.SemaphoreType.DMA((3,)),
         ],
         compiler_params=params,
         name="imaging",
-    )(
-        in_hbm(socs_weight),
-        in_hbm(dose),
-        in_hbm(threshold),
-        mine,
-        other,
-        half_v,
-        field_v,
-        spread_v,
-        across_v,
-        kernels_v,
-    )
+    )(mine, other, half_v, field_v, spread_v, across_v, kernels_v, *gains)
     other = lax.ppermute(send, "cond", [(0, 1), (1, 0)])
     keep = pl.pallas_call(
         own_share,
@@ -366,7 +376,7 @@
         out_specs=vmem,
         compiler_params=params,
         name="own_share",
-    )(level, gain, spread_v)
+    )(level, gains[1], spread_v)
     other = other.astype(jnp.float32)
     return (jnp.maximum(keep[0], other[0])[None], jnp.minimum(keep[1], other[1])[None])
 

time: 24.4 us -> 23.6 us (0.967)
  Pallas kernels: 9.12 us -> 7.61 us
  waiting for transfers between devices: 8.26 us -> 9.12 us
    ppermute x1, waiting for transfers between devices: 1 us -> 3.69 us  [shifted(): lax.ppermute(block, axis, [((i - distance) % count, i) for i in range(cou...]
    ppermute x1, waiting for transfers between devices: 5.28 us -> 3.45 us  [on_device(): lax.ppermute(jnp.where(left_core, tile[:, -wide:], tile[:, :wide]), ('til...]
    pallas_call x2 -> x3, Pallas kernels: 2.82 us -> 1.97 us  [the longest x1 1.83 us: on_device(): pl.pallas_call(lambda *refs: staging(*refs, count=len(fixed)), out_shape=...]
    pallas_call x1, Pallas kernels: 5.62 us -> 4.96 us  [on_device(): pl.pallas_call(lambda *refs: imaging(*refs, pad=pad), out_shape=(jax.Shap...]
    select_n x2 -> x1, other arithmetic: 0.9 us -> 0.88 us  [on_device(): jnp.where(left_core, tile[:, -wide:], tile[:, :wide])]
  transfers between devices with their start and end apart: 4 -> 4, of which waited for: 4 -> 4; matrix products, arithmetic and copies ran while one was open for 0% -> 0% of each run, Pallas kernels for 13% -> 10%
where the time goes in v4:
time: 23.6 us; the launch traced here: 23.4 us
  waiting for transfers between devices  9.12 us (39%)
  Pallas kernels  7.61 us (32%)
  starting transfers between devices  4.3 us (18%)
  other arithmetic  1.64 us (7%)
  between operations  0.69 us (3%)
    pallas_call x1, Pallas kernels, on_device(): pl.pallas_call(lambda *refs: imaging(*refs, pad=pad), out_shape=(jax.Shap...  4.96 us
    ppermute x1, waiting for transfers between devices, shifted(): lax.ppermute(block, axis, [((i - distance) % count, i) for i in range(cou...  3.69 us
    ppermute x1, waiting for transfers between devices, on_device(): lax.ppermute(jnp.where(left_core, tile[:, -wide:], tile[:, :wide]), ('til...  3.45 us
    ppermute x1, starting transfers between devices, on_device(): lax.ppermute(jnp.where(left_core, tile[:, -wide:], tile[:, :wide]), ('til...  3.02 us
    pallas_call x1, Pallas kernels, on_device(): pl.pallas_call(lambda *refs: staging(*refs, count=len(fixed)), out_shape=...  1.83 us
    ppermute x1, waiting for transfers between devices, on_device(): other = lax.ppermute(mine, 'cond', [(0, 1), (1, 0)])  1.19 us
    ppermute x1, starting transfers between devices, shifted(): lax.ppermute(block, axis, [((i - distance) % count, i) for i in range(cou...  0.98 us
    select_n x1, other arithmetic, on_device(): jnp.where(left_core, tile[:, -wide:], tile[:, :wide])  0.88 us
  transfers between devices with their start and end apart: 4, of which 4 were waited for; matrix products, arithmetic and copies ran while one was open for 0% of the time, Pallas kernels for 10%

profile of v4, /device:TPU:0, one launch (start us, length us, event | category | flops | bytes accessed | tf_op | source)
XLA Modules:
  0.0 23.4 jit_solution(251554411952880405)
XLA Ops:
  0.6 0.9 %slice_select_fusion = bf16[256,128]{1,0:T(8,128)(2,1)S(1)} fusion(bf16[256,256]{1,0:T(8,128)(2,1)} %bitcast.1, pred[]{:T(512)S(6)} %eq.3), kind=kLoop, calls=%fused_computation.2 | loop fusion | flops 32768 | bytes 196609 | tf_op jit(solution)/shard_map/jit(_where)/select_n | solution.py:287
  1.5 3.0 %collective-permute-start = (bf16[256,128]{1,0:T(8,128)(2,1)S(1)}, bf16[256,128]{1,0:T(8,128)(2,1)S(1)}, u32[]{:S(2)}, u32[]{:S(2)}) collective-permute-start(bf16[256,128]{1,0:T(8,128)(2,1)S(1)} %slice_select_fusion), channel_id=1, source_target_pairs={{14,0},{0,2},{2,4},{4,6},{6,8},{8,10},{10,12},{12,14},{1,15},{3,1}... | collective-permute-start | bytes 196616 | tf_op jit(solution)/shard_map/ppermute | solution.py:286
  4.5 1.8 %staging.1 = (bf16[2,256,128]{2,1,0:T(8,128)(2,1)S(1)}, bf16[128,256]{1,0:T(8,128)(2,1)S(1)}, bf16[2,128,64]{2,1,0:T(8,128)(2,1)S(1)}, bf16[128,256]{1,0:T(8,128...) custom-call(bf16[256,256]{1,0:T(8,128)(2,1)} %bitcast.2, ...), custom_call_target="tpu_custom_call" | custom-call | tf_op jit(solution)/shard_map/staging/pallas_call | solution.py:316
  6.4 3.4 %collective-permute-done.strip_ref.refs_1_ = bf16[256,128]{1,0:T(8,128)(2,1)S(1)} collective-permute-done((bf16[256,128]{1,0:T(8,128)(2,1)S(1)}, bf16[256,128]{1,0:T(8,128)(2,1)S(1)}, u32[]{:S(2)}, u32[]{:S(2)}) %collective-permute-start) | collective-permute-done | bytes 65568 | tf_op jit(solution)/shard_map/ppermute | solution.py:286
  9.8 1.0 %collective-permute-start.1 = (bf16[64,256]{1,0:T(8,128)(2,1)S(1)}, bf16[64,256]{1,0:T(8,128)(2,1)S(1)}, u32[]{:S(2)}, u32[]{:S(2)}) collective-permute-start(bf16[64,256]{1,0:T(8,128)(2,1)S(1)} %pack.1), channel_id=1, source_target_pairs={{8,0},{10,2},{12,4},{14,6},{0,8},{2,10},{4,12},{6,14},{9,1},{11,3}... | collective-permute-start | bytes 98312 | tf_op jit(solution)/shard_map/ppermute | solution.py:269
  10.8 0.1 edge_analysis.1.refs_1_
  11.0 3.7 %collective-permute-done.1.refs_4_ = bf16[64,256]{1,0:T(8,128)(2,1)S(1)} collective-permute-done((bf16[64,256]{1,0:T(8,128)(2,1)S(1)}, bf16[64,256]{1,0:T(8,128)(2,1)S(1)}, u32[]{:S(2)}, u32[]{:S(2)}) %collective-permute-start.1) | collective-permute-done | bytes 32800 | tf_op jit(solution)/shard_map/ppermute | solution.py:269
  14.6 0.3 %spectrum.1.refs_0_ = f32[64,128]{1,0:T(8,128)S(1)} custom-call(f32[128,128]{1,0:T(8,128)S(1)} %get-tuple-element.16.refs_0_, f32[128,128]{1,0:T(8,128)S(1)} %edge_analysis.1.refs_1_, bf16[2,128,64]{2,1,0:T(8,128)(2,1)S(1)} %get-tuple-element.18.refs_2_, bf16[2,256,128]{2,1,0:T(8,128)(2,1)S(1)} %get-tuple-element.19.refs_3_, ...), custom_call_target="tpu_custom_call" | custom-call | tf_op jit(solution)/shard_map/spectrum/pallas_call | solution.py:347
  14.9 0.1 collective-permute-start.2
  15.0 1.2 %collective-permute-done.2.refs_1_ = f32[64,128]{1,0:T(8,128)S(1)} collective-permute-done((f32[64,128]{1,0:T(8,128)S(1)}, f32[64,128]{1,0:T(8,128)S(1)}, u32[]{:S(2)}, u32[]{:S(2)}) %collective-permute-start.2) | collective-permute-done | bytes 32800 | tf_op jit(solution)/shard_map/ppermute | solution.py:355
  16.2 5.0 %imaging.1 = (bf16[2,128,256]{2,1,0:T(8,128)(2,1)S(1)}, bf16[2,512,256]{2,1,0:T(8,128)(2,1)S(1)}) custom-call(f32[64,128]{1,0:T(8,128)S(1)} %spectrum.1.refs_0_, f32[64,128]{1,0:T(8,128)S(1)} %collective-permute-done.2.refs_1_, bf16[128,256]{1,0:T(8,128)(2,1)S(1)} %get-tuple-element.21.refs_2_, bf16[256,128]{1,0:T(8,128)(2,1)S(1)} %get-tuple-element.22.refs_3_, ...), custom_call_target="tpu_custom_call" | custom-call | tf_op jit(solution)/shard_map/imaging/pallas_call | solution.py:356
  21.2 0.2 collective-permute-start.3
  21.4 0.4 %own_share.1 = f32[2,128,256]{2,1,0:T(8,128)S(1)} custom-call(bf16[2,512,256]{2,1,0:T(8,128)(2,1)S(1)} %get-tuple-element.28.level_ref, f32[2,4,8,256]{3,2,1,0:T(8,128)S(1)} %get-tuple-element.27.refs_8_.gain_ref, bf16[2,256,128]{2,1,0:T(8,128)(2,1)S(1)} %get-tuple-element.23.refs_4_.spread_ref), custom_call_target="tpu_custom_call" | custom-call | tf_op jit(solution)/shard_map/own_share/pallas_call | solution.py:372
  21.8 0.8 %collective-permute-done.3 = bf16[2,128,256]{2,1,0:T(8,128)(2,1)S(1)} collective-permute-done((bf16[2,128,256]{2,1,0:T(8,128)(2,1)S(1)}, bf16[2,128,256]{2,1,0:T(8,128)(2,1)S(1)}, u32[]{:S(2)}, u32[]{:S(2)}) %collective-permute-start.3) | collective-permute-done | bytes 131104 | tf_op jit(solution)/shard_map/ppermute | solution.py:371
  22.6 0.7 %slice_minimum_fusion = (f32[1,128,256]{2,1,0:T(8,128)}, f32[1,128,256]{2,1,0:T(8,128)}) fusion(f32[2,128,256]{2,1,0:T(8,128)S(1)} %convert_element_type.3, f32[2,128,256]{2,1,0:T(8,128)S(1)} %own_share.1), kind=kLoop, calls=%fused_computation | loop fusion | flops 65536 | bytes 786432 | tf_op jit(solution)/shard_map/min | solution.py:381
  (2 shorter events, 0.0 us)
Async XLA Ops:
  1.5 8.3 %collective-permute-start = (bf16[256,128]{1,0:T(8,128)(2,1)S(1)}, bf16[256,128]{1,0:T(8,128)(2,1)S(1)}, u32[]{:S(2)}, u32[]{:S(2)}) collective-permute-start(bf16[256,128]{1,0:T(8,128)(2,1)S(1)} %slice_select_fusion), channel_id=1, source_target_pairs={{14,0},{0,2},{2,4},{4,6},{6,8},{8,10},{10,12},{12,14},{1,15},{3,1}... | collective-permute-start | bytes 196616 | tf_op jit(solution)/shard_map/ppermute | solution.py:286
  9.8 4.8 %collective-permute-start.1 = (bf16[64,256]{1,0:T(8,128)(2,1)S(1)}, bf16[64,256]{1,0:T(8,128)(2,1)S(1)}, u32[]{:S(2)}, u32[]{:S(2)}) collective-permute-start(bf16[64,256]{1,0:T(8,128)(2,1)S(1)} %pack.1), channel_id=1, source_target_pairs={{8,0},{10,2},{12,4},{14,6},{0,8},{2,10},{4,12},{6,14},{9,1},{11,3}... | collective-permute-start | bytes 98312 | tf_op jit(solution)/shard_map/ppermute | solution.py:269
  14.9 1.3 %collective-permute-start.2 = (f32[64,128]{1,0:T(8,128)S(1)}, f32[64,128]{1,0:T(8,128)S(1)}, u32[]{:S(2)}, u32[]{:S(2)}) collective-permute-start(f32[64,128]{1,0:T(8,128)S(1)} %spectrum.1.refs_0_), channel_id=1, source_target_pairs={{0,1},{1,0},{2,3},{3,2},{4,5},{5,4},{6,7},{7,6},{8,9},{9,8},{10,11... | collective-permute-start | bytes 98312 | tf_op jit(solution)/shard_map/ppermute | solution.py:355
  21.2 1.4 %collective-permute-start.3 = (bf16[2,128,256]{2,1,0:T(8,128)(2,1)S(1)}, bf16[2,128,256]{2,1,0:T(8,128)(2,1)S(1)}, u32[]{:S(2)}, u32[]{:S(2)}) collective-permute-start(bf16[2,128,256]{2,1,0:T(8,128)(2,1)S(1)} %get-tuple-element.29), channel_id=1, source_target_pairs={{0,1},{1,0},{2,3},{3,2},{4,5},{5,4},{6,7},{7,6},{8,9},{9,8},{10,11... | collective-permute-start | bytes 393224 | tf_op jit(solution)/shard_map/ppermute | solution.py:371

commit v5 on v4

--- a/solution.py
+++ b/solution.py
@@ -26,7 +26,7 @@
     cos_in, sin_in = phases(np.arange(pad), freqs, pad)
     row_all = np.concatenate([cos_in, -sin_in], axis=1).T
     row_core = row_all[:, MARGIN : MARGIN + core]
-    row_side = np.stack([row_all[:, :MARGIN], row_all[:, MARGIN + core :]])
+    row_side = np.stack([row_all[:, :MARGIN].T, row_all[:, MARGIN + core :].T])
     table = np.stack(
         [np.concatenate([cos_in, -sin_in], axis=1), np.concatenate([sin_in, cos_in], axis=1)]
     )
@@ -92,6 +92,22 @@
         top=row == 0,
         half=lax.axis_index("cond"),
     )
+
+
+def dot_first(a, b):
+    return lax.dot_general(a, b, (((0,), (0,)), ((), ())), preferred_element_type=jnp.float32)
+
+
+def native_lanes(shape):
+    upper = (lax.broadcasted_iota(jnp.int32, shape, 1) >= MARGIN).astype(jnp.int32)
+    return upper != lax.axis_index("cond")
+
+
+def folded(block):
+    rows = block.shape[0] // 2
+    block = block.astype(jnp.float32)
+    back = pltpu.roll(block[rows:], MARGIN, 1)
+    return jnp.where(native_lanes(back.shape), block[:rows], back).astype(jnp.bfloat16)
 
 
 def dma_all(pairs, sems):
@@ -136,40 +152,60 @@
         copy.wait()
 
 
-def pack(tile_ref, strip_ref, *out_refs, sides):
-    core, half = tile_ref.shape
-    for side, out_ref in zip(sides, out_refs):
+def cut(tile_hbm, strip_ref, *refs, sides):
+    upright_refs, corner_refs = refs[: len(sides)], refs[len(sides) : 2 * len(sides)]
+    block_ref, sems = refs[2 * len(sides) :]
+    core, wide = block_ref.shape
+    half = upright_refs[0].shape[1]
+    own = lax.axis_index("cond")
+    beside = pl.multiple_of((1 - own) * (core - wide), wide)
+    first = pl.multiple_of(own * half, half)
+    rows = []
+    for side in sides:
         if side is None:
             lower = placement()["top"].astype(jnp.int32)
-            first = pl.multiple_of(lower * (core - MARGIN), MARGIN)
+            rows.append(pl.ds(pl.multiple_of(lower * (core - MARGIN), MARGIN), MARGIN))
         else:
-            first = 0 if side else core - MARGIN
-        out_ref[:, :half] = tile_ref[pl.ds(first, MARGIN)]
-        out_ref[:, half:] = strip_ref[pl.ds(first, MARGIN)]
-
-
-def edge_analysis(row_core_ref, strip_ref, part_ref):
-    part_ref[...] = dot(row_core_ref[...], strip_ref[...])
-
-
-def spectrum(core_ref, edge_ref, row_side_ref, columns_ref, *rest, sides):
-    *upright_refs, spec_ref = rest
+            rows.append(pl.ds(0 if side else core - MARGIN, MARGIN))
+    pairs = [(tile_hbm.at[:, pl.ds(beside, wide)], block_ref)]
+    for r, upright_ref in zip(rows, upright_refs):
+        pairs.append((tile_hbm.at[r, pl.ds(first, half)], upright_ref))
+    copies = dma_all(pairs, sems)
+    for copy in copies:
+        copy.start()
+    copies[0].wait()
+    strip_ref[...] = folded(block_ref[...])
+    for r, corner_ref in zip(rows, corner_refs):
+        corner_ref[...] = folded(block_ref[r])
+    for copy in copies[1:]:
+        copy.wait()
+
+
+def spectrum(core_ref, row_core_ref, row_side_ref, columns_ref, strip_ref, *rest, sides):
+    upright_refs, corner_refs = rest[: len(sides)], rest[len(sides) : 2 * len(sides)]
+    spec_ref = rest[-1]
     place = placement()
     band = spec_ref.shape[0]
-    half = core_ref.shape[1]
-    part = jnp.concatenate([core_ref[...], edge_ref[...]], axis=1)
+    fold = strip_ref.shape[0]
+    fold_side = corner_refs[0].shape[0]
+    core = core_ref[...]
+    ahead = dot(row_core_ref[:, :fold], strip_ref[...])
+    behind = dot(row_core_ref[:, fold:], strip_ref[...])
     for n, side in enumerate(sides):
-        if side is None:
-            table = row_side_ref[place["top"].astype(jnp.int32)]
-            part = part + dot(table, upright_refs[n][...])
-        else:
+        table = row_side_ref.at[place["top"].astype(jnp.int32) if side is None else side]
+        more = (
+            dot_first(table[...], upright_refs[n][...]),
+            dot_first(table[:fold_side], corner_refs[n][...]),
+            dot_first(table[fold_side:], corner_refs[n][...]),
+        )
+        if side is not None:
             there = place["below"] if side else place["above"]
-            more = dot(row_side_ref[side], upright_refs[n][...])
-            part = part + jnp.where(there, more, jnp.zeros_like(more))
-    edge = part[:, half:]
+            more = [jnp.where(there, m, jnp.zeros_like(m)) for m in more]
+        core, ahead, behind = core + more[0], ahead + more[1], behind + more[2]
+    edge = ahead + pltpu.roll(behind, MARGIN, 1)
     beside = jnp.where(place["half"] == 0, place["left"], place["right"])
     edge = jnp.where(beside, edge, jnp.zeros_like(edge))
-    part = jnp.concatenate([part[:, :half], edge], axis=1).astype(jnp.bfloat16)
+    part = jnp.concatenate([core, edge], axis=1).astype(jnp.bfloat16)
     spec_ref[...] = dot(part[:band], columns_ref[0]) + dot(part[band:], columns_ref[1])
 
 
@@ -280,13 +316,36 @@
     columns, grid_rows = place["columns"], place["grid_rows"]
 
     half, wide = core // 2, 2 * MARGIN
-    left_core = lax.axis_index("cond") == 0
-    others = [((t - 1) % count, t) for t in range(count)]
-    route = [(2 * a, 2 * b) for a, b in others] + [(2 * b + 1, 2 * a + 1) for a, b in others]
-    strip = lax.ppermute(
-        jnp.where(left_core, tile[:, -wide:], tile[:, :wide]), ("tile", "cond"), route
-    )
     sides = (None,) if grid_rows == 2 else (0, 1)
+    vmem = pl.BlockSpec(memory_space=pltpu.VMEM)
+    hbm = pl.BlockSpec(memory_space=pltpu.HBM)
+    params = pltpu.CompilerParams(vmem_limit_bytes=16 * 2**20)
+    strip, *blocks = pl.pallas_call(
+        lambda *refs: cut(*refs, sides=sides),
+        out_shape=[jax.ShapeDtypeStruct((core // 2, wide), tile.dtype)]
+        + [jax.ShapeDtypeStruct((MARGIN, half), tile.dtype)] * len(sides)
+        + [jax.ShapeDtypeStruct((MARGIN // 2, wide), tile.dtype)] * len(sides),
+        in_specs=[hbm],
+        out_specs=[vmem] * (1 + 2 * len(sides)),
+        scratch_shapes=[
+            pltpu.VMEM((core, wide), tile.dtype),
+            pltpu.SemaphoreType.DMA((1 + len(sides),)),
+        ],
+        compiler_params=params,
+        name="cut",
+    )(in_hbm(tile))
+
+    def passed(block, shift):
+        pairs = []
+        for t in range(count):
+            pairs.append((2 * ((t - shift - 1) % count), 2 * t))
+            pairs.append((2 * ((t - shift + 1) % count) + 1, 2 * t + 1))
+        return lax.ppermute(block, ("tile", "cond"), pairs)
+
+    shifts = [-columns if side else columns for side in sides]
+    strip = passed(strip, 0)
+    corners = [passed(t, d) for t, d in zip(blocks[len(sides) :], shifts)]
+    uprights = [shifted(t, "tile", d) for t, d in zip(blocks, shifts)]
     row_core, row_side, col_table, half_t, field_t, spread = make_tables(core, band)
     bf = lambda t: jnp.asarray(np.asarray(t).astype(jnp.bfloat16))
     fixed = [
@@ -299,10 +358,7 @@
         jnp.asarray(two_parts(spread.T)),
         kernels,
     ]
-    vmem = pl.BlockSpec(memory_space=pltpu.VMEM)
-    hbm = pl.BlockSpec(memory_space=pltpu.HBM)
     share = core // lax.axis_size("cond")
-    params = pltpu.CompilerParams(vmem_limit_bytes=16 * 2**20)
     outs = [jax.ShapeDtypeStruct(t.shape, t.dtype) for t in fixed]
     outs[0] = jax.ShapeDtypeStruct(fixed[0].shape[1:], fixed[0].dtype)
     outs += [
@@ -324,34 +380,14 @@
             name="staging",
         )(*map(in_hbm, (tile, *scalars, *fixed)))
     )
-    block = jax.ShapeDtypeStruct((MARGIN, half + wide), tile.dtype)
-    blocks = pl.pallas_call(
-        lambda *refs: pack(*refs, sides=sides),
-        out_shape=[block] * len(sides),
-        in_specs=[vmem, vmem],
-        out_specs=[vmem] * len(sides),
-        compiler_params=params,
-        name="pack",
-    )(tile_v, strip)
-    uprights = [
-        shifted(t, "tile", -columns if side else columns) for t, side in zip(blocks, sides)
-    ]
-    edge = pl.pallas_call(
-        edge_analysis,
-        out_shape=jax.ShapeDtypeStruct((2 * band, wide), jnp.float32),
-        in_specs=[vmem, vmem],
-        out_specs=vmem,
-        compiler_params=params,
-        name="edge_analysis",
-    )(row_v, strip)
     mine = pl.pallas_call(
         lambda *refs: spectrum(*refs, sides=sides),
         out_shape=jax.ShapeDtypeStruct((band, grid), jnp.float32),
-        in_specs=[vmem] * (4 + len(uprights)),
+        in_specs=[vmem] * (5 + 2 * len(sides)),
         out_specs=vmem,
         compiler_params=params,
         name="spectrum",
-    )(part, edge, side_v, col_v, *uprights)
+    )(part, row_v, side_v, col_v, strip, *uprights, *corners)
     other = lax.ppermute(mine, "cond", [(0, 1), (1, 0)])
     send, level = pl.pallas_call(
         lambda *refs: imaging(*refs, pad=pad),

time: 23.6 us -> 20.9 us (0.89)
  waiting for transfers between devices: 9.12 us -> 2.79 us
  starting transfers between devices: 4.3 us -> 7.23 us
  Pallas kernels: 7.61 us -> 9.21 us
  other arithmetic: 1.64 us -> 0.75 us
    ppermute x1, waiting for transfers between devices: 3.69 us -> 0.01 us  [shifted(): lax.ppermute(block, axis, [((i - distance) % count, i) for i in range(cou...]
    ppermute x1 -> x2, waiting for transfers between devices: 3.45 us -> 0.8 us  [passed(): return lax.ppermute(block, ('tile', 'cond'), pairs)]
    ppermute x1, starting transfers between devices: 0.98 us -> 2.59 us  [shifted(): lax.ppermute(block, axis, [((i - distance) % count, i) for i in range(cou...]
    ppermute x1 -> x2, starting transfers between devices: 3.02 us -> 4.34 us  [passed(): return lax.ppermute(block, ('tile', 'cond'), pairs)]
    select_n x1 -> x0, other arithmetic: 0.88 us -> none  [on_device(): jnp.where(left_core, tile[:, -wide:], tile[:, :wide])]
    pallas_call x2 -> x1, Pallas kernels: 0.15 us -> 0.95 us  [on_device(): pl.pallas_call(lambda *refs: cut(*refs, sides=sides), out_shape=[jax.Shap...]
    pallas_call x1, Pallas kernels: 1.83 us -> 2.44 us  [on_device(): pl.pallas_call(lambda *refs: staging(*refs, count=len(fixed)), out_shape=...]
  transfers between devices with their start and end apart: 4 -> 5, of which waited for: 4 -> 3; matrix products, arithmetic and copies ran while one was open for 0% -> 0% of each run, Pallas kernels for 10% -> 14%
where the time goes in v5:
time: 20.9 us; the launch traced here: 20.7 us
  Pallas kernels  9.21 us (44%)
  starting transfers between devices  7.23 us (35%)
  waiting for transfers between devices  2.79 us (13%)
  other arithmetic  0.75 us (4%)
  between operations  0.68 us (3%)
    pallas_call x1, Pallas kernels, on_device(): pl.pallas_call(lambda *refs: imaging(*refs, pad=pad), out_shape=(jax.Shap...  4.96 us
    ppermute x2, starting transfers between devices, passed(): return lax.ppermute(block, ('tile', 'cond'), pairs)  4.34 us
    ppermute x1, starting transfers between devices, shifted(): lax.ppermute(block, axis, [((i - distance) % count, i) for i in range(cou...  2.59 us
    pallas_call x1, Pallas kernels, on_device(): pl.pallas_call(lambda *refs: staging(*refs, count=len(fixed)), out_shape=...  2.44 us
    ppermute x1, waiting for transfers between devices, on_device(): other = lax.ppermute(mine, 'cond', [(0, 1), (1, 0)])  1.19 us
    pallas_call x1, Pallas kernels, on_device(): pl.pallas_call(lambda *refs: cut(*refs, sides=sides), out_shape=[jax.Shap...  0.95 us
    ppermute x2, waiting for transfers between devices, passed(): return lax.ppermute(block, ('tile', 'cond'), pairs)  0.8 us
    ppermute x1, waiting for transfers between devices, on_device(): other = lax.ppermute(send, 'cond', [(0, 1), (1, 0)])  0.79 us
  transfers between devices with their start and end apart: 5, of which 3 were waited for; matrix products, arithmetic and copies ran while one was open for 0% of the time, Pallas kernels for 14%

profile of v5, /device:TPU:0, one launch (start us, length us, event | category | flops | bytes accessed | tf_op | source)
XLA Modules:
  0.0 20.7 jit_solution(13484011767843371134)
XLA Ops:
  0.6 0.9 %cut.1 = (bf16[128,128]{1,0:T(8,128)(2,1)S(1)}, bf16[64,128]{1,0:T(8,128)(2,1)S(1)}, bf16[32,128]{1,0:T(8,128)(2,1)S(1)}) custom-call(bf16[256,256]{1,0:T(8,128)(2,1)} %bitcast.1), custom_call_target="tpu_custom_call" | custom-call | tf_op jit(solution)/shard_map/cut/pallas_call | solution.py:323
  1.6 3.0 %collective-permute-start = (bf16[128,128]{1,0:T(8,128)(2,1)S(1)}, bf16[128,128]{1,0:T(8,128)(2,1)S(1)}, u32[]{:S(2)}, u32[]{:S(2)}) collective-permute-start(bf16[128,128]{1,0:T(8,128)(2,1)S(1)} %get-tuple-element.22), channel_id=1, source_target_pairs={{14,0},{3,1},{0,2},{5,3},{2,4},{7,5},{4,6},{9,7},{6,8},{11,9},{8,1... | collective-permute-start | bytes 98312 | tf_op jit(solution)/shard_map/ppermute | solution.py:343
  4.6 2.6 %collective-permute-start.1 = (bf16[64,128]{1,0:T(8,128)(2,1)S(1)}, bf16[64,128]{1,0:T(8,128)(2,1)S(1)}, u32[]{:S(2)}, u32[]{:S(2)}) collective-permute-start(bf16[64,128]{1,0:T(8,128)(2,1)S(1)} %get-tuple-element.23), channel_id=1, source_target_pairs={{8,0},{10,2},{12,4},{14,6},{0,8},{2,10},{4,12},{6,14},{9,1},{11,3}... | collective-permute-start | bytes 49160 | tf_op jit(solution)/shard_map/ppermute | solution.py:305
  7.2 1.3 %collective-permute-start.2 = (bf16[32,128]{1,0:T(8,128)(2,1)S(1)}, bf16[32,128]{1,0:T(8,128)(2,1)S(1)}, u32[]{:S(2)}, u32[]{:S(2)}) collective-permute-start(bf16[32,128]{1,0:T(8,128)(2,1)S(1)} %get-tuple-element.24), channel_id=1, source_target_pairs={{6,0},{11,1},{8,2},{13,3},{10,4},{15,5},{12,6},{1,7},{14,8},{3,9},... | collective-permute-start | bytes 24584 | tf_op jit(solution)/shard_map/ppermute | solution.py:343
  8.5 2.4 %staging.1 = (bf16[2,256,128]{2,1,0:T(8,128)(2,1)S(1)}, bf16[128,256]{1,0:T(8,128)(2,1)S(1)}, bf16[2,64,128]{2,1,0:T(8,128)(2,1)S(1)}, bf16[128,256]{1,0:T(8,128...) custom-call(bf16[256,256]{1,0:T(8,128)(2,1)} %bitcast.2, ...), custom_call_target="tpu_custom_call" | custom-call | tf_op jit(solution)/shard_map/staging/pallas_call | solution.py:372
  11.0 0.8 %collective-permute-done.2.refs_6_ = bf16[32,128]{1,0:T(8,128)(2,1)S(1)} collective-permute-done((bf16[32,128]{1,0:T(8,128)(2,1)S(1)}, bf16[32,128]{1,0:T(8,128)(2,1)S(1)}, u32[]{:S(2)}, u32[]{:S(2)}) %collective-permute-start.2) | collective-permute-done | bytes 8224 | tf_op jit(solution)/shard_map/ppermute | solution.py:343
  11.8 0.0 collective-permute-done.1.refs_5_
  11.8 0.0 collective-permute-done.refs_4_
  11.8 0.5 %spectrum.1.refs_0_ = f32[64,128]{1,0:T(8,128)S(1)} custom-call(f32[128,128]{1,0:T(8,128)S(1)} %get-tuple-element.18.refs_0_, bf16[128,256]{1,0:T(8,128)(2,1)S(1)} %get-tuple-element.19.refs_1_, bf16[2,64,128]{2,1,0:T(8,128)(2,1)S(1)} %get-tuple-element.20.refs_2_, bf16[2,256,128]{2,1,0:T(8,128)(2,1)S(1)} %get-tuple-element.21.refs_3_, ...), custom_call_target="tpu_custom_call" | custom-call | tf_op jit(solution)/shard_map/spectrum/pallas_call | solution.py:383
  12.3 0.1 collective-permute-start.3
  12.3 1.2 %collective-permute-done.3.refs_1_ = f32[64,128]{1,0:T(8,128)S(1)} collective-permute-done((f32[64,128]{1,0:T(8,128)S(1)}, f32[64,128]{1,0:T(8,128)S(1)}, u32[]{:S(2)}, u32[]{:S(2)}) %collective-permute-start.3) | collective-permute-done | bytes 32800 | tf_op jit(solution)/shard_map/ppermute | solution.py:391
  13.5 5.0 %imaging.1 = (bf16[2,128,256]{2,1,0:T(8,128)(2,1)S(1)}, bf16[2,512,256]{2,1,0:T(8,128)(2,1)S(1)}) custom-call(f32[64,128]{1,0:T(8,128)S(1)} %spectrum.1.refs_0_, f32[64,128]{1,0:T(8,128)S(1)} %collective-permute-done.3.refs_1_, bf16[128,256]{1,0:T(8,128)(2,1)S(1)} %get-tuple-element.25.refs_2_, bf16[256,128]{1,0:T(8,128)(2,1)S(1)} %get-tuple-element.26.refs_3_, ...), custom_call_target="tpu_custom_call" | custom-call | tf_op jit(solution)/shard_map/imaging/pallas_call | solution.py:392
  18.5 0.2 %collective-permute-start.4 = (bf16[2,128,256]{2,1,0:T(8,128)(2,1)S(1)}, bf16[2,128,256]{2,1,0:T(8,128)(2,1)S(1)}, u32[]{:S(2)}, u32[]{:S(2)}) collective-permute-start(bf16[2,128,256]{2,1,0:T(8,128)(2,1)S(1)} %get-tuple-element.33), channel_id=1, source_target_pairs={{0,1},{1,0},{2,3},{3,2},{4,5},{5,4},{6,7},{7,6},{8,9},{9,8},{10,11... | collective-permute-start | bytes 393224 | tf_op jit(solution)/shard_map/ppermute | solution.py:407
  18.7 0.4 %own_share.1 = f32[2,128,256]{2,1,0:T(8,128)S(1)} custom-call(bf16[2,512,256]{2,1,0:T(8,128)(2,1)S(1)} %get-tuple-element.32.level_ref, f32[2,4,8,256]{3,2,1,0:T(8,128)S(1)} %get-tuple-element.31.refs_8_.gain_ref, bf16[2,256,128]{2,1,0:T(8,128)(2,1)S(1)} %get-tuple-element.27.refs_4_.spread_ref), custom_call_target="tpu_custom_call" | custom-call | tf_op jit(solution)/shard_map/own_share/pallas_call | solution.py:408
  19.1 0.8 %collective-permute-done.4 = bf16[2,128,256]{2,1,0:T(8,128)(2,1)S(1)} collective-permute-done((bf16[2,128,256]{2,1,0:T(8,128)(2,1)S(1)}, bf16[2,128,256]{2,1,0:T(8,128)(2,1)S(1)}, u32[]{:S(2)}, u32[]{:S(2)}) %collective-permute-start.4) | collective-permute-done | bytes 131104 | tf_op jit(solution)/shard_map/ppermute | solution.py:407
  19.9 0.7 %slice_minimum_fusion = (f32[1,128,256]{2,1,0:T(8,128)}, f32[1,128,256]{2,1,0:T(8,128)}) fusion(f32[2,128,256]{2,1,0:T(8,128)S(1)} %convert_element_type.3, f32[2,128,256]{2,1,0:T(8,128)S(1)} %own_share.1), kind=kLoop, calls=%fused_computation | loop fusion | flops 65536 | bytes 786432 | tf_op jit(solution)/shard_map/min | solution.py:417
  (1 shorter events, 0.0 us)
Async XLA Ops:
  1.6 10.2 %collective-permute-start = (bf16[128,128]{1,0:T(8,128)(2,1)S(1)}, bf16[128,128]{1,0:T(8,128)(2,1)S(1)}, u32[]{:S(2)}, u32[]{:S(2)}) collective-permute-start(bf16[128,128]{1,0:T(8,128)(2,1)S(1)} %get-tuple-element.22), channel_id=1, source_target_pairs={{14,0},{3,1},{0,2},{5,3},{2,4},{7,5},{4,6},{9,7},{6,8},{11,9},{8,1... | collective-permute-start | bytes 98312 | tf_op jit(solution)/shard_map/ppermute | solution.py:343
  4.6 7.2 %collective-permute-start.1 = (bf16[64,128]{1,0:T(8,128)(2,1)S(1)}, bf16[64,128]{1,0:T(8,128)(2,1)S(1)}, u32[]{:S(2)}, u32[]{:S(2)}) collective-permute-start(bf16[64,128]{1,0:T(8,128)(2,1)S(1)} %get-tuple-element.23), channel_id=1, source_target_pairs={{8,0},{10,2},{12,4},{14,6},{0,8},{2,10},{4,12},{6,14},{9,1},{11,3}... | collective-permute-start | bytes 49160 | tf_op jit(solution)/shard_map/ppermute | solution.py:305
  7.2 4.6 %collective-permute-start.2 = (bf16[32,128]{1,0:T(8,128)(2,1)S(1)}, bf16[32,128]{1,0:T(8,128)(2,1)S(1)}, u32[]{:S(2)}, u32[]{:S(2)}) collective-permute-start(bf16[32,128]{1,0:T(8,128)(2,1)S(1)} %get-tuple-element.24), channel_id=1, source_target_pairs={{6,0},{11,1},{8,2},{13,3},{10,4},{15,5},{12,6},{1,7},{14,8},{3,9},... | collective-permute-start | bytes 24584 | tf_op jit(solution)/shard_map/ppermute | solution.py:343
  12.3 1.3 %collective-permute-start.3 = (f32[64,128]{1,0:T(8,128)S(1)}, f32[64,128]{1,0:T(8,128)S(1)}, u32[]{:S(2)}, u32[]{:S(2)}) collective-permute-start(f32[64,128]{1,0:T(8,128)S(1)} %spectrum.1.refs_0_), channel_id=1, source_target_pairs={{0,1},{1,0},{2,3},{3,2},{4,5},{5,4},{6,7},{7,6},{8,9},{9,8},{10,11... | collective-permute-start | bytes 98312 | tf_op jit(solution)/shard_map/ppermute | solution.py:391
  18.5 1.4 %collective-permute-start.4 = (bf16[2,128,256]{2,1,0:T(8,128)(2,1)S(1)}, bf16[2,128,256]{2,1,0:T(8,128)(2,1)S(1)}, u32[]{:S(2)}, u32[]{:S(2)}) collective-permute-start(bf16[2,128,256]{2,1,0:T(8,128)(2,1)S(1)} %get-tuple-element.33), channel_id=1, source_target_pairs={{0,1},{1,0},{2,3},{3,2},{4,5},{5,4},{6,7},{7,6},{8,9},{9,8},{10,11... | collective-permute-start | bytes 393224 | tf_op jit(solution)/shard_map/ppermute | solution.py:407

commit v6 on v5

--- a/solution.py
+++ b/solution.py
@@ -235,7 +235,7 @@
     spec_same = jnp.where(first, spec, swapped)
     spec_cross = jnp.where(first, -swapped, spec)
 
-    def condition(c, carry):
+    def condition(c, halves_ref):
         prods = []
         for k in range(kerns):
             kern = kern_ref[c, k].astype(jnp.float32)
@@ -258,11 +258,21 @@
             shares = share_ref[pl.ds(c * kerns + k, 1)], share_ref[pl.ds(c * kerns + k + 1, 1)]
             total = total + shares[0] * power[:, :grid] + shares[1] * power[:, grid:]
         coarse_ref[c] = total
+
+    turns = 4
+
+    def turn(i, carry):
+        for j in range(turns):
+            condition(i * turns + j, halves_ref.at[j])
         return carry
 
-    lax.fori_loop(0, conds, condition, 0)
+    if conds == turns:
+        turn(0, 0)
+    else:
+        lax.fori_loop(0, conds // turns, turn, 0)
     high, low = split(coarse_ref[...].reshape(conds * grid, grid))
-    across = dot(high, across_ref[0]) + dot(low, across_ref[0]) + dot(high, across_ref[1])
+    twice = jnp.concatenate([across_ref[0], across_ref[0]], axis=0)
+    across = dot(jnp.concatenate([high, low], axis=1), twice) + dot(high, across_ref[1])
     level_ref[0], level_ref[1] = split(across)
     most, least = band_of(1 - lax.axis_index("cond"), level_ref, gain_ref, spread_ref)
     send_ref[0] = most.astype(jnp.bfloat16)
@@ -275,11 +285,12 @@
     grid = level_ref.shape[1] // conds
     share = core // 2
     rows = pl.ds(pl.multiple_of(part_of * share, share), share)
+    fine, rest = spread_ref[0, rows], spread_ref[1, rows]
+    twice = jnp.concatenate([fine, fine], axis=1)
     for c in range(conds):
         h = level_ref[0, c * grid : (c + 1) * grid]
         l = level_ref[1, c * grid : (c + 1) * grid]
-        blurred = dot(spread_ref[0, rows], h)
-        blurred = blurred + dot(spread_ref[0, rows], l) + dot(spread_ref[1, rows], h)
+        blurred = dot(twice, jnp.concatenate([h, l], axis=0)) + dot(rest, h)
         level = gain_ref[0, c, :1] * blurred - gain_ref[1, c, :1]
         most = level if c == 0 else jnp.maximum(most, level)
         least = level if c == 0 else jnp.minimum(least, level)
@@ -398,7 +409,7 @@
         in_specs=[vmem] * 9,
         out_specs=(vmem, vmem),
         scratch_shapes=[
-            pltpu.VMEM((kerns * band, 2 * grid), jnp.bfloat16),
+            pltpu.VMEM((4, kerns * band, 2 * grid), jnp.bfloat16),
             pltpu.VMEM((conds, grid, grid), jnp.float32),
         ],
         compiler_params=params,

time: 20.9 us -> 19.4 us (0.928)
  Pallas kernels: 9.21 us -> 7.72 us
    pallas_call x1, Pallas kernels: 4.96 us -> 3.54 us  [on_device(): pl.pallas_call(lambda *refs: imaging(*refs, pad=pad), out_shape=(jax.Shap...]
where the time goes in v6:
time: 19.4 us; the launch traced here: 19.2 us
  Pallas kernels  7.72 us (40%)
  starting transfers between devices  7.23 us (37%)
  waiting for transfers between devices  2.86 us (15%)
  other arithmetic  0.75 us (4%)
  between operations  0.68 us (4%)
    ppermute x2, starting transfers between devices, passed(): return lax.ppermute(block, ('tile', 'cond'), pairs)  4.34 us
    pallas_call x1, Pallas kernels, on_device(): pl.pallas_call(lambda *refs: imaging(*refs, pad=pad), out_shape=(jax.Shap...  3.54 us
    ppermute x1, starting transfers between devices, shifted(): lax.ppermute(block, axis, [((i - distance) % count, i) for i in range(cou...  2.59 us
    pallas_call x1, Pallas kernels, on_device(): pl.pallas_call(lambda *refs: staging(*refs, count=len(fixed)), out_shape=...  2.44 us
    ppermute x1, waiting for transfers between devices, on_device(): other = lax.ppermute(mine, 'cond', [(0, 1), (1, 0)])  1.19 us
    pallas_call x1, Pallas kernels, on_device(): pl.pallas_call(lambda *refs: cut(*refs, sides=sides), out_shape=[jax.Shap...  0.95 us
    ppermute x1, waiting for transfers between devices, on_device(): other = lax.ppermute(send, 'cond', [(0, 1), (1, 0)])  0.86 us
    ppermute x2, waiting for transfers between devices, passed(): return lax.ppermute(block, ('tile', 'cond'), pairs)  0.8 us
  transfers between devices with their start and end apart: 5, of which 3 were waited for; matrix products, arithmetic and copies ran while one was open for 0% of the time, Pallas kernels for 14%

profile of v6, /device:TPU:0, one launch (start us, length us, event | category | flops | bytes accessed | tf_op | source)
XLA Modules:
  0.0 19.2 jit_solution(12841784948660065609)
XLA Ops:
  0.6 0.9 %cut.1 = (bf16[128,128]{1,0:T(8,128)(2,1)S(1)}, bf16[64,128]{1,0:T(8,128)(2,1)S(1)}, bf16[32,128]{1,0:T(8,128)(2,1)S(1)}) custom-call(bf16[256,256]{1,0:T(8,128)(2,1)} %bitcast.1), custom_call_target="tpu_custom_call" | custom-call | tf_op jit(solution)/shard_map/cut/pallas_call | solution.py:334
  1.6 3.0 %collective-permute-start = (bf16[128,128]{1,0:T(8,128)(2,1)S(1)}, bf16[128,128]{1,0:T(8,128)(2,1)S(1)}, u32[]{:S(2)}, u32[]{:S(2)}) collective-permute-start(bf16[128,128]{1,0:T(8,128)(2,1)S(1)} %get-tuple-element.22), channel_id=1, source_target_pairs={{14,0},{3,1},{0,2},{5,3},{2,4},{7,5},{4,6},{9,7},{6,8},{11,9},{8,1... | collective-permute-start | bytes 98312 | tf_op jit(solution)/shard_map/ppermute | solution.py:354
  4.6 2.6 %collective-permute-start.1 = (bf16[64,128]{1,0:T(8,128)(2,1)S(1)}, bf16[64,128]{1,0:T(8,128)(2,1)S(1)}, u32[]{:S(2)}, u32[]{:S(2)}) collective-permute-start(bf16[64,128]{1,0:T(8,128)(2,1)S(1)} %get-tuple-element.23), channel_id=1, source_target_pairs={{8,0},{10,2},{12,4},{14,6},{0,8},{2,10},{4,12},{6,14},{9,1},{11,3}... | collective-permute-start | bytes 49160 | tf_op jit(solution)/shard_map/ppermute | solution.py:316
  7.2 1.3 %collective-permute-start.2 = (bf16[32,128]{1,0:T(8,128)(2,1)S(1)}, bf16[32,128]{1,0:T(8,128)(2,1)S(1)}, u32[]{:S(2)}, u32[]{:S(2)}) collective-permute-start(bf16[32,128]{1,0:T(8,128)(2,1)S(1)} %get-tuple-element.24), channel_id=1, source_target_pairs={{6,0},{11,1},{8,2},{13,3},{10,4},{15,5},{12,6},{1,7},{14,8},{3,9},... | collective-permute-start | bytes 24584 | tf_op jit(solution)/shard_map/ppermute | solution.py:354
  8.5 2.4 %staging.1 = (bf16[2,256,128]{2,1,0:T(8,128)(2,1)S(1)}, bf16[128,256]{1,0:T(8,128)(2,1)S(1)}, bf16[2,64,128]{2,1,0:T(8,128)(2,1)S(1)}, bf16[128,256]{1,0:T(8,128...) custom-call(bf16[256,256]{1,0:T(8,128)(2,1)} %bitcast.2, ...), custom_call_target="tpu_custom_call" | custom-call | tf_op jit(solution)/shard_map/staging/pallas_call | solution.py:383
  11.0 0.8 %collective-permute-done.2.refs_6_ = bf16[32,128]{1,0:T(8,128)(2,1)S(1)} collective-permute-done((bf16[32,128]{1,0:T(8,128)(2,1)S(1)}, bf16[32,128]{1,0:T(8,128)(2,1)S(1)}, u32[]{:S(2)}, u32[]{:S(2)}) %collective-permute-start.2) | collective-permute-done | bytes 8224 | tf_op jit(solution)/shard_map/ppermute | solution.py:354
  11.8 0.0 collective-permute-done.1.refs_5_
  11.8 0.0 collective-permute-done.refs_4_
  11.8 0.5 %spectrum.1.refs_0_ = f32[64,128]{1,0:T(8,128)S(1)} custom-call(f32[128,128]{1,0:T(8,128)S(1)} %get-tuple-element.18.refs_0_, bf16[128,256]{1,0:T(8,128)(2,1)S(1)} %get-tuple-element.19.refs_1_, bf16[2,64,128]{2,1,0:T(8,128)(2,1)S(1)} %get-tuple-element.20.refs_2_, bf16[2,256,128]{2,1,0:T(8,128)(2,1)S(1)} %get-tuple-element.21.refs_3_, ...), custom_call_target="tpu_custom_call" | custom-call | tf_op jit(solution)/shard_map/spectrum/pallas_call | solution.py:394
  12.3 0.1 collective-permute-start.3
  12.3 1.2 %collective-permute-done.3.refs_1_ = f32[64,128]{1,0:T(8,128)S(1)} collective-permute-done((f32[64,128]{1,0:T(8,128)S(1)}, f32[64,128]{1,0:T(8,128)S(1)}, u32[]{:S(2)}, u32[]{:S(2)}) %collective-permute-start.3) | collective-permute-done | bytes 32800 | tf_op jit(solution)/shard_map/ppermute | solution.py:402
  13.5 3.5 %imaging.1 = (bf16[2,128,256]{2,1,0:T(8,128)(2,1)S(1)}, bf16[2,512,256]{2,1,0:T(8,128)(2,1)S(1)}) custom-call(f32[64,128]{1,0:T(8,128)S(1)} %spectrum.1.refs_0_, f32[64,128]{1,0:T(8,128)S(1)} %collective-permute-done.3.refs_1_, bf16[128,256]{1,0:T(8,128)(2,1)S(1)} %get-tuple-element.25.refs_2_, bf16[256,128]{1,0:T(8,128)(2,1)S(1)} %get-tuple-element.26.refs_3_, ...), custom_call_target="tpu_custom_call" | custom-call | tf_op jit(solution)/shard_map/imaging/pallas_call | solution.py:403
  17.1 0.2 %collective-permute-start.4 = (bf16[2,128,256]{2,1,0:T(8,128)(2,1)S(1)}, bf16[2,128,256]{2,1,0:T(8,128)(2,1)S(1)}, u32[]{:S(2)}, u32[]{:S(2)}) collective-permute-start(bf16[2,128,256]{2,1,0:T(8,128)(2,1)S(1)} %get-tuple-element.33), channel_id=1, source_target_pairs={{0,1},{1,0},{2,3},{3,2},{4,5},{5,4},{6,7},{7,6},{8,9},{9,8},{10,11... | collective-permute-start | bytes 393224 | tf_op jit(solution)/shard_map/ppermute | solution.py:418
  17.3 0.3 %own_share.1 = f32[2,128,256]{2,1,0:T(8,128)S(1)} custom-call(bf16[2,512,256]{2,1,0:T(8,128)(2,1)S(1)} %get-tuple-element.32.level_ref, f32[2,4,8,256]{3,2,1,0:T(8,128)S(1)} %get-tuple-element.31.refs_8_.gain_ref, bf16[2,256,128]{2,1,0:T(8,128)(2,1)S(1)} %get-tuple-element.27.refs_4_.spread_ref), custom_call_target="tpu_custom_call" | custom-call | tf_op jit(solution)/shard_map/own_share/pallas_call | solution.py:419
  17.6 0.9 %collective-permute-done.4 = bf16[2,128,256]{2,1,0:T(8,128)(2,1)S(1)} collective-permute-done((bf16[2,128,256]{2,1,0:T(8,128)(2,1)S(1)}, bf16[2,128,256]{2,1,0:T(8,128)(2,1)S(1)}, u32[]{:S(2)}, u32[]{:S(2)}) %collective-permute-start.4) | collective-permute-done | bytes 131104 | tf_op jit(solution)/shard_map/ppermute | solution.py:418
  18.5 0.7 %slice_minimum_fusion = (f32[1,128,256]{2,1,0:T(8,128)}, f32[1,128,256]{2,1,0:T(8,128)}) fusion(f32[2,128,256]{2,1,0:T(8,128)S(1)} %convert_element_type.3, f32[2,128,256]{2,1,0:T(8,128)S(1)} %own_share.1), kind=kLoop, calls=%fused_computation | loop fusion | flops 65536 | bytes 786432 | tf_op jit(solution)/shard_map/min | solution.py:428
  (1 shorter events, 0.0 us)
Async XLA Ops:
  1.6 10.2 %collective-permute-start = (bf16[128,128]{1,0:T(8,128)(2,1)S(1)}, bf16[128,128]{1,0:T(8,128)(2,1)S(1)}, u32[]{:S(2)}, u32[]{:S(2)}) collective-permute-start(bf16[128,128]{1,0:T(8,128)(2,1)S(1)} %get-tuple-element.22), channel_id=1, source_target_pairs={{14,0},{3,1},{0,2},{5,3},{2,4},{7,5},{4,6},{9,7},{6,8},{11,9},{8,1... | collective-permute-start | bytes 98312 | tf_op jit(solution)/shard_map/ppermute | solution.py:354
  4.6 7.2 %collective-permute-start.1 = (bf16[64,128]{1,0:T(8,128)(2,1)S(1)}, bf16[64,128]{1,0:T(8,128)(2,1)S(1)}, u32[]{:S(2)}, u32[]{:S(2)}) collective-permute-start(bf16[64,128]{1,0:T(8,128)(2,1)S(1)} %get-tuple-element.23), channel_id=1, source_target_pairs={{8,0},{10,2},{12,4},{14,6},{0,8},{2,10},{4,12},{6,14},{9,1},{11,3}... | collective-permute-start | bytes 49160 | tf_op jit(solution)/shard_map/ppermute | solution.py:316
  7.2 4.6 %collective-permute-start.2 = (bf16[32,128]{1,0:T(8,128)(2,1)S(1)}, bf16[32,128]{1,0:T(8,128)(2,1)S(1)}, u32[]{:S(2)}, u32[]{:S(2)}) collective-permute-start(bf16[32,128]{1,0:T(8,128)(2,1)S(1)} %get-tuple-element.24), channel_id=1, source_target_pairs={{6,0},{11,1},{8,2},{13,3},{10,4},{15,5},{12,6},{1,7},{14,8},{3,9},... | collective-permute-start | bytes 24584 | tf_op jit(solution)/shard_map/ppermute | solution.py:354
  12.3 1.3 %collective-permute-start.3 = (f32[64,128]{1,0:T(8,128)S(1)}, f32[64,128]{1,0:T(8,128)S(1)}, u32[]{:S(2)}, u32[]{:S(2)}) collective-permute-start(f32[64,128]{1,0:T(8,128)S(1)} %spectrum.1.refs_0_), channel_id=1, source_target_pairs={{0,1},{1,0},{2,3},{3,2},{4,5},{5,4},{6,7},{7,6},{8,9},{9,8},{10,11... | collective-permute-start | bytes 98312 | tf_op jit(solution)/shard_map/ppermute | solution.py:402
  17.1 1.4 %collective-permute-start.4 = (bf16[2,128,256]{2,1,0:T(8,128)(2,1)S(1)}, bf16[2,128,256]{2,1,0:T(8,128)(2,1)S(1)}, u32[]{:S(2)}, u32[]{:S(2)}) collective-permute-start(bf16[2,128,256]{2,1,0:T(8,128)(2,1)S(1)} %get-tuple-element.33), channel_id=1, source_target_pairs={{0,1},{1,0},{2,3},{3,2},{4,5},{5,4},{6,7},{7,6},{8,9},{9,8},{10,11... | collective-permute-start | bytes 393224 | tf_op jit(solution)/shard_map/ppermute | solution.py:418

commit v7 on v6

--- a/solution.py
+++ b/solution.py
@@ -90,7 +90,7 @@
         above=row > 0,
         below=row < grid_rows - 1,
         top=row == 0,
-        half=lax.axis_index("cond"),
+        side=(lax.axis_index("cond") == column % 2).astype(jnp.int32),
     )
 
 
@@ -100,7 +100,7 @@
 
 def native_lanes(shape):
     upper = (lax.broadcasted_iota(jnp.int32, shape, 1) >= MARGIN).astype(jnp.int32)
-    return upper != lax.axis_index("cond")
+    return upper == placement()["side"]
 
 
 def folded(block):
@@ -122,7 +122,7 @@
         2 * count + 4 :
     ]
     core, half = tile_ref.shape
-    own = lax.axis_index("cond")
+    own = placement()["side"]
     first = pl.multiple_of(own * half, half)
     pairs = [
         (weight_hbm, weight_ref),
@@ -157,8 +157,8 @@
     block_ref, sems = refs[2 * len(sides) :]
     core, wide = block_ref.shape
     half = upright_refs[0].shape[1]
-    own = lax.axis_index("cond")
-    beside = pl.multiple_of((1 - own) * (core - wide), wide)
+    own = placement()["side"]
+    beside = pl.multiple_of(own * (core - wide), wide)
     first = pl.multiple_of(own * half, half)
     rows = []
     for side in sides:
@@ -203,7 +203,7 @@
             more = [jnp.where(there, m, jnp.zeros_like(m)) for m in more]
         core, ahead, behind = core + more[0], ahead + more[1], behind + more[2]
     edge = ahead + pltpu.roll(behind, MARGIN, 1)
-    beside = jnp.where(place["half"] == 0, place["left"], place["right"])
+    beside = jnp.where(place["side"] == 0, place["left"], place["right"])
     edge = jnp.where(beside, edge, jnp.zeros_like(edge))
     part = jnp.concatenate([core, edge], axis=1).astype(jnp.bfloat16)
     spec_ref[...] = dot(part[:band], columns_ref[0]) + dot(part[band:], columns_ref[1])
@@ -325,6 +325,7 @@
     place = placement()
     count = lax.axis_size("tile")
     columns, grid_rows = place["columns"], place["grid_rows"]
+    assert columns % 4 == 0
 
     half, wide = core // 2, 2 * MARGIN
     sides = (None,) if grid_rows == 2 else (0, 1)
@@ -349,8 +350,9 @@
     def passed(block, shift):
         pairs = []
         for t in range(count):
-            pairs.append((2 * ((t - shift - 1) % count), 2 * t))
-            pairs.append((2 * ((t - shift + 1) % count) + 1, 2 * t + 1))
+            for c in range(2):
+                partner = t + 1 if t % 2 == c else t - 1
+                pairs.append((2 * ((partner - shift) % count) + c, 2 * t + c))
         return lax.ppermute(block, ("tile", "cond"), pairs)
 
     shifts = [-columns if side else columns for side in sides]

time: 19.4 us -> 20.3 us (1.046)
  waiting for transfers between devices: 2.86 us -> 5.05 us
  starting transfers between devices: 7.23 us -> 5.92 us
    ppermute x2, waiting for transfers between devices: 0.8 us -> 3 us  [passed(): return lax.ppermute(block, ('tile', 'cond'), pairs)]
    ppermute x2, starting transfers between devices: 4.34 us -> 3.03 us  [passed(): return lax.ppermute(block, ('tile', 'cond'), pairs)]
where the time goes in v7:
time: 20.3 us; the launch traced here: 20.2 us
  Pallas kernels  7.74 us (38%)
  starting transfers between devices  5.92 us (29%)
  waiting for transfers between devices  5.05 us (25%)
  other arithmetic  0.75 us (4%)
  between operations  0.68 us (3%)
    pallas_call x1, Pallas kernels, on_device(): pl.pallas_call(lambda *refs: imaging(*refs, pad=pad), out_shape=(jax.Shap...  3.54 us
    ppermute x2, starting transfers between devices, passed(): return lax.ppermute(block, ('tile', 'cond'), pairs)  3.03 us
    ppermute x2, waiting for transfers between devices, passed(): return lax.ppermute(block, ('tile', 'cond'), pairs)  3 us
    ppermute x1, starting transfers between devices, shifted(): lax.ppermute(block, axis, [((i - distance) % count, i) for i in range(cou...  2.59 us
    pallas_call x1, Pallas kernels, on_device(): pl.pallas_call(lambda *refs: staging(*refs, count=len(fixed)), out_shape=...  2.44 us
    ppermute x1, waiting for transfers between devices, on_device(): other = lax.ppermute(mine, 'cond', [(0, 1), (1, 0)])  1.19 us
    pallas_call x1, Pallas kernels, on_device(): pl.pallas_call(lambda *refs: cut(*refs, sides=sides), out_shape=[jax.Shap...  0.97 us
    ppermute x1, waiting for transfers between devices, on_device(): other = lax.ppermute(send, 'cond', [(0, 1), (1, 0)])  0.86 us
  transfers between devices with their start and end apart: 5, of which 3 were waited for; matrix products, arithmetic and copies ran while one was open for 0% of the time, Pallas kernels for 14%

profile of v7, /device:TPU:0, one launch (start us, length us, event | category | flops | bytes accessed | tf_op | source)
XLA Modules:
  0.0 20.2 jit_solution(10656168943944612033)
XLA Ops:
  0.6 1.0 %cut.1 = (bf16[128,128]{1,0:T(8,128)(2,1)S(1)}, bf16[64,128]{1,0:T(8,128)(2,1)S(1)}, bf16[32,128]{1,0:T(8,128)(2,1)S(1)}) custom-call(bf16[256,256]{1,0:T(8,128)(2,1)} %bitcast.1), custom_call_target="tpu_custom_call" | custom-call | tf_op jit(solution)/shard_map/cut/pallas_call | solution.py:335
  1.6 3.0 %collective-permute-start = (bf16[128,128]{1,0:T(8,128)(2,1)S(1)}, bf16[128,128]{1,0:T(8,128)(2,1)S(1)}, u32[]{:S(2)}, u32[]{:S(2)}) collective-permute-start(bf16[128,128]{1,0:T(8,128)(2,1)S(1)} %get-tuple-element.22), channel_id=1, source_target_pairs={{2,0},{15,1},{0,2},{5,3},{6,4},{3,5},{4,6},{9,7},{10,8},{7,9},{8,1... | collective-permute-start | bytes 98312 | tf_op jit(solution)/shard_map/ppermute | solution.py:356
  4.6 2.6 %collective-permute-start.1 = (bf16[64,128]{1,0:T(8,128)(2,1)S(1)}, bf16[64,128]{1,0:T(8,128)(2,1)S(1)}, u32[]{:S(2)}, u32[]{:S(2)}) collective-permute-start(bf16[64,128]{1,0:T(8,128)(2,1)S(1)} %get-tuple-element.23), channel_id=1, source_target_pairs={{8,0},{10,2},{12,4},{14,6},{0,8},{2,10},{4,12},{6,14},{9,1},{11,3}... | collective-permute-start | bytes 49160 | tf_op jit(solution)/shard_map/ppermute | solution.py:316
  7.2 0.0 collective-permute-start.2
  7.2 2.4 %staging.1 = (bf16[2,256,128]{2,1,0:T(8,128)(2,1)S(1)}, bf16[128,256]{1,0:T(8,128)(2,1)S(1)}, bf16[2,64,128]{2,1,0:T(8,128)(2,1)S(1)}, bf16[128,256]{1,0:T(8,128...) custom-call(bf16[256,256]{1,0:T(8,128)(2,1)} %bitcast.2, ...), custom_call_target="tpu_custom_call" | custom-call | tf_op jit(solution)/shard_map/staging/pallas_call | solution.py:385
  9.7 3.0 %collective-permute-done.2.refs_6_ = bf16[32,128]{1,0:T(8,128)(2,1)S(1)} collective-permute-done((bf16[32,128]{1,0:T(8,128)(2,1)S(1)}, bf16[32,128]{1,0:T(8,128)(2,1)S(1)}, u32[]{:S(2)}, u32[]{:S(2)}) %collective-permute-start.2) | collective-permute-done | bytes 8224 | tf_op jit(solution)/shard_map/ppermute | solution.py:356
  12.7 0.0 collective-permute-done.1.refs_5_
  12.7 0.0 collective-permute-done.refs_4_
  12.7 0.5 %spectrum.1.refs_0_ = f32[64,128]{1,0:T(8,128)S(1)} custom-call(f32[128,128]{1,0:T(8,128)S(1)} %get-tuple-element.18.refs_0_, bf16[128,256]{1,0:T(8,128)(2,1)S(1)} %get-tuple-element.19.refs_1_, bf16[2,64,128]{2,1,0:T(8,128)(2,1)S(1)} %get-tuple-element.20.refs_2_, bf16[2,256,128]{2,1,0:T(8,128)(2,1)S(1)} %get-tuple-element.21.refs_3_, ...), custom_call_target="tpu_custom_call" | custom-call | tf_op jit(solution)/shard_map/spectrum/pallas_call | solution.py:396
  13.2 0.1 collective-permute-start.3
  13.2 1.2 %collective-permute-done.3.refs_1_ = f32[64,128]{1,0:T(8,128)S(1)} collective-permute-done((f32[64,128]{1,0:T(8,128)S(1)}, f32[64,128]{1,0:T(8,128)S(1)}, u32[]{:S(2)}, u32[]{:S(2)}) %collective-permute-start.3) | collective-permute-done | bytes 32800 | tf_op jit(solution)/shard_map/ppermute | solution.py:404
  14.4 3.5 %imaging.1 = (bf16[2,128,256]{2,1,0:T(8,128)(2,1)S(1)}, bf16[2,512,256]{2,1,0:T(8,128)(2,1)S(1)}) custom-call(f32[64,128]{1,0:T(8,128)S(1)} %spectrum.1.refs_0_, f32[64,128]{1,0:T(8,128)S(1)} %collective-permute-done.3.refs_1_, bf16[128,256]{1,0:T(8,128)(2,1)S(1)} %get-tuple-element.25.refs_2_, bf16[256,128]{1,0:T(8,128)(2,1)S(1)} %get-tuple-element.26.refs_3_, ...), custom_call_target="tpu_custom_call" | custom-call | tf_op jit(solution)/shard_map/imaging/pallas_call | solution.py:405
  18.0 0.2 %collective-permute-start.4 = (bf16[2,128,256]{2,1,0:T(8,128)(2,1)S(1)}, bf16[2,128,256]{2,1,0:T(8,128)(2,1)S(1)}, u32[]{:S(2)}, u32[]{:S(2)}) collective-permute-start(bf16[2,128,256]{2,1,0:T(8,128)(2,1)S(1)} %get-tuple-element.33), channel_id=1, source_target_pairs={{0,1},{1,0},{2,3},{3,2},{4,5},{5,4},{6,7},{7,6},{8,9},{9,8},{10,11... | collective-permute-start | bytes 393224 | tf_op jit(solution)/shard_map/ppermute | solution.py:420
  18.2 0.3 %own_share.1 = f32[2,128,256]{2,1,0:T(8,128)S(1)} custom-call(bf16[2,512,256]{2,1,0:T(8,128)(2,1)S(1)} %get-tuple-element.32.level_ref, f32[2,4,8,256]{3,2,1,0:T(8,128)S(1)} %get-tuple-element.31.refs_8_.gain_ref, bf16[2,256,128]{2,1,0:T(8,128)(2,1)S(1)} %get-tuple-element.27.refs_4_.spread_ref), custom_call_target="tpu_custom_call" | custom-call | tf_op jit(solution)/shard_map/own_share/pallas_call | solution.py:421
  18.5 0.9 %collective-permute-done.4 = bf16[2,128,256]{2,1,0:T(8,128)(2,1)S(1)} collective-permute-done((bf16[2,128,256]{2,1,0:T(8,128)(2,1)S(1)}, bf16[2,128,256]{2,1,0:T(8,128)(2,1)S(1)}, u32[]{:S(2)}, u32[]{:S(2)}) %collective-permute-start.4) | collective-permute-done | bytes 131104 | tf_op jit(solution)/shard_map/ppermute | solution.py:420
  19.4 0.7 %slice_minimum_fusion = (f32[1,128,256]{2,1,0:T(8,128)}, f32[1,128,256]{2,1,0:T(8,128)}) fusion(f32[2,128,256]{2,1,0:T(8,128)S(1)} %convert_element_type.3, f32[2,128,256]{2,1,0:T(8,128)S(1)} %own_share.1), kind=kLoop, calls=%fused_computation | loop fusion | flops 65536 | bytes 786432 | tf_op jit(solution)/shard_map/min | solution.py:430
  (1 shorter events, 0.0 us)
Async XLA Ops:
  1.6 11.1 %collective-permute-start = (bf16[128,128]{1,0:T(8,128)(2,1)S(1)}, bf16[128,128]{1,0:T(8,128)(2,1)S(1)}, u32[]{:S(2)}, u32[]{:S(2)}) collective-permute-start(bf16[128,128]{1,0:T(8,128)(2,1)S(1)} %get-tuple-element.22), channel_id=1, source_target_pairs={{2,0},{15,1},{0,2},{5,3},{6,4},{3,5},{4,6},{9,7},{10,8},{7,9},{8,1... | collective-permute-start | bytes 98312 | tf_op jit(solution)/shard_map/ppermute | solution.py:356
  4.6 8.0 %collective-permute-start.1 = (bf16[64,128]{1,0:T(8,128)(2,1)S(1)}, bf16[64,128]{1,0:T(8,128)(2,1)S(1)}, u32[]{:S(2)}, u32[]{:S(2)}) collective-permute-start(bf16[64,128]{1,0:T(8,128)(2,1)S(1)} %get-tuple-element.23), channel_id=1, source_target_pairs={{8,0},{10,2},{12,4},{14,6},{0,8},{2,10},{4,12},{6,14},{9,1},{11,3}... | collective-permute-start | bytes 49160 | tf_op jit(solution)/shard_map/ppermute | solution.py:316
  7.2 5.4 %collective-permute-start.2 = (bf16[32,128]{1,0:T(8,128)(2,1)S(1)}, bf16[32,128]{1,0:T(8,128)(2,1)S(1)}, u32[]{:S(2)}, u32[]{:S(2)}) collective-permute-start(bf16[32,128]{1,0:T(8,128)(2,1)S(1)} %get-tuple-element.24), channel_id=1, source_target_pairs={{10,0},{7,1},{8,2},{13,3},{14,4},{11,5},{12,6},{1,7},{2,8},{15,9},... | collective-permute-start | bytes 24584 | tf_op jit(solution)/shard_map/ppermute | solution.py:356
  13.2 1.3 %collective-permute-start.3 = (f32[64,128]{1,0:T(8,128)S(1)}, f32[64,128]{1,0:T(8,128)S(1)}, u32[]{:S(2)}, u32[]{:S(2)}) collective-permute-start(f32[64,128]{1,0:T(8,128)S(1)} %spectrum.1.refs_0_), channel_id=1, source_target_pairs={{0,1},{1,0},{2,3},{3,2},{4,5},{5,4},{6,7},{7,6},{8,9},{9,8},{10,11... | collective-permute-start | bytes 98312 | tf_op jit(solution)/shard_map/ppermute | solution.py:404
  18.0 1.4 %collective-permute-start.4 = (bf16[2,128,256]{2,1,0:T(8,128)(2,1)S(1)}, bf16[2,128,256]{2,1,0:T(8,128)(2,1)S(1)}, u32[]{:S(2)}, u32[]{:S(2)}) collective-permute-start(bf16[2,128,256]{2,1,0:T(8,128)(2,1)S(1)} %get-tuple-element.33), channel_id=1, source_target_pairs={{0,1},{1,0},{2,3},{3,2},{4,5},{5,4},{6,7},{7,6},{8,9},{9,8},{10,11... | collective-permute-start | bytes 393224 | tf_op jit(solution)/shard_map/ppermute | solution.py:420

commit v8 on v6

--- a/solution.py
+++ b/solution.py
@@ -181,32 +181,48 @@
         copy.wait()
 
 
-def spectrum(core_ref, row_core_ref, row_side_ref, columns_ref, strip_ref, *rest, sides):
-    upright_refs, corner_refs = rest[: len(sides)], rest[len(sides) : 2 * len(sides)]
-    spec_ref = rest[-1]
+def vertical(place, side, row_side_ref):
+    if side is None:
+        return row_side_ref.at[place["top"].astype(jnp.int32)], None
+    return row_side_ref.at[side], place["below"] if side else place["above"]
+
+
+def kept(there, value):
+    return value if there is None else jnp.where(there, value, jnp.zeros_like(value))
+
+
+def window(core_ref, row_core_ref, row_side_ref, strip_ref, *rest, sides):
+    *upright_refs, out_ref, edge_ref = rest
+    place = placement()
+    fold = strip_ref.shape[0]
+    core = core_ref[...]
+    for side, upright_ref in zip(sides, upright_refs):
+        table, there = vertical(place, side, row_side_ref)
+        core = core + kept(there, dot_first(table[...], upright_ref[...]))
+    out_ref[...] = core.astype(jnp.bfloat16)
+    ahead = dot(row_core_ref[:, :fold], strip_ref[...])
+    behind = dot(row_core_ref[:, fold:], strip_ref[...])
+    edge_ref[...] = ahead + pltpu.roll(behind, MARGIN, 1)
+
+
+def spectrum(core_ref, edge_ref, row_side_ref, columns_ref, *rest, sides):
+    *corner_refs, spec_ref = rest
     place = placement()
     band = spec_ref.shape[0]
-    fold = strip_ref.shape[0]
-    fold_side = corner_refs[0].shape[0]
+    half = core_ref.shape[1]
+    edge = edge_ref[...]
+    for side, corner_ref in zip(sides, corner_refs):
+        table, there = vertical(place, side, row_side_ref)
+        fold = corner_ref.shape[0]
+        behind = pltpu.roll(dot_first(table[fold:], corner_ref[...]), MARGIN, 1)
+        edge = edge + kept(there, dot_first(table[:fold], corner_ref[...]) + behind)
+    beside = jnp.where(place["half"] == 0, place["left"], place["right"])
+    edge = kept(beside, edge).astype(jnp.bfloat16)
     core = core_ref[...]
-    ahead = dot(row_core_ref[:, :fold], strip_ref[...])
-    behind = dot(row_core_ref[:, fold:], strip_ref[...])
-    for n, side in enumerate(sides):
-        table = row_side_ref.at[place["top"].astype(jnp.int32) if side is None else side]
-        more = (
-            dot_first(table[...], upright_refs[n][...]),
-            dot_first(table[:fold_side], corner_refs[n][...]),
-            dot_first(table[fold_side:], corner_refs[n][...]),
-        )
-        if side is not None:
-            there = place["below"] if side else place["above"]
-            more = [jnp.where(there, m, jnp.zeros_like(m)) for m in more]
-        core, ahead, behind = core + more[0], ahead + more[1], behind + more[2]
-    edge = ahead + pltpu.roll(behind, MARGIN, 1)
-    beside = jnp.where(place["half"] == 0, place["left"], place["right"])
-    edge = jnp.where(beside, edge, jnp.zeros_like(edge))
-    part = jnp.concatenate([core, edge], axis=1).astype(jnp.bfloat16)
-    spec_ref[...] = dot(part[:band], columns_ref[0]) + dot(part[band:], columns_ref[1])
+    spec = dot(core[:band], columns_ref[0, :half]) + dot(core[band:], columns_ref[1, :half])
+    spec_ref[...] = (
+        spec + dot(edge[:band], columns_ref[0, half:]) + dot(edge[band:], columns_ref[1, half:])
+    )
 
 
 def imaging(
@@ -259,21 +275,14 @@
             total = total + shares[0] * power[:, :grid] + shares[1] * power[:, grid:]
         coarse_ref[c] = total
 
-    turns = 4
-
-    def turn(i, carry):
-        for j in range(turns):
-            condition(i * turns + j, halves_ref.at[j])
-        return carry
-
-    if conds == turns:
-        turn(0, 0)
-    else:
-        lax.fori_loop(0, conds // turns, turn, 0)
-    high, low = split(coarse_ref[...].reshape(conds * grid, grid))
+    for c in range(conds):
+        condition(c, halves_ref.at[c])
     twice = jnp.concatenate([across_ref[0], across_ref[0]], axis=0)
-    across = dot(jnp.concatenate([high, low], axis=1), twice) + dot(high, across_ref[1])
-    level_ref[0], level_ref[1] = split(across)
+    for c in range(conds):
+        rows = slice(c * grid, (c + 1) * grid)
+        high, low = split(coarse_ref[c])
+        across = dot(jnp.concatenate([high, low], axis=1), twice) + dot(high, across_ref[1])
+        level_ref[0, rows], level_ref[1, rows] = split(across)
     most, least = band_of(1 - lax.axis_index("cond"), level_ref, gain_ref, spread_ref)
     send_ref[0] = most.astype(jnp.bfloat16)
     send_ref[1] = least.astype(jnp.bfloat16)
@@ -391,14 +400,25 @@
             name="staging",
         )(*map(in_hbm, (tile, *scalars, *fixed)))
     )
+    part, edge = pl.pallas_call(
+        lambda *refs: window(*refs, sides=sides),
+        out_shape=[
+            jax.ShapeDtypeStruct((2 * band, half), jnp.bfloat16),
+            jax.ShapeDtypeStruct((2 * band, wide), jnp.float32),
+        ],
+        in_specs=[vmem] * (4 + len(sides)),
+        out_specs=[vmem] * 2,
+        compiler_params=params,
+        name="window",
+    )(part, row_v, side_v, strip, *uprights)
     mine = pl.pallas_call(
         lambda *refs: spectrum(*refs, sides=sides),
         out_shape=jax.ShapeDtypeStruct((band, grid), jnp.float32),
-        in_specs=[vmem] * (5 + 2 * len(sides)),
+        in_specs=[vmem] * (4 + len(sides)),
         out_specs=vmem,
         compiler_params=params,
         name="spectrum",
-    )(part, row_v, side_v, col_v, strip, *uprights, *corners)
+    )(part, edge, side_v, col_v, *corners)
     other = lax.ppermute(mine, "cond", [(0, 1), (1, 0)])
     send, level = pl.pallas_call(
         lambda *refs: imaging(*refs, pad=pad),
@@ -409,7 +429,7 @@
         in_specs=[vmem] * 9,
         out_specs=(vmem, vmem),
         scratch_shapes=[
-            pltpu.VMEM((4, kerns * band, 2 * grid), jnp.bfloat16),
+            pltpu.VMEM((conds, kerns * band, 2 * grid), jnp.bfloat16),
             pltpu.VMEM((conds, grid, grid), jnp.float32),
         ],
         compiler_params=params,

time: 19.4 us -> 19.1 us (0.985)
  waiting for transfers between devices: 2.86 us -> 2.62 us
    ppermute x2, waiting for transfers between devices: 0.8 us -> 0.55 us  [passed(): return lax.ppermute(block, ('tile', 'cond'), pairs)]
    pallas_call x0 -> x1, Pallas kernels: none -> 0.23 us  [on_device(): pl.pallas_call(lambda *refs: window(*refs, sides=sides), out_shape=[jax.S...]
  transfers between devices with their start and end apart: 5 -> 5, of which waited for: 3 -> 3; matrix products, arithmetic and copies ran while one was open for 0% -> 0% of each run, Pallas kernels for 14% -> 16%
where the time goes in v8:
time: 19.1 us; the launch traced here: 18.9 us
  Pallas kernels  7.68 us (40%)
  starting transfers between devices  7.16 us (37%)
  waiting for transfers between devices  2.62 us (14%)
  other arithmetic  0.75 us (4%)
  between operations  0.7 us (4%)
    ppermute x2, starting transfers between devices, passed(): return lax.ppermute(block, ('tile', 'cond'), pairs)  4.34 us
    pallas_call x1, Pallas kernels, on_device(): pl.pallas_call(lambda *refs: imaging(*refs, pad=pad), out_shape=(jax.Shap...  3.35 us
    ppermute x1, starting transfers between devices, shifted(): lax.ppermute(block, axis, [((i - distance) % count, i) for i in range(cou...  2.59 us
    pallas_call x1, Pallas kernels, on_device(): pl.pallas_call(lambda *refs: staging(*refs, count=len(fixed)), out_shape=...  2.44 us
    ppermute x1, waiting for transfers between devices, on_device(): other = lax.ppermute(mine, 'cond', [(0, 1), (1, 0)])  1.2 us
    pallas_call x1, Pallas kernels, on_device(): pl.pallas_call(lambda *refs: cut(*refs, sides=sides), out_shape=[jax.Shap...  0.95 us
    ppermute x1, waiting for transfers between devices, on_device(): other = lax.ppermute(send, 'cond', [(0, 1), (1, 0)])  0.86 us
    min x1, other arithmetic, on_device(): jnp.minimum(keep[1], other[1])[None]  0.73 us
  transfers between devices with their start and end apart: 5, of which 3 were waited for; matrix products, arithmetic and copies ran while one was open for 0% of the time, Pallas kernels for 16%

profile of v8, /device:TPU:0, one launch (start us, length us, event | category | flops | bytes accessed | tf_op | source)
XLA Modules:
  0.0 18.9 jit_solution(7595334982084767408)
XLA Ops:
  0.6 0.9 %cut.1 = (bf16[128,128]{1,0:T(8,128)(2,1)S(1)}, bf16[64,128]{1,0:T(8,128)(2,1)S(1)}, bf16[32,128]{1,0:T(8,128)(2,1)S(1)}) custom-call(bf16[256,256]{1,0:T(8,128)(2,1)} %bitcast.1), custom_call_target="tpu_custom_call" | custom-call | tf_op jit(solution)/shard_map/cut/pallas_call | solution.py:343
  1.6 3.0 %collective-permute-start = (bf16[128,128]{1,0:T(8,128)(2,1)S(1)}, bf16[128,128]{1,0:T(8,128)(2,1)S(1)}, u32[]{:S(2)}, u32[]{:S(2)}) collective-permute-start(bf16[128,128]{1,0:T(8,128)(2,1)S(1)} %get-tuple-element.23), channel_id=1, source_target_pairs={{14,0},{3,1},{0,2},{5,3},{2,4},{7,5},{4,6},{9,7},{6,8},{11,9},{8,1... | collective-permute-start | bytes 98312 | tf_op jit(solution)/shard_map/ppermute | solution.py:363
  4.6 2.6 %collective-permute-start.1 = (bf16[64,128]{1,0:T(8,128)(2,1)S(1)}, bf16[64,128]{1,0:T(8,128)(2,1)S(1)}, u32[]{:S(2)}, u32[]{:S(2)}) collective-permute-start(bf16[64,128]{1,0:T(8,128)(2,1)S(1)} %get-tuple-element.24), channel_id=1, source_target_pairs={{8,0},{10,2},{12,4},{14,6},{0,8},{2,10},{4,12},{6,14},{9,1},{11,3}... | collective-permute-start | bytes 49160 | tf_op jit(solution)/shard_map/ppermute | solution.py:325
  7.2 1.3 %collective-permute-start.2 = (bf16[32,128]{1,0:T(8,128)(2,1)S(1)}, bf16[32,128]{1,0:T(8,128)(2,1)S(1)}, u32[]{:S(2)}, u32[]{:S(2)}) collective-permute-start(bf16[32,128]{1,0:T(8,128)(2,1)S(1)} %get-tuple-element.28), channel_id=1, source_target_pairs={{6,0},{11,1},{8,2},{13,3},{10,4},{15,5},{12,6},{1,7},{14,8},{3,9},... | collective-permute-start | bytes 24584 | tf_op jit(solution)/shard_map/ppermute | solution.py:363
  8.5 2.4 %staging.1 = (bf16[2,256,128]{2,1,0:T(8,128)(2,1)S(1)}, bf16[128,256]{1,0:T(8,128)(2,1)S(1)}, bf16[2,64,128]{2,1,0:T(8,128)(2,1)S(1)}, bf16[128,256]{1,0:T(8,128...) custom-call(bf16[256,256]{1,0:T(8,128)(2,1)} %bitcast.2, ...), custom_call_target="tpu_custom_call" | custom-call | tf_op jit(solution)/shard_map/staging/pallas_call | solution.py:392
  11.0 0.0 collective-permute-done.1.refs_4_
  11.0 0.0 collective-permute-done.refs_3_
  11.0 0.2 %window.1 = (bf16[128,128]{1,0:T(8,128)(2,1)S(1)}, f32[128,128]{1,0:T(8,128)S(1)}) custom-call(f32[128,128]{1,0:T(8,128)S(1)} %get-tuple-element.20.refs_0_, bf16[128,256]{1,0:T(8,128)(2,1)S(1)} %get-tuple-element.21.refs_1_, bf16[2,64,128]{2,1,0:T(8,128)(2,1)S(1)} %get-tuple-element.22.refs_2_, bf16[128,128]{1,0:T(8,128)(2,1)S(1)} %collective-permute-done.refs_3_, ...), custom_call_target="tpu_custom_call" | custom-call | tf_op jit(solution)/shard_map/window/pallas_call | solution.py:403
  11.2 0.6 %collective-permute-done.2.refs_4_ = bf16[32,128]{1,0:T(8,128)(2,1)S(1)} collective-permute-done((bf16[32,128]{1,0:T(8,128)(2,1)S(1)}, bf16[32,128]{1,0:T(8,128)(2,1)S(1)}, u32[]{:S(2)}, u32[]{:S(2)}) %collective-permute-start.2) | collective-permute-done | bytes 8224 | tf_op jit(solution)/shard_map/ppermute | solution.py:363
  11.8 0.4 %spectrum.1.refs_0_ = f32[64,128]{1,0:T(8,128)S(1)} custom-call(bf16[128,128]{1,0:T(8,128)(2,1)S(1)} %get-tuple-element.25.refs_0_, f32[128,128]{1,0:T(8,128)S(1)} %get-tuple-element.26.refs_1_, bf16[2,64,128]{2,1,0:T(8,128)(2,1)S(1)} %get-tuple-element.22.refs_2_, bf16[2,256,128]{2,1,0:T(8,128)(2,1)S(1)} %get-tuple-element.27.refs_3_, ...), custom_call_target="tpu_custom_call" | custom-call | tf_op jit(solution)/shard_map/spectrum/pallas_call | solution.py:414
  12.2 0.0 collective-permute-start.3
  12.2 1.2 %collective-permute-done.3.refs_1_ = f32[64,128]{1,0:T(8,128)S(1)} collective-permute-done((f32[64,128]{1,0:T(8,128)S(1)}, f32[64,128]{1,0:T(8,128)S(1)}, u32[]{:S(2)}, u32[]{:S(2)}) %collective-permute-start.3) | collective-permute-done | bytes 32800 | tf_op jit(solution)/shard_map/ppermute | solution.py:422
  13.4 3.3 %imaging.1 = (bf16[2,128,256]{2,1,0:T(8,128)(2,1)S(1)}, bf16[2,512,256]{2,1,0:T(8,128)(2,1)S(1)}) custom-call(f32[64,128]{1,0:T(8,128)S(1)} %spectrum.1.refs_0_, f32[64,128]{1,0:T(8,128)S(1)} %collective-permute-done.3.refs_1_, bf16[128,256]{1,0:T(8,128)(2,1)S(1)} %get-tuple-element.29.refs_2_, bf16[256,128]{1,0:T(8,128)(2,1)S(1)} %get-tuple-element.30.refs_3_, ...), custom_call_target="tpu_custom_call" | custom-call | tf_op jit(solution)/shard_map/imaging/pallas_call | solution.py:423
  16.7 0.2 %collective-permute-start.4 = (bf16[2,128,256]{2,1,0:T(8,128)(2,1)S(1)}, bf16[2,128,256]{2,1,0:T(8,128)(2,1)S(1)}, u32[]{:S(2)}, u32[]{:S(2)}) collective-permute-start(bf16[2,128,256]{2,1,0:T(8,128)(2,1)S(1)} %get-tuple-element.37), channel_id=1, source_target_pairs={{0,1},{1,0},{2,3},{3,2},{4,5},{5,4},{6,7},{7,6},{8,9},{9,8},{10,11... | collective-permute-start | bytes 393224 | tf_op jit(solution)/shard_map/ppermute | solution.py:438
  17.0 0.3 %own_share.1 = f32[2,128,256]{2,1,0:T(8,128)S(1)} custom-call(bf16[2,512,256]{2,1,0:T(8,128)(2,1)S(1)} %get-tuple-element.36.level_ref, f32[2,4,8,256]{3,2,1,0:T(8,128)S(1)} %get-tuple-element.35.refs_8_.gain_ref, bf16[2,256,128]{2,1,0:T(8,128)(2,1)S(1)} %get-tuple-element.31.refs_4_.spread_ref), custom_call_target="tpu_custom_call" | custom-call | tf_op jit(solution)/shard_map/own_share/pallas_call | solution.py:439
  17.3 0.9 %collective-permute-done.4 = bf16[2,128,256]{2,1,0:T(8,128)(2,1)S(1)} collective-permute-done((bf16[2,128,256]{2,1,0:T(8,128)(2,1)S(1)}, bf16[2,128,256]{2,1,0:T(8,128)(2,1)S(1)}, u32[]{:S(2)}, u32[]{:S(2)}) %collective-permute-start.4) | collective-permute-done | bytes 131104 | tf_op jit(solution)/shard_map/ppermute | solution.py:438
  18.2 0.7 %slice_minimum_fusion = (f32[1,128,256]{2,1,0:T(8,128)}, f32[1,128,256]{2,1,0:T(8,128)}) fusion(f32[2,128,256]{2,1,0:T(8,128)S(1)} %convert_element_type.3, f32[2,128,256]{2,1,0:T(8,128)S(1)} %own_share.1), kind=kLoop, calls=%fused_computation | loop fusion | flops 65536 | bytes 786432 | tf_op jit(solution)/shard_map/min | solution.py:448
  (1 shorter events, 0.0 us)
Async XLA Ops:
  1.6 9.4 %collective-permute-start = (bf16[128,128]{1,0:T(8,128)(2,1)S(1)}, bf16[128,128]{1,0:T(8,128)(2,1)S(1)}, u32[]{:S(2)}, u32[]{:S(2)}) collective-permute-start(bf16[128,128]{1,0:T(8,128)(2,1)S(1)} %get-tuple-element.23), channel_id=1, source_target_pairs={{14,0},{3,1},{0,2},{5,3},{2,4},{7,5},{4,6},{9,7},{6,8},{11,9},{8,1... | collective-permute-start | bytes 98312 | tf_op jit(solution)/shard_map/ppermute | solution.py:363
  4.6 6.4 %collective-permute-start.1 = (bf16[64,128]{1,0:T(8,128)(2,1)S(1)}, bf16[64,128]{1,0:T(8,128)(2,1)S(1)}, u32[]{:S(2)}, u32[]{:S(2)}) collective-permute-start(bf16[64,128]{1,0:T(8,128)(2,1)S(1)} %get-tuple-element.24), channel_id=1, source_target_pairs={{8,0},{10,2},{12,4},{14,6},{0,8},{2,10},{4,12},{6,14},{9,1},{11,3}... | collective-permute-start | bytes 49160 | tf_op jit(solution)/shard_map/ppermute | solution.py:325
  7.2 4.6 %collective-permute-start.2 = (bf16[32,128]{1,0:T(8,128)(2,1)S(1)}, bf16[32,128]{1,0:T(8,128)(2,1)S(1)}, u32[]{:S(2)}, u32[]{:S(2)}) collective-permute-start(bf16[32,128]{1,0:T(8,128)(2,1)S(1)} %get-tuple-element.28), channel_id=1, source_target_pairs={{6,0},{11,1},{8,2},{13,3},{10,4},{15,5},{12,6},{1,7},{14,8},{3,9},... | collective-permute-start | bytes 24584 | tf_op jit(solution)/shard_map/ppermute | solution.py:363
  12.2 1.2 %collective-permute-start.3 = (f32[64,128]{1,0:T(8,128)S(1)}, f32[64,128]{1,0:T(8,128)S(1)}, u32[]{:S(2)}, u32[]{:S(2)}) collective-permute-start(f32[64,128]{1,0:T(8,128)S(1)} %spectrum.1.refs_0_), channel_id=1, source_target_pairs={{0,1},{1,0},{2,3},{3,2},{4,5},{5,4},{6,7},{7,6},{8,9},{9,8},{10,11... | collective-permute-start | bytes 98312 | tf_op jit(solution)/shard_map/ppermute | solution.py:422
  16.7 1.4 %collective-permute-start.4 = (bf16[2,128,256]{2,1,0:T(8,128)(2,1)S(1)}, bf16[2,128,256]{2,1,0:T(8,128)(2,1)S(1)}, u32[]{:S(2)}, u32[]{:S(2)}) collective-permute-start(bf16[2,128,256]{2,1,0:T(8,128)(2,1)S(1)} %get-tuple-element.37), channel_id=1, source_target_pairs={{0,1},{1,0},{2,3},{3,2},{4,5},{5,4},{6,7},{7,6},{8,9},{9,8},{10,11... | collective-permute-start | bytes 393224 | tf_op jit(solution)/shard_map/ppermute | solution.py:438

commit v9 on v8

--- a/solution.py
+++ b/solution.py
@@ -96,18 +96,6 @@
 
 def dot_first(a, b):
     return lax.dot_general(a, b, (((0,), (0,)), ((), ())), preferred_element_type=jnp.float32)
-
-
-def native_lanes(shape):
-    upper = (lax.broadcasted_iota(jnp.int32, shape, 1) >= MARGIN).astype(jnp.int32)
-    return upper != lax.axis_index("cond")
-
-
-def folded(block):
-    rows = block.shape[0] // 2
-    block = block.astype(jnp.float32)
-    back = pltpu.roll(block[rows:], MARGIN, 1)
-    return jnp.where(native_lanes(back.shape), block[:rows], back).astype(jnp.bfloat16)
 
 
 def dma_all(pairs, sems):
@@ -152,10 +140,19 @@
         copy.wait()
 
 
+def late_staging(order_ref, *refs):
+    count = (len(refs) - 1) // 2
+    copies = dma_all(zip(refs[:count], refs[count : 2 * count]), refs[-1])
+    for copy in copies:
+        copy.start()
+    for copy in copies:
+        copy.wait()
+
+
 def cut(tile_hbm, strip_ref, *refs, sides):
     upright_refs, corner_refs = refs[: len(sides)], refs[len(sides) : 2 * len(sides)]
-    block_ref, sems = refs[2 * len(sides) :]
-    core, wide = block_ref.shape
+    sems = refs[-1]
+    core, wide = strip_ref.shape
     half = upright_refs[0].shape[1]
     own = lax.axis_index("cond")
     beside = pl.multiple_of((1 - own) * (core - wide), wide)
@@ -167,17 +164,14 @@
             rows.append(pl.ds(pl.multiple_of(lower * (core - MARGIN), MARGIN), MARGIN))
         else:
             rows.append(pl.ds(0 if side else core - MARGIN, MARGIN))
-    pairs = [(tile_hbm.at[:, pl.ds(beside, wide)], block_ref)]
-    for r, upright_ref in zip(rows, upright_refs):
+    pairs = [(tile_hbm.at[:, pl.ds(beside, wide)], strip_ref)]
+    for r, upright_ref, corner_ref in zip(rows, upright_refs, corner_refs):
         pairs.append((tile_hbm.at[r, pl.ds(first, half)], upright_ref))
+        pairs.append((tile_hbm.at[r, pl.ds(beside, wide)], corner_ref))
     copies = dma_all(pairs, sems)
     for copy in copies:
         copy.start()
-    copies[0].wait()
-    strip_ref[...] = folded(block_ref[...])
-    for r, corner_ref in zip(rows, corner_refs):
-        corner_ref[...] = folded(block_ref[r])
-    for copy in copies[1:]:
+    for copy in copies:
         copy.wait()
 
 
@@ -194,15 +188,12 @@
 def window(core_ref, row_core_ref, row_side_ref, strip_ref, *rest, sides):
     *upright_refs, out_ref, edge_ref = rest
     place = placement()
-    fold = strip_ref.shape[0]
     core = core_ref[...]
     for side, upright_ref in zip(sides, upright_refs):
         table, there = vertical(place, side, row_side_ref)
         core = core + kept(there, dot_first(table[...], upright_ref[...]))
     out_ref[...] = core.astype(jnp.bfloat16)
-    ahead = dot(row_core_ref[:, :fold], strip_ref[...])
-    behind = dot(row_core_ref[:, fold:], strip_ref[...])
-    edge_ref[...] = ahead + pltpu.roll(behind, MARGIN, 1)
+    edge_ref[...] = dot(row_core_ref[...], strip_ref[...])
 
 
 def spectrum(core_ref, edge_ref, row_side_ref, columns_ref, *rest, sides):
@@ -213,9 +204,7 @@
     edge = edge_ref[...]
     for side, corner_ref in zip(sides, corner_refs):
         table, there = vertical(place, side, row_side_ref)
-        fold = corner_ref.shape[0]
-        behind = pltpu.roll(dot_first(table[fold:], corner_ref[...]), MARGIN, 1)
-        edge = edge + kept(there, dot_first(table[:fold], corner_ref[...]) + behind)
+        edge = edge + kept(there, dot_first(table[...], corner_ref[...]))
     beside = jnp.where(place["half"] == 0, place["left"], place["right"])
     edge = kept(beside, edge).astype(jnp.bfloat16)
     core = core_ref[...]
@@ -252,12 +241,14 @@
     spec_cross = jnp.where(first, -swapped, spec)
 
     def condition(c, halves_ref):
-        prods = []
-        for k in range(kerns):
-            kern = kern_ref[c, k].astype(jnp.float32)
-            prod = kern * spec_same + pltpu.roll(kern, band, 1) * spec_cross
-            prods.append(prod.astype(jnp.bfloat16))
-        halves_ref[...] = dot(jnp.concatenate(prods, axis=0), half_ref[...]).astype(jnp.bfloat16)
+        for k in range(0, kerns, 12):
+            prods = []
+            for m in range(k, k + 12):
+                kern = kern_ref[c, m].astype(jnp.float32)
+                prod = kern * spec_same + pltpu.roll(kern, band, 1) * spec_cross
+                prods.append(prod.astype(jnp.bfloat16))
+            half = dot(jnp.concatenate(prods, axis=0), half_ref[...]).astype(jnp.bfloat16)
+            halves_ref[k * band : (k + 12) * band] = half
         total = jnp.zeros((grid, grid), jnp.float32)
         for k in range(0, kerns, 2):
             a = halves_ref[k * band : (k + 1) * band]
@@ -342,14 +333,13 @@
     params = pltpu.CompilerParams(vmem_limit_bytes=16 * 2**20)
     strip, *blocks = pl.pallas_call(
         lambda *refs: cut(*refs, sides=sides),
-        out_shape=[jax.ShapeDtypeStruct((core // 2, wide), tile.dtype)]
+        out_shape=[jax.ShapeDtypeStruct((core, wide), tile.dtype)]
         + [jax.ShapeDtypeStruct((MARGIN, half), tile.dtype)] * len(sides)
-        + [jax.ShapeDtypeStruct((MARGIN // 2, wide), tile.dtype)] * len(sides),
+        + [jax.ShapeDtypeStruct((MARGIN, wide), tile.dtype)] * len(sides),
         in_specs=[hbm],
         out_specs=[vmem] * (1 + 2 * len(sides)),
         scratch_shapes=[
-            pltpu.VMEM((core, wide), tile.dtype),
-            pltpu.SemaphoreType.DMA((1 + len(sides),)),
+            pltpu.SemaphoreType.DMA((1 + 2 * len(sides),)),
         ],
         compiler_params=params,
         name="cut",
@@ -374,10 +364,9 @@
         bf(row_side),
         bf(half_t),
         bf(field_t),
-        jnp.asarray(two_parts(spread)),
-        jnp.asarray(two_parts(spread.T)),
         kernels,
     ]
+    fixed_late = [jnp.asarray(two_parts(spread)), jnp.asarray(two_parts(spread.T))]
     share = core // lax.axis_size("cond")
     outs = [jax.ShapeDtypeStruct(t.shape, t.dtype) for t in fixed]
     outs[0] = jax.ShapeDtypeStruct(fixed[0].shape[1:], fixed[0].dtype)
@@ -388,7 +377,7 @@
         jax.ShapeDtypeStruct((2, conds, 8, core), jnp.float32),
     ]
     scalars = (socs_weight, dose, threshold)
-    (col_v, row_v, side_v, half_v, field_v, spread_v, across_v, kernels_v, tile_v, part, *gains) = (
+    (col_v, row_v, side_v, half_v, field_v, kernels_v, tile_v, part, *gains) = (
         pl.pallas_call(
             lambda *refs: staging(*refs, count=len(fixed)),
             out_shape=outs,
@@ -420,6 +409,16 @@
         name="spectrum",
     )(part, edge, side_v, col_v, *corners)
     other = lax.ppermute(mine, "cond", [(0, 1), (1, 0)])
+    late = [fixed_late[0], fixed_late[1]]
+    spread_v, across_v = pl.pallas_call(
+        late_staging,
+        out_shape=[jax.ShapeDtypeStruct(t.shape, t.dtype) for t in late],
+        in_specs=[vmem] + [hbm] * len(late),
+        out_specs=[vmem] * len(late),
+        scratch_shapes=[pltpu.SemaphoreType.DMA((len(late),))],
+        compiler_params=params,
+        name="late_staging",
+    )(mine, *map(in_hbm, late))
     send, level = pl.pallas_call(
         lambda *refs: imaging(*refs, pad=pad),
         out_shape=(

time: 19.1 us -> 19.1 us (level)
  waiting for transfers between devices: 2.62 us -> 1.8 us
  Pallas kernels: 7.68 us -> 8.29 us
    ppermute x1, waiting for transfers between devices: 1.2 us -> 0.21 us  [on_device(): other = lax.ppermute(mine, 'cond', [(0, 1), (1, 0)])]
    pallas_call x0 -> x1, Pallas kernels: none -> 0.99 us  [on_device(): pl.pallas_call(late_staging, out_shape=[jax.ShapeDtypeStruct(t.shape, t.d...]
    ppermute x2, waiting for transfers between devices: 0.55 us -> 0.88 us  [passed(): return lax.ppermute(block, ('tile', 'cond'), pairs)]
  transfers between devices with their start and end apart: 5 -> 5, of which waited for: 3 -> 3; matrix products, arithmetic and copies ran while one was open for 0% -> 0% of each run, Pallas kernels for 16% -> 20%
where the time goes in v9:
time: 19.1 us; the launch traced here: 18.9 us
  Pallas kernels  8.29 us (43%)
  starting transfers between devices  7.32 us (38%)
  waiting for transfers between devices  1.8 us (9%)
  other arithmetic  0.75 us (4%)
  between operations  0.7 us (4%)
    ppermute x2, starting transfers between devices, passed(): return lax.ppermute(block, ('tile', 'cond'), pairs)  4.34 us
    pallas_call x1, Pallas kernels, on_device(): pl.pallas_call(lambda *refs: imaging(*refs, pad=pad), out_shape=(jax.Shap...  3.28 us
    ppermute x1, starting transfers between devices, shifted(): lax.ppermute(block, axis, [((i - distance) % count, i) for i in range(cou...  2.59 us
    pallas_call x1, Pallas kernels, on_device(): pl.pallas_call(lambda *refs: staging(*refs, count=len(fixed)), out_shape=...  2.3 us
    pallas_call x1, Pallas kernels, on_device(): pl.pallas_call(late_staging, out_shape=[jax.ShapeDtypeStruct(t.shape, t.d...  0.99 us
    pallas_call x1, Pallas kernels, on_device(): pl.pallas_call(lambda *refs: cut(*refs, sides=sides), out_shape=[jax.Shap...  0.88 us
    ppermute x2, waiting for transfers between devices, passed(): return lax.ppermute(block, ('tile', 'cond'), pairs)  0.88 us
    min x1, other arithmetic, on_device(): jnp.minimum(keep[1], other[1])[None]  0.73 us
  transfers between devices with their start and end apart: 5, of which 3 were waited for; matrix products, arithmetic and copies ran while one was open for 0% of the time, Pallas kernels for 20%

profile of v9, /device:TPU:0, one launch (start us, length us, event | category | flops | bytes accessed | tf_op | source)
XLA Modules:
  0.0 18.9 jit_solution(4439402439198761964)
XLA Ops:
  0.6 0.9 %cut.1 = (bf16[256,128]{1,0:T(8,128)(2,1)S(1)}, bf16[64,128]{1,0:T(8,128)(2,1)S(1)}, bf16[64,128]{1,0:T(8,128)(2,1)S(1)}) custom-call(bf16[256,256]{1,0:T(8,128)(2,1)} %bitcast.1), custom_call_target="tpu_custom_call" | custom-call | tf_op jit(solution)/shard_map/cut/pallas_call | solution.py:334
  1.5 3.0 %collective-permute-start = (bf16[256,128]{1,0:T(8,128)(2,1)S(1)}, bf16[256,128]{1,0:T(8,128)(2,1)S(1)}, u32[]{:S(2)}, u32[]{:S(2)}) collective-permute-start(bf16[256,128]{1,0:T(8,128)(2,1)S(1)} %get-tuple-element.23), channel_id=1, source_target_pairs={{14,0},{3,1},{0,2},{5,3},{2,4},{7,5},{4,6},{9,7},{6,8},{11,9},{8,1... | collective-permute-start | bytes 196616 | tf_op jit(solution)/shard_map/ppermute | solution.py:353
  4.5 2.6 %collective-permute-start.1 = (bf16[64,128]{1,0:T(8,128)(2,1)S(1)}, bf16[64,128]{1,0:T(8,128)(2,1)S(1)}, u32[]{:S(2)}, u32[]{:S(2)}) collective-permute-start(bf16[64,128]{1,0:T(8,128)(2,1)S(1)} %get-tuple-element.24), channel_id=1, source_target_pairs={{8,0},{10,2},{12,4},{14,6},{0,8},{2,10},{4,12},{6,14},{9,1},{11,3}... | collective-permute-start | bytes 49160 | tf_op jit(solution)/shard_map/ppermute | solution.py:316
  7.1 1.3 %collective-permute-start.2 = (bf16[64,128]{1,0:T(8,128)(2,1)S(1)}, bf16[64,128]{1,0:T(8,128)(2,1)S(1)}, u32[]{:S(2)}, u32[]{:S(2)}) collective-permute-start(bf16[64,128]{1,0:T(8,128)(2,1)S(1)} %get-tuple-element.28), channel_id=1, source_target_pairs={{6,0},{11,1},{8,2},{13,3},{10,4},{15,5},{12,6},{1,7},{14,8},{3,9},... | collective-permute-start | bytes 49160 | tf_op jit(solution)/shard_map/ppermute | solution.py:353
  8.4 2.3 %staging.1 = (bf16[2,256,128]{2,1,0:T(8,128)(2,1)S(1)}, bf16[128,256]{1,0:T(8,128)(2,1)S(1)}, bf16[2,64,128]{2,1,0:T(8,128)(2,1)S(1)}, bf16[128,256]{1,0:T(8,128...) custom-call(bf16[256,256]{1,0:T(8,128)(2,1)} %bitcast.2, ...), custom_call_target="tpu_custom_call" | custom-call | tf_op jit(solution)/shard_map/staging/pallas_call | solution.py:381
  10.8 0.0 collective-permute-done.1.refs_4_
  10.8 0.0 collective-permute-done.refs_3_
  10.8 0.2 %window.1 = (bf16[128,128]{1,0:T(8,128)(2,1)S(1)}, f32[128,128]{1,0:T(8,128)S(1)}) custom-call(f32[128,128]{1,0:T(8,128)S(1)} %get-tuple-element.20.refs_0_, bf16[128,256]{1,0:T(8,128)(2,1)S(1)} %get-tuple-element.21.refs_1_, bf16[2,64,128]{2,1,0:T(8,128)(2,1)S(1)} %get-tuple-element.22.refs_2_, bf16[256,128]{1,0:T(8,128)(2,1)S(1)} %collective-permute-done.refs_3_, ...), custom_call_target="tpu_custom_call" | custom-call | tf_op jit(solution)/shard_map/window/pallas_call | solution.py:392
  11.0 0.9 %collective-permute-done.2.refs_4_ = bf16[64,128]{1,0:T(8,128)(2,1)S(1)} collective-permute-done((bf16[64,128]{1,0:T(8,128)(2,1)S(1)}, bf16[64,128]{1,0:T(8,128)(2,1)S(1)}, u32[]{:S(2)}, u32[]{:S(2)}) %collective-permute-start.2) | collective-permute-done | bytes 16416 | tf_op jit(solution)/shard_map/ppermute | solution.py:353
  11.9 0.3 %spectrum.1.order_ref.refs_0_ = f32[64,128]{1,0:T(8,128)S(1)} custom-call(bf16[128,128]{1,0:T(8,128)(2,1)S(1)} %get-tuple-element.25.refs_0_, f32[128,128]{1,0:T(8,128)S(1)} %get-tuple-element.26.refs_1_, bf16[2,64,128]{2,1,0:T(8,128)(2,1)S(1)} %get-tuple-element.22.refs_2_, bf16[2,256,128]{2,1,0:T(8,128)(2,1)S(1)} %get-tuple-element.27.refs_3_, ...), custom_call_target="tpu_custom_call" | custom-call | tf_op jit(solution)/shard_map/spectrum/pallas_call | solution.py:403
  12.2 0.0 collective-permute-start.3
  12.2 1.0 %late_staging.1 = (bf16[2,256,128]{2,1,0:T(8,128)(2,1)S(1)}, bf16[2,128,256]{2,1,0:T(8,128)(2,1)S(1)}) custom-call(f32[64,128]{1,0:T(8,128)S(1)} %spectrum.1.order_ref.refs_0_, bf16[2,256,128]{2,1,0:T(8,128)(2,1)} %constant.19.clone.refs_0_, bf16[2,128,256]{2,1,0:T(8,128)(2,1)} %constant.20.clone.refs_1_), custom_call_target="tpu_custom_call" | custom-call | tf_op jit(solution)/shard_map/late_staging/pallas_call | solution.py:413
  13.2 0.2 %collective-permute-done.3.refs_1_ = f32[64,128]{1,0:T(8,128)S(1)} collective-permute-done((f32[64,128]{1,0:T(8,128)S(1)}, f32[64,128]{1,0:T(8,128)S(1)}, u32[]{:S(2)}, u32[]{:S(2)}) %collective-permute-start.3) | collective-permute-done | bytes 32800 | tf_op jit(solution)/shard_map/ppermute | solution.py:411
  13.4 3.3 %imaging.1 = (bf16[2,128,256]{2,1,0:T(8,128)(2,1)S(1)}, bf16[2,512,256]{2,1,0:T(8,128)(2,1)S(1)}) custom-call(f32[64,128]{1,0:T(8,128)S(1)} %spectrum.1.order_ref.refs_0_, f32[64,128]{1,0:T(8,128)S(1)} %collective-permute-done.3.refs_1_, bf16[128,256]{1,0:T(8,128)(2,1)S(1)} %get-tuple-element.29.refs_2_, bf16[256,128]{1,0:T(8,128)(2,1)S(1)} %get-tuple-element.30.refs_3_, ...), custom_call_target="tpu_custom_call" | custom-call | tf_op jit(solution)/shard_map/imaging/pallas_call | solution.py:422
  16.7 0.4 %collective-permute-start.4 = (bf16[2,128,256]{2,1,0:T(8,128)(2,1)S(1)}, bf16[2,128,256]{2,1,0:T(8,128)(2,1)S(1)}, u32[]{:S(2)}, u32[]{:S(2)}) collective-permute-start(bf16[2,128,256]{2,1,0:T(8,128)(2,1)S(1)} %get-tuple-element.37), channel_id=1, source_target_pairs={{0,1},{1,0},{2,3},{3,2},{4,5},{5,4},{6,7},{7,6},{8,9},{9,8},{10,11... | collective-permute-start | bytes 393224 | tf_op jit(solution)/shard_map/ppermute | solution.py:437
  17.1 0.3 %own_share.1 = f32[2,128,256]{2,1,0:T(8,128)S(1)} custom-call(bf16[2,512,256]{2,1,0:T(8,128)(2,1)S(1)} %get-tuple-element.36.level_ref, f32[2,4,8,256]{3,2,1,0:T(8,128)S(1)} %get-tuple-element.35.refs_8_.gain_ref, bf16[2,256,128]{2,1,0:T(8,128)(2,1)S(1)} %get-tuple-element.31.refs_4_.spread_ref), custom_call_target="tpu_custom_call" | custom-call | tf_op jit(solution)/shard_map/own_share/pallas_call | solution.py:438
  17.4 0.7 %collective-permute-done.4 = bf16[2,128,256]{2,1,0:T(8,128)(2,1)S(1)} collective-permute-done((bf16[2,128,256]{2,1,0:T(8,128)(2,1)S(1)}, bf16[2,128,256]{2,1,0:T(8,128)(2,1)S(1)}, u32[]{:S(2)}, u32[]{:S(2)}) %collective-permute-start.4) | collective-permute-done | bytes 131104 | tf_op jit(solution)/shard_map/ppermute | solution.py:437
  18.1 0.7 %slice_minimum_fusion = (f32[1,128,256]{2,1,0:T(8,128)}, f32[1,128,256]{2,1,0:T(8,128)}) fusion(f32[2,128,256]{2,1,0:T(8,128)S(1)} %convert_element_type.3, f32[2,128,256]{2,1,0:T(8,128)S(1)} %own_share.1), kind=kLoop, calls=%fused_computation | loop fusion | flops 65536 | bytes 786432 | tf_op jit(solution)/shard_map/min | solution.py:447
  (1 shorter events, 0.0 us)
Async XLA Ops:
  1.5 9.2 %collective-permute-start = (bf16[256,128]{1,0:T(8,128)(2,1)S(1)}, bf16[256,128]{1,0:T(8,128)(2,1)S(1)}, u32[]{:S(2)}, u32[]{:S(2)}) collective-permute-start(bf16[256,128]{1,0:T(8,128)(2,1)S(1)} %get-tuple-element.23), channel_id=1, source_target_pairs={{14,0},{3,1},{0,2},{5,3},{2,4},{7,5},{4,6},{9,7},{6,8},{11,9},{8,1... | collective-permute-start | bytes 196616 | tf_op jit(solution)/shard_map/ppermute | solution.py:353
  4.5 6.2 %collective-permute-start.1 = (bf16[64,128]{1,0:T(8,128)(2,1)S(1)}, bf16[64,128]{1,0:T(8,128)(2,1)S(1)}, u32[]{:S(2)}, u32[]{:S(2)}) collective-permute-start(bf16[64,128]{1,0:T(8,128)(2,1)S(1)} %get-tuple-element.24), channel_id=1, source_target_pairs={{8,0},{10,2},{12,4},{14,6},{0,8},{2,10},{4,12},{6,14},{9,1},{11,3}... | collective-permute-start | bytes 49160 | tf_op jit(solution)/shard_map/ppermute | solution.py:316
  7.1 4.7 %collective-permute-start.2 = (bf16[64,128]{1,0:T(8,128)(2,1)S(1)}, bf16[64,128]{1,0:T(8,128)(2,1)S(1)}, u32[]{:S(2)}, u32[]{:S(2)}) collective-permute-start(bf16[64,128]{1,0:T(8,128)(2,1)S(1)} %get-tuple-element.28), channel_id=1, source_target_pairs={{6,0},{11,1},{8,2},{13,3},{10,4},{15,5},{12,6},{1,7},{14,8},{3,9},... | collective-permute-start | bytes 49160 | tf_op jit(solution)/shard_map/ppermute | solution.py:353
  12.2 1.2 %collective-permute-start.3 = (f32[64,128]{1,0:T(8,128)S(1)}, f32[64,128]{1,0:T(8,128)S(1)}, u32[]{:S(2)}, u32[]{:S(2)}) collective-permute-start(f32[64,128]{1,0:T(8,128)S(1)} %spectrum.1.order_ref.refs_0_), channel_id=1, source_target_pairs={{0,1},{1,0},{2,3},{3,2},{4,5},{5,4},{6,7},{7,6},{8,9},{9,8},{10,11... | collective-permute-start | bytes 98312 | tf_op jit(solution)/shard_map/ppermute | solution.py:411
  16.7 1.4 %collective-permute-start.4 = (bf16[2,128,256]{2,1,0:T(8,128)(2,1)S(1)}, bf16[2,128,256]{2,1,0:T(8,128)(2,1)S(1)}, u32[]{:S(2)}, u32[]{:S(2)}) collective-permute-start(bf16[2,128,256]{2,1,0:T(8,128)(2,1)S(1)} %get-tuple-element.37), channel_id=1, source_target_pairs={{0,1},{1,0},{2,3},{3,2},{4,5},{5,4},{6,7},{7,6},{8,9},{9,8},{10,11... | collective-permute-start | bytes 393224 | tf_op jit(solution)/shard_map/ppermute | solution.py:437
